TPU v7x, 512 devices: a whole 4x4x16 slice. The times are simulated.
512 devices in a mesh: gx: 16 (over z_hi, y, core), gy: 32 (over z_lo, x).
Axes of the slice: x: 4, y: 4, z: 16 (z_hi: 2, z_lo: 8; z = z_hi * 8 + z_lo), core: 2. Of those that a mesh axis runs over, the one named last changes fastest.
Arguments:
- particle_cell: int32 [16, 32, 65536], P('gx', 'gy'), may hold values from -1 to 16383, as said below
- particle_mass: float32 [16, 32, 65536], P('gx', 'gy'), may hold values from 0.5 to 2
Outputs:
- potential: float32 [256, 256, 128], P('gx', 'gy')
- residual: float32 [256, 256, 128], P('gx', 'gy')
- residual_norms: float32 [2], replicated
Inputs may be any that keep to these rules, and one draw needn't show every extreme that they name: `particle_cell`: -1 marks an empty slot; any other value v names the cell (v // 1024, v // 128 % 8, v % 128) of the block of 16 x 8 x 128 cells that belongs to the slot's tile.
All inputs are finite; a program needn't handle non-finite values.
Results may differ from a plain program's by a relative error of at most 0.0003.
Values sent between devices are 32-bit elements; how exact they have to be, the bound alone decides.
No kernel may reach another device: no remote copies, remote signals or barrier semaphores. Data moves between devices by JAX's collectives and lax.ppermute only.
A program may use at most 64 MiB of HBM per device.

v0:
```python
import jax
import jax.numpy as jnp
from jax import lax
from jax.sharding import Mesh
from jax.sharding import PartitionSpec as P

CX = 16
CY = 8
NZ = 128
LEVELS = 4
CYCLES = 2
COARSE_SWEEPS = 2
GX_GY = ("gx_0", "gx_1", "gx_2", "gy_0", "gy_1")
GX = ("gx_0", "gx_1", "gx_2")
GY = ("gy_0", "gy_1")


coupling = 0.03125
norm_eps = 1e-06


def extended(x, sides, width):
    edges = {}
    for axis, dim in sides:
        devices, length = (lax.axis_size(axis), x.shape[dim])
        up = [(i, (i + 1) % devices) for i in range(devices)]
        last = lax.slice_in_dim(x, length - width, length, axis=dim)
        initial = lax.slice_in_dim(x, 0, width, axis=dim)
        edges[dim] = (
            lax.ppermute(last, axis, up),
            lax.ppermute(initial, axis, [(b, a) for a, b in up]),
        )
    done = []
    for _, dim in sides:
        low, high = edges[dim]
        around = [(width, width) if d in done else (0, 0) for d in range(x.ndim)]
        x = jnp.concatenate([jnp.pad(low, around), x, jnp.pad(high, around)], axis=dim)
        done.append(dim)
    return x


def by_axis(x, axes):
    for axis in axes:
        x = lax.psum(x, axis)
    return x


def with_halo(cells, sides, width):
    for axis, dim in sides:
        count = lax.axis_size(axis)
        head = lax.slice_in_dim(cells, 0, width, axis=dim)
        tail = lax.slice_in_dim(cells, cells.shape[dim] - width, cells.shape[dim], axis=dim)
        cells = jnp.concatenate(
            [
                lax.ppermute(tail, axis, [(i, (i + 1) % count) for i in range(count)]),
                cells,
                lax.ppermute(head, axis, [((i + 1) % count, i) for i in range(count)]),
            ],
            axis=dim,
        )
    return cells


def parity_mask(shape, start_x, start_y):
    index_x = jnp.arange(shape[0], dtype=jnp.int32)[:, None, None] + start_x
    index_y = jnp.arange(shape[1], dtype=jnp.int32)[None, :, None] + start_y
    index_z = jnp.arange(shape[2], dtype=jnp.int32)[None, None, :]
    return (index_x + index_y + index_z) % 2 == 0


def restrict(values):
    rows_x, rows_y, rows_z = values.shape
    return values.reshape(rows_x // 2, 2, rows_y // 2, 2, rows_z // 2, 2).mean(axis=(1, 3, 5))


def prolong(values):
    rows_x, rows_y, rows_z = values.shape
    spread = jnp.broadcast_to(values[:, None, :, None, :, None], (rows_x, 2, rows_y, 2, rows_z, 2))
    return spread.reshape(2 * rows_x, 2 * rows_y, 2 * rows_z)


def narrow_pad(values):
    return extended(values, ((GX, 0), (GY, 1)), 1)


def edge_sum(padded):
    centre = padded[1:-1, 1:-1]
    beside = padded[:-2, 1:-1] + padded[2:, 1:-1]
    beside = beside + padded[1:-1, :-2] + padded[1:-1, 2:]
    return (centre, beside + jnp.roll(centre, 1, 2) + jnp.roll(centre, -1, 2))


def relax_colour(padded, source, chosen, spacing_squared):
    centre, beside = edge_sum(padded)
    updated = (beside + spacing_squared * source) / 6.0
    return jnp.where(chosen, updated, centre)


def local_residual(estimate, source, spacing_squared):
    centre, beside = edge_sum(narrow_pad(estimate))
    return source - (6.0 * centre - beside) / spacing_squared


def per_device(particle_cell, particle_mass):
    block_cells = CX * CY * NZ
    tiles_x = lax.axis_size(GX)
    tiles_y = lax.axis_size(GY)
    tile_x = lax.axis_index(GX)
    tile_y = lax.axis_index(GY)
    grid_cells = block_cells * tiles_x * tiles_y
    slot_ids = particle_cell.reshape(-1)
    masses = particle_mass.reshape(-1)
    occupied = slot_ids >= 0
    target = jnp.where(occupied, slot_ids, block_cells)
    density = jnp.zeros((block_cells + 1,), jnp.float32).at[target].add(masses)[:block_cells]
    density = density.reshape(CX, CY, NZ)
    total_mass = by_axis(jnp.sum(jnp.where(occupied, masses, 0.0)), GX_GY)
    mean_mass = total_mass / grid_cells
    source = coupling * (1.0 - density / mean_mass)

    def deep_pad(values):
        return with_halo(values, ((GX, 0), (GY, 1)), 2)

    def smooth_level(estimate, level_source, spacing_squared, wide_source):
        rows_x, rows_y, rows_z = estimate.shape
        start_x = tile_x * rows_x
        start_y = tile_y * rows_y
        red_cells = parity_mask(estimate.shape, start_x, start_y)
        black_cells = jnp.logical_not(red_cells)
        if wide_source is None:
            estimate = relax_colour(narrow_pad(estimate), level_source, red_cells, spacing_squared)
            return relax_colour(narrow_pad(estimate), level_source, black_cells, spacing_squared)
        wide_red = parity_mask((rows_x + 2, rows_y + 2, rows_z), start_x - 1, start_y - 1)
        grown_field = relax_colour(deep_pad(estimate), wide_source, wide_red, spacing_squared)
        return relax_colour(grown_field, level_source, black_cells, spacing_squared)

    def multigrid_cycle(grid_level, estimate, level_source):
        spacing_squared = float(4**grid_level)
        wide_source = None
        if deep_pad is not None and min(estimate.shape[0], estimate.shape[1]) >= 2:
            wide_source = deep_pad(level_source)[1:-1, 1:-1]
        if grid_level == LEVELS - 1:
            for repeat in range(COARSE_SWEEPS):
                estimate = smooth_level(estimate, level_source, spacing_squared, wide_source)
            return estimate
        estimate = smooth_level(estimate, level_source, spacing_squared, wide_source)
        coarse_source = restrict(local_residual(estimate, level_source, spacing_squared))
        correction = multigrid_cycle(grid_level + 1, jnp.zeros_like(coarse_source), coarse_source)
        estimate = estimate + prolong(correction)
        return smooth_level(estimate, level_source, spacing_squared, wide_source)

    potential = jnp.zeros((CX, CY, NZ), jnp.float32)
    residual = source
    square_sums = []
    for cycle_index in range(CYCLES):
        potential = multigrid_cycle(0, potential, source)
        residual = local_residual(potential, source, 1.0) / coupling
        square_sum = jnp.sum(residual * residual)
        square_sums.append(by_axis(square_sum, GX_GY))
    totals = jnp.stack(square_sums)
    residual_norms = jnp.sqrt(totals / grid_cells + norm_eps)
    return (potential, residual, residual_norms)


def solution(mesh):
    split = Mesh(mesh.devices.reshape(2, 4, 2, 8, 4), ("gx_0", "gx_1", "gx_2", "gy_0", "gy_1"))
    placed = (P(GX, GY, None), P(GX, GY, None))
    return jax.shard_map(
        per_device,
        mesh=split,
        in_specs=placed,
        out_specs=(P(GX, GY, None), P(GX, GY, None), P()),
        check_vma=False,
    )
```

profile of v0, /device:TPU:1, one launch (start us, length us, event | category | flops | bytes accessed | tf_op | source)
XLA Modules:
  0.0 1496.8 jit_solution(6138256872459830110)
XLA Ops:
  16.6 14.0 psum.105
  30.6 14.7 collective-permute-start.21
  45.3 15.9 %psum.106 = f32[]{:T(128)} all-reduce(f32[]{:T(128)} %psum.105), channel_id=1, replica_groups=mesh['gx_0'=2,'gx_1'=4,'gx_2'=2,'gy_0'=8,'gy_1'=4] {'gx_1'}, use_global_device_ids=true, to_apply=%region_3.4 | all-reduce | flops 1 | bytes 8 | tf_op jit(solution)/shard_map/psum | solution.py:44
  73.1 27.8 %psum.108 = f32[]{:T(128)} all-reduce(f32[]{:T(128)} %psum.107), channel_id=1, replica_groups=mesh['gx_0'=2,'gx_1'=4,'gx_2'=2,'gy_0'=8,'gy_1'=4] {'gy_0'}, use_global_device_ids=true, to_apply=%region_5.6 | all-reduce | flops 1 | bytes 8 | tf_op jit(solution)/shard_map/psum | solution.py:44
  100.9 351.2 %scatter_custom_fusion = f32[16385]{0:T(1024)S(1)} fusion(s32[65536]{0:T(1024)S(1)} %bitcast.81, f32[65536]{0:T(1024)} %bitcast.80, f32[]{:T(128)} %constant.260.clone.1), kind=kCustom, calls=%fused_computation.257 | custom fusion | flops 65536 | bytes 66052 | tf_op jit(solution)/shard_map/scatter-add | solution.py:115
  461.0 13.0 collective-permute-start.9
  478.0 12.1 collective-permute-start.23
  541.0 12.3 collective-permute-start.15
  558.8 12.7 collective-permute-start.13
  582.5 15.0 %collective-permute-start.17 = (f32[2,4,64]{2,1,0:T(4,128)S(1)}, f32[2,4,64]{2,1,0:T(4,128)S(1)}, u32[]{:S(2)}, u32[]{:S(2)}) collective-permute-start(f32[2,4,64]{2,1,0:T(4,128)S(1)} %get-tuple-element.192), channel_id=1, source_target_pairs={{32,0},{64,32},{96,64},{128,96},{160,128},{192,160},{224,192},{256... | collective-permute-start | bytes 6152 | tf_op jit(solution)/shard_map/ppermute | solution.py:57
  615.5 12.3 collective-permute-start.27
  629.8 16.7 %collective-permute-start.25 = (f32[1,4,64]{2,1,0:T(4,128)S(1)}, f32[1,4,64]{2,1,0:T(4,128)S(1)}, u32[]{:S(2)}, u32[]{:S(2)}) collective-permute-start(f32[1,4,64]{2,1,0:T(4,128)S(1)} %get-tuple-element.190), channel_id=1, source_target_pairs={{32,0},{64,32},{96,64},{128,96},{160,128},{192,160},{224,192},{256... | collective-permute-start | bytes 3080 | tf_op jit(solution)/shard_map/ppermute | solution.py:31
  650.0 15.0 collective-permute-start.29
  682.9 12.3 collective-permute-start.39
  697.2 16.7 %collective-permute-start.37 = (f32[1,2,32]{2,0,1:T(1,128)S(1)}, f32[1,2,32]{2,0,1:T(1,128)S(1)}, u32[]{:S(2)}, u32[]{:S(2)}) collective-permute-start(f32[1,2,32]{2,0,1:T(1,128)S(1)} %get-tuple-element.210), channel_id=1, source_target_pairs={{32,0},{64,32},{96,64},{128,96},{160,128},{192,160},{224,192},{256... | collective-permute-start | bytes 776 | tf_op jit(solution)/shard_map/ppermute | solution.py:31
  719.5 14.7 collective-permute-start.33
  751.3 15.5 %collective-permute-start.41 = (f32[1,1,16]{2,0,1:T(1,128)S(1)}, f32[1,1,16]{2,0,1:T(1,128)S(1)}, u32[]{:S(2)}, u32[]{:S(2)}) collective-permute-start(f32[1,1,16]{2,0,1:T(1,128)S(1)} %get-tuple-element.260), channel_id=1, source_target_pairs={{32,0},{64,32},{96,64},{128,96},{160,128},{192,160},{224,192},{256... | collective-permute-start | bytes 200 | tf_op jit(solution)/shard_map/ppermute | solution.py:31
  783.7 15.5 %collective-permute-start.45 = (f32[1,1,16]{2,0,1:T(1,128)S(1)}, f32[1,1,16]{2,0,1:T(1,128)S(1)}, u32[]{:S(2)}, u32[]{:S(2)}) collective-permute-start(f32[1,1,16]{2,0,1:T(1,128)S(1)} %get-tuple-element.252), channel_id=1, source_target_pairs={{32,0},{64,32},{96,64},{128,96},{160,128},{192,160},{224,192},{256... | collective-permute-start | bytes 200 | tf_op jit(solution)/shard_map/ppermute | solution.py:31
  816.2 15.5 %collective-permute-start.49 = (f32[1,1,16]{2,0,1:T(1,128)S(1)}, f32[1,1,16]{2,0,1:T(1,128)S(1)}, u32[]{:S(2)}, u32[]{:S(2)}) collective-permute-start(f32[1,1,16]{2,0,1:T(1,128)S(1)} %get-tuple-element.244), channel_id=1, source_target_pairs={{32,0},{64,32},{96,64},{128,96},{160,128},{192,160},{224,192},{256... | collective-permute-start | bytes 200 | tf_op jit(solution)/shard_map/ppermute | solution.py:31
  834.8 14.9 collective-permute-start.53
  868.2 16.1 %collective-permute-start.57 = (f32[2,4,64]{2,1,0:T(4,128)S(1)}, f32[2,4,64]{2,1,0:T(4,128)S(1)}, u32[]{:S(2)}, u32[]{:S(2)}) collective-permute-start(f32[2,4,64]{2,1,0:T(4,128)S(1)} %get-tuple-element.174), channel_id=1, source_target_pairs={{32,0},{64,32},{96,64},{128,96},{160,128},{192,160},{224,192},{256... | collective-permute-start | bytes 6152 | tf_op jit(solution)/shard_map/ppermute | solution.py:57
  887.0 12.8 collective-permute-start.59
  909.6 15.8 %collective-permute-start.61 = (f32[2,8,128]{2,1,0:T(8,128)S(1)}, f32[2,8,128]{2,1,0:T(8,128)S(1)}, u32[]{:S(2)}, u32[]{:S(2)}) collective-permute-start(f32[2,8,128]{2,1,0:T(8,128)S(1)} %get-tuple-element.92), channel_id=1, source_target_pairs={{32,0},{64,32},{96,64},{128,96},{160,128},{192,160},{224,192},{256... | collective-permute-start | bytes 24584 | tf_op jit(solution)/shard_map/ppermute | solution.py:57
  928.2 12.6 collective-permute-start.63
  944.5 15.9 %collective-permute-start.65 = (f32[2,8,128]{2,1,0:T(8,128)S(1)}, f32[2,8,128]{2,1,0:T(8,128)S(1)}, u32[]{:S(2)}, u32[]{:S(2)}) collective-permute-start(f32[2,8,128]{2,1,0:T(8,128)S(1)} %get-tuple-element.90), channel_id=1, source_target_pairs={{32,0},{64,32},{96,64},{128,96},{160,128},{192,160},{224,192},{256... | collective-permute-start | bytes 24584 | tf_op jit(solution)/shard_map/ppermute | solution.py:57
  963.1 12.6 collective-permute-start.67
  979.5 12.3 collective-permute-start.71
  993.8 16.4 %collective-permute-start.69 = (f32[1,8,128]{2,1,0:T(8,128)S(1)}, f32[1,8,128]{2,1,0:T(8,128)S(1)}, u32[]{:S(2)}, u32[]{:S(2)}) collective-permute-start(f32[1,8,128]{2,1,0:T(8,128)S(1)} %get-tuple-element.88), channel_id=1, source_target_pairs={{32,0},{64,32},{96,64},{128,96},{160,128},{192,160},{224,192},{256... | collective-permute-start | bytes 12296 | tf_op jit(solution)/shard_map/ppermute | solution.py:31
  1021.2 15.0 %collective-permute-start.73 = (f32[2,4,64]{2,1,0:T(4,128)S(1)}, f32[2,4,64]{2,1,0:T(4,128)S(1)}, u32[]{:S(2)}, u32[]{:S(2)}) collective-permute-start(f32[2,4,64]{2,1,0:T(4,128)S(1)} %get-tuple-element.172), channel_id=1, source_target_pairs={{32,0},{64,32},{96,64},{128,96},{160,128},{192,160},{224,192},{256... | collective-permute-start | bytes 6152 | tf_op jit(solution)/shard_map/ppermute | solution.py:57
  1054.2 12.3 collective-permute-start.79
  1068.5 16.7 %collective-permute-start.77 = (f32[1,4,64]{2,1,0:T(4,128)S(1)}, f32[1,4,64]{2,1,0:T(4,128)S(1)}, u32[]{:S(2)}, u32[]{:S(2)}) collective-permute-start(f32[1,4,64]{2,1,0:T(4,128)S(1)} %get-tuple-element.170), channel_id=1, source_target_pairs={{32,0},{64,32},{96,64},{128,96},{160,128},{192,160},{224,192},{256... | collective-permute-start | bytes 3080 | tf_op jit(solution)/shard_map/ppermute | solution.py:31
  1088.7 15.0 collective-permute-start.81
  1121.6 12.3 collective-permute-start.87
  1135.8 16.7 %collective-permute-start.85 = (f32[1,2,32]{2,0,1:T(1,128)S(1)}, f32[1,2,32]{2,0,1:T(1,128)S(1)}, u32[]{:S(2)}, u32[]{:S(2)}) collective-permute-start(f32[1,2,32]{2,0,1:T(1,128)S(1)} %get-tuple-element.198), channel_id=1, source_target_pairs={{32,0},{64,32},{96,64},{128,96},{160,128},{192,160},{224,192},{256... | collective-permute-start | bytes 776 | tf_op jit(solution)/shard_map/ppermute | solution.py:31
  1169.8 15.5 %collective-permute-start.89 = (f32[1,1,16]{2,0,1:T(1,128)S(1)}, f32[1,1,16]{2,0,1:T(1,128)S(1)}, u32[]{:S(2)}, u32[]{:S(2)}) collective-permute-start(f32[1,1,16]{2,0,1:T(1,128)S(1)} %get-tuple-element.236), channel_id=1, source_target_pairs={{32,0},{64,32},{96,64},{128,96},{160,128},{192,160},{224,192},{256... | collective-permute-start | bytes 200 | tf_op jit(solution)/shard_map/ppermute | solution.py:31
  1202.3 15.5 %collective-permute-start.93 = (f32[1,1,16]{2,0,1:T(1,128)S(1)}, f32[1,1,16]{2,0,1:T(1,128)S(1)}, u32[]{:S(2)}, u32[]{:S(2)}) collective-permute-start(f32[1,1,16]{2,0,1:T(1,128)S(1)} %get-tuple-element.228), channel_id=1, source_target_pairs={{32,0},{64,32},{96,64},{128,96},{160,128},{192,160},{224,192},{256... | collective-permute-start | bytes 200 | tf_op jit(solution)/shard_map/ppermute | solution.py:31
  1234.8 15.5 %collective-permute-start.97 = (f32[1,1,16]{2,0,1:T(1,128)S(1)}, f32[1,1,16]{2,0,1:T(1,128)S(1)}, u32[]{:S(2)}, u32[]{:S(2)}) collective-permute-start(f32[1,1,16]{2,0,1:T(1,128)S(1)} %get-tuple-element.220), channel_id=1, source_target_pairs={{32,0},{64,32},{96,64},{128,96},{160,128},{192,160},{224,192},{256... | collective-permute-start | bytes 200 | tf_op jit(solution)/shard_map/ppermute | solution.py:31
  1253.3 14.9 collective-permute-start.101
  1286.7 16.1 %collective-permute-start.105 = (f32[2,4,64]{2,1,0:T(4,128)S(1)}, f32[2,4,64]{2,1,0:T(4,128)S(1)}, u32[]{:S(2)}, u32[]{:S(2)}) collective-permute-start(f32[2,4,64]{2,1,0:T(4,128)S(1)} %get-tuple-element.154), channel_id=1, source_target_pairs={{32,0},{64,32},{96,64},{128,96},{160,128},{192,160},{224,192},{256... | collective-permute-start | bytes 6152 | tf_op jit(solution)/shard_map/ppermute | solution.py:57
  1305.5 12.6 collective-permute-start.107
  1328.1 15.8 %collective-permute-start.109 = (f32[2,8,128]{2,1,0:T(8,128)S(1)}, f32[2,8,128]{2,1,0:T(8,128)S(1)}, u32[]{:S(2)}, u32[]{:S(2)}) collective-permute-start(f32[2,8,128]{2,1,0:T(8,128)S(1)} %get-tuple-element.80), channel_id=1, source_target_pairs={{32,0},{64,32},{96,64},{128,96},{160,128},{192,160},{224,192},{256... | collective-permute-start | bytes 24584 | tf_op jit(solution)/shard_map/ppermute | solution.py:57
  1345.9 12.6 collective-permute-start.119
  1360.5 14.7 collective-permute-start.117
  1393.0 12.4 collective-permute-start.115
  1407.3 16.2 %collective-permute-start.113 = (f32[1,8,128]{2,1,0:T(8,128)S(1)}, f32[1,8,128]{2,1,0:T(8,128)S(1)}, u32[]{:S(2)}, u32[]{:S(2)}) collective-permute-start(f32[1,8,128]{2,1,0:T(8,128)S(1)} %get-tuple-element.74), channel_id=1, source_target_pairs={{32,0},{64,32},{96,64},{128,96},{160,128},{192,160},{224,192},{256... | collective-permute-start | bytes 12296 | tf_op jit(solution)/shard_map/ppermute | solution.py:31
  1425.6 13.2 all-reduce.23
  1438.8 22.2 %all-reduce.21 = (f32[]{:T(128)}, f32[]{:T(128)}) all-reduce(f32[]{:T(128)} %get-tuple-element.11, f32[]{:T(128)} %get-tuple-element.12), channel_id=1, replica_groups=mesh['gx_0'=2,'gx_1'=4,'gx_2'=2,'gy_0'=8,'gy_1'=4] {'gx_1'}, use_global_device_ids=true, to_apply=%region_23.24 | all-reduce | flops 2 | bytes 16 | tf_op jit(solution)/shard_map/psum | solution.py:44
  1464.1 22.3 %all-reduce.19 = (f32[]{:T(128)}, f32[]{:T(128)}) all-reduce(f32[]{:T(128)} %get-tuple-element.9, f32[]{:T(128)} %get-tuple-element.10), channel_id=1, replica_groups=mesh['gx_0'=2,'gx_1'=4,'gx_2'=2,'gy_0'=8,'gy_1'=4] {'gy_0'}, use_global_device_ids=true, to_apply=%region_25.26 | all-reduce | flops 2 | bytes 16 | tf_op jit(solution)/shard_map/psum | solution.py:44
  (460 shorter events, 432.9 us)
Async XLA Ops:
  0.6 508.5 %collective-permute-start = (f32[2,8,128]{2,1,0:T(8,128)S(1)}, f32[2,8,128]{2,1,0:T(8,128)S(1)}, u32[]{:S(2)}, u32[]{:S(2)}) collective-permute-start(f32[2,8,128]{2,1,0:T(8,128)S(1)} %broadcast.592), channel_id=1, source_target_pairs={{0,32},{32,64},{64,96},{96,128},{128,160},{160,192},{192,224},{224... | collective-permute-start | bytes 24584 | tf_op jit(solution)/shard_map/ppermute | solution.py:55
  5.2 505.8 %collective-permute-start.1 = (f32[2,8,128]{2,1,0:T(8,128)S(1)}, f32[2,8,128]{2,1,0:T(8,128)S(1)}, u32[]{:S(2)}, u32[]{:S(2)}) collective-permute-start(f32[2,8,128]{2,1,0:T(8,128)S(1)} %broadcast.592), channel_id=1, source_target_pairs={{32,0},{64,32},{96,64},{128,96},{160,128},{192,160},{224,192},{256... | collective-permute-start | bytes 24584 | tf_op jit(solution)/shard_map/ppermute | solution.py:57
  14.7 446.3 %collective-permute-start.20 = (f32[2,2,32]{2,0,1:T(2,128)S(1)}, f32[2,2,32]{2,0,1:T(2,128)S(1)}, u32[]{:S(2)}, u32[]{:S(2)}) collective-permute-start(f32[2,2,32]{2,0,1:T(2,128)S(1)} %broadcast.610), channel_id=1, source_target_pairs={{0,32},{32,64},{64,96},{96,128},{128,160},{160,192},{192,224},{224... | collective-permute-start | bytes 1544 | tf_op jit(solution)/shard_map/ppermute | solution.py:55
  30.6 443.4 %collective-permute-start.21 = (f32[2,2,32]{2,0,1:T(2,128)S(1)}, f32[2,2,32]{2,0,1:T(2,128)S(1)}, u32[]{:S(2)}, u32[]{:S(2)}) collective-permute-start(f32[2,2,32]{2,0,1:T(2,128)S(1)} %broadcast.610), channel_id=1, source_target_pairs={{32,0},{64,32},{96,64},{128,96},{160,128},{192,160},{224,192},{256... | collective-permute-start | bytes 1544 | tf_op jit(solution)/shard_map/ppermute | solution.py:57
  61.3 414.7 %collective-permute-start.8 = (f32[2,4,64]{2,1,0:T(4,128)S(1)}, f32[2,4,64]{2,1,0:T(4,128)S(1)}, u32[]{:S(2)}, u32[]{:S(2)}) collective-permute-start(f32[2,4,64]{2,1,0:T(4,128)S(1)} %broadcast.601), channel_id=1, source_target_pairs={{0,32},{32,64},{64,96},{96,128},{128,160},{160,192},{192,224},{224... | collective-permute-start | bytes 6152 | tf_op jit(solution)/shard_map/ppermute | solution.py:55
  474.1 21.0 %collective-permute-start.4 = (f32[2,8,128]{2,1,0:T(8,128)S(1)}, f32[2,8,128]{2,1,0:T(8,128)S(1)}, u32[]{:S(2)}, u32[]{:S(2)}) collective-permute-start(f32[2,8,128]{2,1,0:T(8,128)S(1)} %get-tuple-element.101), channel_id=1, source_target_pairs={{0,32},{32,64},{64,96},{96,128},{128,160},{160,192},{192,224},{224... | collective-permute-start | bytes 24584 | tf_op jit(solution)/shard_map/ppermute | solution.py:55
  493.1 242.0 %collective-permute-start.34 = (f32[2,1,16]{2,0,1:T(2,128)S(1)}, f32[2,1,16]{2,0,1:T(2,128)S(1)}, u32[]{:S(2)}, u32[]{:S(2)}) collective-permute-start(f32[2,1,16]{2,0,1:T(2,128)S(1)} %broadcast.620), channel_id=1, source_target_pairs={{0,1},{1,2},{2,3},{3,4},{4,5},{5,6},{6,7},{7,8},{8,9},{9,10},{10,1... | collective-permute-start | bytes 392 | tf_op jit(solution)/shard_map/ppermute | solution.py:30
  495.1 28.1 %collective-permute-start.10 = (f32[12,2,64]{2,1,0:T(2,128)S(1)}, f32[12,2,64]{2,1,0:T(2,128)S(1)}, u32[]{:S(2)}, u32[]{:S(2)}) collective-permute-start(f32[12,2,64]{2,1,0:T(2,128)S(1)} %get-tuple-element.151), channel_id=1, source_target_pairs={{0,1},{1,2},{2,3},{3,4},{4,5},{5,6},{6,7},{7,8},{8,9},{9,10},{10,1... | collective-permute-start | bytes 18440 | tf_op jit(solution)/shard_map/ppermute | solution.py:55
  497.0 28.1 %collective-permute-start.11 = (f32[12,2,64]{2,1,0:T(2,128)S(1)}, f32[12,2,64]{2,1,0:T(2,128)S(1)}, u32[]{:S(2)}, u32[]{:S(2)}) collective-permute-start(f32[12,2,64]{2,1,0:T(2,128)S(1)} %get-tuple-element.152), channel_id=1, source_target_pairs={{1,0},{2,1},{3,2},{4,3},{5,4},{6,5},{7,6},{8,7},{9,8},{10,9},{11,1... | collective-permute-start | bytes 18440 | tf_op jit(solution)/shard_map/ppermute | solution.py:57
  509.1 29.2 %collective-permute-start.6 = (f32[20,2,128]{2,1,0:T(2,128)S(1)}, f32[20,2,128]{2,1,0:T(2,128)S(1)}, u32[]{:S(2)}, u32[]{:S(2)}) collective-permute-start(f32[20,2,128]{2,1,0:T(2,128)S(1)} %get-tuple-element.59), channel_id=1, source_target_pairs={{0,1},{1,2},{2,3},{3,4},{4,5},{5,6},{6,7},{7,8},{8,9},{9,10},{10,1... | collective-permute-start | bytes 61448 | tf_op jit(solution)/shard_map/ppermute | solution.py:55
  511.1 27.3 %collective-permute-start.7 = (f32[20,2,128]{2,1,0:T(2,128)S(1)}, f32[20,2,128]{2,1,0:T(2,128)S(1)}, u32[]{:S(2)}, u32[]{:S(2)}) collective-permute-start(f32[20,2,128]{2,1,0:T(2,128)S(1)} %get-tuple-element.60), channel_id=1, source_target_pairs={{1,0},{2,1},{3,2},{4,3},{5,4},{6,5},{7,6},{8,7},{9,8},{10,9},{11,1... | collective-permute-start | bytes 61448 | tf_op jit(solution)/shard_map/ppermute | solution.py:57
  539.1 33.3 %collective-permute-start.14 = (f32[16,1,128]{2,1,0:T(1,128)S(1)}, f32[16,1,128]{2,1,0:T(1,128)S(1)}, u32[]{:S(2)}, u32[]{:S(2)}) collective-permute-start(f32[16,1,128]{2,1,0:T(1,128)S(1)} %get-tuple-element.97), channel_id=1, source_target_pairs={{0,1},{1,2},{2,3},{3,4},{4,5},{5,6},{6,7},{7,8},{8,9},{9,10},{10,1... | collective-permute-start | bytes 24584 | tf_op jit(solution)/shard_map/ppermute | solution.py:30
  541.0 31.3 %collective-permute-start.15 = (f32[16,1,128]{2,1,0:T(1,128)S(1)}, f32[16,1,128]{2,1,0:T(1,128)S(1)}, u32[]{:S(2)}, u32[]{:S(2)}) collective-permute-start(f32[16,1,128]{2,1,0:T(1,128)S(1)} %get-tuple-element.98), channel_id=1, source_target_pairs={{1,0},{2,1},{3,2},{4,3},{5,4},{6,5},{7,6},{8,7},{9,8},{10,9},{11,1... | collective-permute-start | bytes 24584 | tf_op jit(solution)/shard_map/ppermute | solution.py:31
  613.6 33.7 %collective-permute-start.26 = (f32[8,1,64]{2,1,0:T(1,128)S(1)}, f32[8,1,64]{2,1,0:T(1,128)S(1)}, u32[]{:S(2)}, u32[]{:S(2)}) collective-permute-start(f32[8,1,64]{2,1,0:T(1,128)S(1)} %get-tuple-element.187), channel_id=1, source_target_pairs={{0,1},{1,2},{2,3},{3,4},{4,5},{5,6},{6,7},{7,8},{8,9},{9,10},{10,1... | collective-permute-start | bytes 6152 | tf_op jit(solution)/shard_map/ppermute | solution.py:30
  615.5 31.8 %collective-permute-start.27 = (f32[8,1,64]{2,1,0:T(1,128)S(1)}, f32[8,1,64]{2,1,0:T(1,128)S(1)}, u32[]{:S(2)}, u32[]{:S(2)}) collective-permute-start(f32[8,1,64]{2,1,0:T(1,128)S(1)} %get-tuple-element.188), channel_id=1, source_target_pairs={{1,0},{2,1},{3,2},{4,3},{5,4},{6,5},{7,6},{8,7},{9,8},{10,9},{11,1... | collective-permute-start | bytes 6152 | tf_op jit(solution)/shard_map/ppermute | solution.py:31
  627.9 18.7 %collective-permute-start.24 = (f32[1,4,64]{2,1,0:T(4,128)S(1)}, f32[1,4,64]{2,1,0:T(4,128)S(1)}, u32[]{:S(2)}, u32[]{:S(2)}) collective-permute-start(f32[1,4,64]{2,1,0:T(4,128)S(1)} %get-tuple-element.189), channel_id=1, source_target_pairs={{0,32},{32,64},{64,96},{96,128},{128,160},{160,192},{192,224},{224... | collective-permute-start | bytes 3080 | tf_op jit(solution)/shard_map/ppermute | solution.py:30
  681.0 38.5 %collective-permute-start.38 = (f32[4,1,32]{2,0,1:T(4,128)S(1)}, f32[4,1,32]{2,0,1:T(4,128)S(1)}, u32[]{:S(2)}, u32[]{:S(2)}) collective-permute-start(f32[4,1,32]{2,0,1:T(4,128)S(1)} %get-tuple-element.207), channel_id=1, source_target_pairs={{0,1},{1,2},{2,3},{3,4},{4,5},{5,6},{6,7},{7,8},{8,9},{9,10},{10,1... | collective-permute-start | bytes 1544 | tf_op jit(solution)/shard_map/ppermute | solution.py:30
  682.9 51.4 %collective-permute-start.39 = (f32[4,1,32]{2,0,1:T(4,128)S(1)}, f32[4,1,32]{2,0,1:T(4,128)S(1)}, u32[]{:S(2)}, u32[]{:S(2)}) collective-permute-start(f32[4,1,32]{2,0,1:T(4,128)S(1)} %get-tuple-element.208), channel_id=1, source_target_pairs={{1,0},{2,1},{3,2},{4,3},{5,4},{6,5},{7,6},{8,7},{9,8},{10,9},{11,1... | collective-permute-start | bytes 1544 | tf_op jit(solution)/shard_map/ppermute | solution.py:31
  695.3 18.7 %collective-permute-start.36 = (f32[1,2,32]{2,0,1:T(1,128)S(1)}, f32[1,2,32]{2,0,1:T(1,128)S(1)}, u32[]{:S(2)}, u32[]{:S(2)}) collective-permute-start(f32[1,2,32]{2,0,1:T(1,128)S(1)} %get-tuple-element.209), channel_id=1, source_target_pairs={{0,32},{32,64},{64,96},{96,128},{128,160},{160,192},{192,224},{224... | collective-permute-start | bytes 776 | tf_op jit(solution)/shard_map/ppermute | solution.py:30
  697.2 20.4 %collective-permute-start.37 = (f32[1,2,32]{2,0,1:T(1,128)S(1)}, f32[1,2,32]{2,0,1:T(1,128)S(1)}, u32[]{:S(2)}, u32[]{:S(2)}) collective-permute-start(f32[1,2,32]{2,0,1:T(1,128)S(1)} %get-tuple-element.210), channel_id=1, source_target_pairs={{32,0},{64,32},{96,64},{128,96},{160,128},{192,160},{224,192},{256... | collective-permute-start | bytes 776 | tf_op jit(solution)/shard_map/ppermute | solution.py:31
  713.9 21.2 %collective-permute-start.35 = (f32[2,1,16]{2,0,1:T(2,128)S(1)}, f32[2,1,16]{2,0,1:T(2,128)S(1)}, u32[]{:S(2)}, u32[]{:S(2)}) collective-permute-start(f32[2,1,16]{2,0,1:T(2,128)S(1)} %broadcast.620), channel_id=1, source_target_pairs={{1,0},{2,1},{3,2},{4,3},{5,4},{6,5},{7,6},{8,7},{9,8},{10,9},{11,1... | collective-permute-start | bytes 392 | tf_op jit(solution)/shard_map/ppermute | solution.py:31
  735.2 32.4 %collective-permute-start.42 = (f32[2,1,16]{2,0,1:T(2,128)S(1)}, f32[2,1,16]{2,0,1:T(2,128)S(1)}, u32[]{:S(2)}, u32[]{:S(2)}) collective-permute-start(f32[2,1,16]{2,0,1:T(2,128)S(1)} %get-tuple-element.15), channel_id=1, source_target_pairs={{0,1},{1,2},{2,3},{3,4},{4,5},{5,6},{6,7},{7,8},{8,9},{9,10},{10,1... | collective-permute-start | bytes 392 | tf_op jit(solution)/shard_map/ppermute | solution.py:30
  737.1 30.5 %collective-permute-start.43 = (f32[2,1,16]{2,0,1:T(2,128)S(1)}, f32[2,1,16]{2,0,1:T(2,128)S(1)}, u32[]{:S(2)}, u32[]{:S(2)}) collective-permute-start(f32[2,1,16]{2,0,1:T(2,128)S(1)} %get-tuple-element.15), channel_id=1, source_target_pairs={{1,0},{2,1},{3,2},{4,3},{5,4},{6,5},{7,6},{8,7},{9,8},{10,9},{11,1... | collective-permute-start | bytes 392 | tf_op jit(solution)/shard_map/ppermute | solution.py:31
  767.7 32.4 %collective-permute-start.46 = (f32[2,1,16]{2,0,1:T(2,128)S(1)}, f32[2,1,16]{2,0,1:T(2,128)S(1)}, u32[]{:S(2)}, u32[]{:S(2)}) collective-permute-start(f32[2,1,16]{2,0,1:T(2,128)S(1)} %fusion.237), channel_id=1, source_target_pairs={{0,1},{1,2},{2,3},{3,4},{4,5},{5,6},{6,7},{7,8},{8,9},{9,10},{10,1... | collective-permute-start | bytes 392 | tf_op jit(solution)/shard_map/ppermute | solution.py:30
  769.6 30.5 %collective-permute-start.47 = (f32[2,1,16]{2,0,1:T(2,128)S(1)}, f32[2,1,16]{2,0,1:T(2,128)S(1)}, u32[]{:S(2)}, u32[]{:S(2)}) collective-permute-start(f32[2,1,16]{2,0,1:T(2,128)S(1)} %fusion.237), channel_id=1, source_target_pairs={{1,0},{2,1},{3,2},{4,3},{5,4},{6,5},{7,6},{8,7},{9,8},{10,9},{11,1... | collective-permute-start | bytes 392 | tf_op jit(solution)/shard_map/ppermute | solution.py:31
  800.2 32.4 %collective-permute-start.50 = (f32[2,1,16]{2,0,1:T(2,128)S(1)}, f32[2,1,16]{2,0,1:T(2,128)S(1)}, u32[]{:S(2)}, u32[]{:S(2)}) collective-permute-start(f32[2,1,16]{2,0,1:T(2,128)S(1)} %fusion.241), channel_id=1, source_target_pairs={{0,1},{1,2},{2,3},{3,4},{4,5},{5,6},{6,7},{7,8},{8,9},{9,10},{10,1... | collective-permute-start | bytes 392 | tf_op jit(solution)/shard_map/ppermute | solution.py:30
  802.1 30.5 %collective-permute-start.51 = (f32[2,1,16]{2,0,1:T(2,128)S(1)}, f32[2,1,16]{2,0,1:T(2,128)S(1)}, u32[]{:S(2)}, u32[]{:S(2)}) collective-permute-start(f32[2,1,16]{2,0,1:T(2,128)S(1)} %fusion.241), channel_id=1, source_target_pairs={{1,0},{2,1},{3,2},{4,3},{5,4},{6,5},{7,6},{8,7},{9,8},{10,9},{11,1... | collective-permute-start | bytes 392 | tf_op jit(solution)/shard_map/ppermute | solution.py:31
  977.5 33.5 %collective-permute-start.70 = (f32[16,1,128]{2,1,0:T(1,128)S(1)}, f32[16,1,128]{2,1,0:T(1,128)S(1)}, u32[]{:S(2)}, u32[]{:S(2)}) collective-permute-start(f32[16,1,128]{2,1,0:T(1,128)S(1)} %get-tuple-element.85), channel_id=1, source_target_pairs={{0,1},{1,2},{2,3},{3,4},{4,5},{5,6},{6,7},{7,8},{8,9},{9,10},{10,1... | collective-permute-start | bytes 24584 | tf_op jit(solution)/shard_map/ppermute | solution.py:30
  979.5 31.5 %collective-permute-start.71 = (f32[16,1,128]{2,1,0:T(1,128)S(1)}, f32[16,1,128]{2,1,0:T(1,128)S(1)}, u32[]{:S(2)}, u32[]{:S(2)}) collective-permute-start(f32[16,1,128]{2,1,0:T(1,128)S(1)} %get-tuple-element.86), channel_id=1, source_target_pairs={{1,0},{2,1},{3,2},{4,3},{5,4},{6,5},{7,6},{8,7},{9,8},{10,9},{11,1... | collective-permute-start | bytes 24584 | tf_op jit(solution)/shard_map/ppermute | solution.py:31
  1052.3 33.7 %collective-permute-start.78 = (f32[8,1,64]{2,1,0:T(1,128)S(1)}, f32[8,1,64]{2,1,0:T(1,128)S(1)}, u32[]{:S(2)}, u32[]{:S(2)}) collective-permute-start(f32[8,1,64]{2,1,0:T(1,128)S(1)} %get-tuple-element.167), channel_id=1, source_target_pairs={{0,1},{1,2},{2,3},{3,4},{4,5},{5,6},{6,7},{7,8},{8,9},{9,10},{10,1... | collective-permute-start | bytes 6152 | tf_op jit(solution)/shard_map/ppermute | solution.py:30
  1054.2 31.8 %collective-permute-start.79 = (f32[8,1,64]{2,1,0:T(1,128)S(1)}, f32[8,1,64]{2,1,0:T(1,128)S(1)}, u32[]{:S(2)}, u32[]{:S(2)}) collective-permute-start(f32[8,1,64]{2,1,0:T(1,128)S(1)} %get-tuple-element.168), channel_id=1, source_target_pairs={{1,0},{2,1},{3,2},{4,3},{5,4},{6,5},{7,6},{8,7},{9,8},{10,9},{11,1... | collective-permute-start | bytes 6152 | tf_op jit(solution)/shard_map/ppermute | solution.py:31
  1066.5 18.7 %collective-permute-start.76 = (f32[1,4,64]{2,1,0:T(4,128)S(1)}, f32[1,4,64]{2,1,0:T(4,128)S(1)}, u32[]{:S(2)}, u32[]{:S(2)}) collective-permute-start(f32[1,4,64]{2,1,0:T(4,128)S(1)} %get-tuple-element.169), channel_id=1, source_target_pairs={{0,32},{32,64},{64,96},{96,128},{128,160},{160,192},{192,224},{224... | collective-permute-start | bytes 3080 | tf_op jit(solution)/shard_map/ppermute | solution.py:30
  1119.7 33.7 %collective-permute-start.86 = (f32[4,1,32]{2,0,1:T(4,128)S(1)}, f32[4,1,32]{2,0,1:T(4,128)S(1)}, u32[]{:S(2)}, u32[]{:S(2)}) collective-permute-start(f32[4,1,32]{2,0,1:T(4,128)S(1)} %get-tuple-element.195), channel_id=1, source_target_pairs={{0,1},{1,2},{2,3},{3,4},{4,5},{5,6},{6,7},{7,8},{8,9},{9,10},{10,1... | collective-permute-start | bytes 1544 | tf_op jit(solution)/shard_map/ppermute | solution.py:30
  1121.6 31.7 %collective-permute-start.87 = (f32[4,1,32]{2,0,1:T(4,128)S(1)}, f32[4,1,32]{2,0,1:T(4,128)S(1)}, u32[]{:S(2)}, u32[]{:S(2)}) collective-permute-start(f32[4,1,32]{2,0,1:T(4,128)S(1)} %get-tuple-element.196), channel_id=1, source_target_pairs={{1,0},{2,1},{3,2},{4,3},{5,4},{6,5},{7,6},{8,7},{9,8},{10,9},{11,1... | collective-permute-start | bytes 1544 | tf_op jit(solution)/shard_map/ppermute | solution.py:31
  1133.9 18.7 %collective-permute-start.84 = (f32[1,2,32]{2,0,1:T(1,128)S(1)}, f32[1,2,32]{2,0,1:T(1,128)S(1)}, u32[]{:S(2)}, u32[]{:S(2)}) collective-permute-start(f32[1,2,32]{2,0,1:T(1,128)S(1)} %get-tuple-element.197), channel_id=1, source_target_pairs={{0,32},{32,64},{64,96},{96,128},{128,160},{160,192},{192,224},{224... | collective-permute-start | bytes 776 | tf_op jit(solution)/shard_map/ppermute | solution.py:30
  1153.7 32.4 %collective-permute-start.90 = (f32[2,1,16]{2,0,1:T(2,128)S(1)}, f32[2,1,16]{2,0,1:T(2,128)S(1)}, u32[]{:S(2)}, u32[]{:S(2)}) collective-permute-start(f32[2,1,16]{2,0,1:T(2,128)S(1)} %fusion.259), channel_id=1, source_target_pairs={{0,1},{1,2},{2,3},{3,4},{4,5},{5,6},{6,7},{7,8},{8,9},{9,10},{10,1... | collective-permute-start | bytes 392 | tf_op jit(solution)/shard_map/ppermute | solution.py:30
  1155.6 30.5 %collective-permute-start.91 = (f32[2,1,16]{2,0,1:T(2,128)S(1)}, f32[2,1,16]{2,0,1:T(2,128)S(1)}, u32[]{:S(2)}, u32[]{:S(2)}) collective-permute-start(f32[2,1,16]{2,0,1:T(2,128)S(1)} %fusion.259), channel_id=1, source_target_pairs={{1,0},{2,1},{3,2},{4,3},{5,4},{6,5},{7,6},{8,7},{9,8},{10,9},{11,1... | collective-permute-start | bytes 392 | tf_op jit(solution)/shard_map/ppermute | solution.py:31
  1186.2 32.4 %collective-permute-start.94 = (f32[2,1,16]{2,0,1:T(2,128)S(1)}, f32[2,1,16]{2,0,1:T(2,128)S(1)}, u32[]{:S(2)}, u32[]{:S(2)}) collective-permute-start(f32[2,1,16]{2,0,1:T(2,128)S(1)} %fusion.249), channel_id=1, source_target_pairs={{0,1},{1,2},{2,3},{3,4},{4,5},{5,6},{6,7},{7,8},{8,9},{9,10},{10,1... | collective-permute-start | bytes 392 | tf_op jit(solution)/shard_map/ppermute | solution.py:30
  1188.1 30.5 %collective-permute-start.95 = (f32[2,1,16]{2,0,1:T(2,128)S(1)}, f32[2,1,16]{2,0,1:T(2,128)S(1)}, u32[]{:S(2)}, u32[]{:S(2)}) collective-permute-start(f32[2,1,16]{2,0,1:T(2,128)S(1)} %fusion.249), channel_id=1, source_target_pairs={{1,0},{2,1},{3,2},{4,3},{5,4},{6,5},{7,6},{8,7},{9,8},{10,9},{11,1... | collective-permute-start | bytes 392 | tf_op jit(solution)/shard_map/ppermute | solution.py:31
  1218.7 32.4 %collective-permute-start.98 = (f32[2,1,16]{2,0,1:T(2,128)S(1)}, f32[2,1,16]{2,0,1:T(2,128)S(1)}, u32[]{:S(2)}, u32[]{:S(2)}) collective-permute-start(f32[2,1,16]{2,0,1:T(2,128)S(1)} %fusion.253), channel_id=1, source_target_pairs={{0,1},{1,2},{2,3},{3,4},{4,5},{5,6},{6,7},{7,8},{8,9},{9,10},{10,1... | collective-permute-start | bytes 392 | tf_op jit(solution)/shard_map/ppermute | solution.py:30
  1220.6 30.5 %collective-permute-start.99 = (f32[2,1,16]{2,0,1:T(2,128)S(1)}, f32[2,1,16]{2,0,1:T(2,128)S(1)}, u32[]{:S(2)}, u32[]{:S(2)}) collective-permute-start(f32[2,1,16]{2,0,1:T(2,128)S(1)} %fusion.253), channel_id=1, source_target_pairs={{1,0},{2,1},{3,2},{4,3},{5,4},{6,5},{7,6},{8,7},{9,8},{10,9},{11,1... | collective-permute-start | bytes 392 | tf_op jit(solution)/shard_map/ppermute | solution.py:31
  1326.2 34.3 %collective-permute-start.108 = (f32[2,8,128]{2,1,0:T(8,128)S(1)}, f32[2,8,128]{2,1,0:T(8,128)S(1)}, u32[]{:S(2)}, u32[]{:S(2)}) collective-permute-start(f32[2,8,128]{2,1,0:T(8,128)S(1)} %get-tuple-element.79), channel_id=1, source_target_pairs={{0,32},{32,64},{64,96},{96,128},{128,160},{160,192},{192,224},{224... | collective-permute-start | bytes 24584 | tf_op jit(solution)/shard_map/ppermute | solution.py:55
  1328.1 47.1 %collective-permute-start.109 = (f32[2,8,128]{2,1,0:T(8,128)S(1)}, f32[2,8,128]{2,1,0:T(8,128)S(1)}, u32[]{:S(2)}, u32[]{:S(2)}) collective-permute-start(f32[2,8,128]{2,1,0:T(8,128)S(1)} %get-tuple-element.80), channel_id=1, source_target_pairs={{32,0},{64,32},{96,64},{128,96},{160,128},{192,160},{224,192},{256... | collective-permute-start | bytes 24584 | tf_op jit(solution)/shard_map/ppermute | solution.py:57
  1344.0 45.3 %collective-permute-start.118 = (f32[16,1,128]{2,1,0:T(1,128)S(1)}, f32[16,1,128]{2,1,0:T(1,128)S(1)}, u32[]{:S(2)}, u32[]{:S(2)}) collective-permute-start(f32[16,1,128]{2,1,0:T(1,128)S(1)} %get-tuple-element.63), channel_id=1, source_target_pairs={{0,1},{1,2},{2,3},{3,4},{4,5},{5,6},{6,7},{7,8},{8,9},{9,10},{10,1... | collective-permute-start | bytes 24584 | tf_op jit(solution)/shard_map/ppermute | solution.py:30
  1345.9 43.4 %collective-permute-start.119 = (f32[16,1,128]{2,1,0:T(1,128)S(1)}, f32[16,1,128]{2,1,0:T(1,128)S(1)}, u32[]{:S(2)}, u32[]{:S(2)}) collective-permute-start(f32[16,1,128]{2,1,0:T(1,128)S(1)} %get-tuple-element.64), channel_id=1, source_target_pairs={{1,0},{2,1},{3,2},{4,3},{5,4},{6,5},{7,6},{8,7},{9,8},{10,9},{11,1... | collective-permute-start | bytes 24584 | tf_op jit(solution)/shard_map/ppermute | solution.py:31
  1360.5 28.8 %collective-permute-start.117 = (f32[1,8,128]{2,1,0:T(8,128)S(1)}, f32[1,8,128]{2,1,0:T(8,128)S(1)}, u32[]{:S(2)}, u32[]{:S(2)}) collective-permute-start(f32[1,8,128]{2,1,0:T(8,128)S(1)} %get-tuple-element.66), channel_id=1, source_target_pairs={{32,0},{64,32},{96,64},{128,96},{160,128},{192,160},{224,192},{256... | collective-permute-start | bytes 12296 | tf_op jit(solution)/shard_map/ppermute | solution.py:31
  1391.1 33.2 %collective-permute-start.114 = (f32[16,1,128]{2,1,0:T(1,128)S(1)}, f32[16,1,128]{2,1,0:T(1,128)S(1)}, u32[]{:S(2)}, u32[]{:S(2)}) collective-permute-start(f32[16,1,128]{2,1,0:T(1,128)S(1)} %get-tuple-element.71), channel_id=1, source_target_pairs={{0,1},{1,2},{2,3},{3,4},{4,5},{5,6},{6,7},{7,8},{8,9},{9,10},{10,1... | collective-permute-start | bytes 24584 | tf_op jit(solution)/shard_map/ppermute | solution.py:30
  1393.0 31.3 %collective-permute-start.115 = (f32[16,1,128]{2,1,0:T(1,128)S(1)}, f32[16,1,128]{2,1,0:T(1,128)S(1)}, u32[]{:S(2)}, u32[]{:S(2)}) collective-permute-start(f32[16,1,128]{2,1,0:T(1,128)S(1)} %get-tuple-element.72), channel_id=1, source_target_pairs={{1,0},{2,1},{3,2},{4,3},{5,4},{6,5},{7,6},{8,7},{9,8},{10,9},{11,1... | collective-permute-start | bytes 24584 | tf_op jit(solution)/shard_map/ppermute | solution.py:31
  (73 other events, 1231.1 us)
where the time goes:
time: 1510 us; the launch traced here: 1500 us
  starting transfers between devices  926 us (61%)
  other arithmetic  370 us (25%)
  blocking collectives  138 us (9%)
  local copies, waits for them, and re-layouts  32.7 us (2%)
  waiting for transfers between devices  26 us (2%)
    ppermute x30, starting transfers between devices, extended(): lax.ppermute(initial, axis, [(b, a) for a, b in up])  410 us
    ppermute x30, starting transfers between devices, with_halo(): lax.ppermute(head, axis, [((i + 1) % count, i) for i in range(count)])  390 us
    scatter-add x1, other arithmetic, per_device(): jnp.zeros((block_cells + 1,), jnp.float32).at[target].add(masses)  351 us
    psum x10, blocking collectives, by_axis(): x = lax.psum(x, axis)  138 us
    ppermute x30, starting transfers between devices, with_halo(): lax.ppermute(tail, axis, [(i, (i + 1) % count) for i in range(count)])  65.7 us
    ppermute x30, starting transfers between devices, extended(): lax.ppermute(last, axis, up)  61 us
  transfers between devices with their start and end apart: 120, of which 35 were waited for; matrix products, arithmetic and copies ran while one was open for 25% of the time, Pallas kernels for 0%

commit v1 on v0

v1 whole, which is shorter than its diff:
```python
import functools

import jax
import jax.numpy as jnp
from jax import lax
from jax.experimental import pallas as pl
from jax.experimental.pallas import tpu as pltpu
from jax.sharding import Mesh
from jax.sharding import PartitionSpec as P

CX = 16
CY = 8
NZ = 128
GX = ("gx_0", "gx_1", "gx_2")
GY = ("gy_0", "gy_1")
Z_RING = ("gx_0", "gy_0")
PLANE = ("gx_1", "gx_2", "gy_1")
TILES_X = 16
TILES_Y = 32
GRID_CELLS = 256 * 256 * 128
COARSE_CELLS = 64 * 64 * 32

coupling = 0.03125
norm_eps = 1e-06

W0X, W0Y = 64, 56
W1X, W1Y = 32, 32
W2X, W2Y = 36, 40
W3X, W3Y = 18, 24
VMEM = pltpu.VMEM


def deposit_kernel(cell_ref, mass_ref, out_ref):
    rows = lax.broadcasted_iota(jnp.int32, (128, 128), 0)

    def step(t, acc):
        cells = cell_ref[pl.ds(pl.multiple_of(t * 8, 8), 8), :]
        masses = mass_ref[pl.ds(pl.multiple_of(t * 8, 8), 8), :]
        high = cells >> 7
        low = cells & 127
        coarse = masses.astype(jnp.bfloat16).astype(jnp.float32)
        fine = masses - coarse
        left, right = [], []
        for r in range(8):
            hit = rows == high[r : r + 1, :]
            first = jnp.where(hit, coarse[r : r + 1, :], 0.0).astype(jnp.bfloat16)
            second = jnp.where(hit, fine[r : r + 1, :], 0.0).astype(jnp.bfloat16)
            left.append(jnp.concatenate([first, second], axis=0))
            right.append(jnp.where(rows == low[r : r + 1, :], 1.0, 0.0).astype(jnp.bfloat16))
        left = jnp.concatenate(left, axis=1)
        right = jnp.concatenate(right, axis=1)
        return acc + lax.dot_general(left, right, (((1,), (1,)), ((), ())), preferred_element_type=jnp.float32)

    total = lax.fori_loop(0, cell_ref.shape[0] // 8, step, jnp.zeros((256, 128), jnp.float32))
    out_ref[...] = total[:128] + total[128:]


def row_parity(rows, lanes_per_cell, extra=0):
    j = lax.broadcasted_iota(jnp.int32, (rows, NZ), 0)
    z = lax.broadcasted_iota(jnp.int32, (rows, NZ), 1) // lanes_per_cell
    return (j + z + extra) & 1


def around(ref, i, rows, lanes):
    c = ref[i]
    n = ref[i - 1] + ref[i + 1]
    n = n + (pltpu.roll(c, 1, 0) + pltpu.roll(c, rows - 1, 0))
    return c, n + (pltpu.roll(c, lanes, 1) + pltpu.roll(c, NZ - lanes, 1))


def pair_z(t, lanes):
    z = lax.broadcasted_iota(jnp.int32, t.shape, 1) // lanes
    return t + jnp.where((z & 1) == 0, pltpu.roll(t, NZ - lanes, 1), pltpu.roll(t, lanes, 1))


def loop(lo, hi, body, unroll=2):
    def step(i, carry):
        body(i)
        return carry

    lax.fori_loop(lo, hi, step, 0, unroll=unroll)


def first_sweep(u, b, parity, rows, lanes, s, lo, hi):
    def body(i):
        c, n = around(b, i, rows, lanes)
        red = parity == (i & 1)
        u[i] = jnp.where(red, c * (s / 6.0), n * (s / 36.0) + c * (s / 6.0))

    loop(lo, hi, body)


def half_sweep(u, get_b, parity, colour, rows, lanes, s, lo, hi):
    def body(i):
        c, n = around(u, i, rows, lanes)
        chosen = parity == ((i + colour) & 1)
        u[i] = jnp.where(chosen, (n + s * get_b(i)) * (1.0 / 6.0), c)

    loop(lo, hi, body)


def residual_at(u, b, i, rows, lanes, s):
    c, n = around(u, i, rows, lanes)
    return b - (6.0 * c - n) * (1.0 / s)


def restrict_to(out, u, get_b, rows, lanes, s, lo, hi, scr, out_rows):
    def body(p):
        t = residual_at(u, get_b(2 * p), 2 * p, rows, lanes, s)
        t = t + residual_at(u, get_b(2 * p + 1), 2 * p + 1, rows, lanes, s)
        scr[0:rows, :] = pair_z(t, lanes)
        out[p] = (scr[pl.ds(0, out_rows, 2), :] + scr[pl.ds(1, out_rows, 2), :]) * 0.125

    loop(lo, hi, body, 1)


def spread_rows(value, rows, scr):
    scr[pl.ds(0, rows, 2), :] = value
    scr[pl.ds(1, rows, 2), :] = value
    return scr[0 : 2 * rows, :]


def own_coarse(u1, b1, send_ref):
    lane = lax.broadcasted_iota(jnp.int32, (W1Y, NZ), 1) & 3
    packed = jnp.zeros((W1Y, NZ), jnp.float32)
    for x in range(4):
        i = 12 + 2 * x
        t = residual_at(u1, b1[i], i, W1Y, 2, 4.0) + residual_at(u1, b1[i + 1], i + 1, W1Y, 2, 4.0)
        t = pair_z(t, 2)
        t = (t + pltpu.roll(t, W1Y - 1, 0)) * 0.125
        packed = jnp.where(lane == x, t, packed)
    for k in range(send_ref.shape[0]):
        send_ref[k, 0:1, :] = packed[12:13, :]
        send_ref[k, 1:2, :] = packed[14:15, :]


def coarse_solve(pos_ref, ag, shift, pw, b2, u2, b3, u3, scr):
    gx, gy = pos_ref[0], pos_ref[1]
    pw[...] = jnp.zeros(pw.shape, jnp.float32)
    for tx in range(9):
        x = lax.rem(gx + (tx - 4 + TILES_X), TILES_X)
        for ty in range(17):
            y = lax.rem(gy + (ty - 8 + TILES_Y), TILES_Y)
            plane = (x & 7) * 4 + (y & 3)
            ring = (x >> 3) * 8 + (y >> 2)
            pw[tx, 2 * ty : 2 * ty + 2, :] = ag[plane * 16 + ring]
    lane = lax.broadcasted_iota(jnp.int32, (W2Y, NZ), 1) & 3

    def unpack(tx):
        t = pw[tx]
        for j in range(4):
            v = jnp.where(lane == j, t, 0.0)
            v = v + pltpu.roll(v, 1 if j % 2 == 0 else NZ - 1, 1)
            v = v + pltpu.roll(v, 2 if j < 2 else NZ - 2, 1)
            b2[4 * tx + j] = v - shift

    loop(0, 9, unpack, 1)
    par2 = row_parity(W2Y, 4)
    u2[0] = jnp.zeros((W2Y, NZ), jnp.float32)
    u2[W2X - 1] = jnp.zeros((W2Y, NZ), jnp.float32)
    first_sweep(u2, b2, par2, W2Y, 4, 16.0, 1, W2X - 1)
    scr[32:64, :] = jnp.zeros((32, NZ), jnp.float32)
    for i in (0, W3X - 1):
        b3[i] = jnp.zeros((W3Y, NZ), jnp.float32)
        u3[i] = jnp.zeros((W3Y, NZ), jnp.float32)
    restrict_to(b3, u2, lambda i: b2[i], W2Y, 4, 16.0, 1, W3X - 1, scr, W3Y)
    par3 = row_parity(W3Y, 8, gy)
    first_sweep(u3, b3, par3, W3Y, 8, 64.0, 1, W3X - 1)
    for colour in (0, 1):
        half_sweep(u3, lambda i: b3[i], par3, colour, W3Y, 8, 64.0, 1, W3X - 1)

    def add(p):
        c = spread_rows(u3[p], W3Y, scr)[0:W2Y]
        u2[2 * p] = u2[2 * p] + c
        u2[2 * p + 1] = u2[2 * p + 1] + c

    loop(4, 14, add, 1)
    half_sweep(u2, lambda i: b2[i], par2, 0, W2Y, 4, 16.0, 9, 27)
    half_sweep(u2, lambda i: b2[i], par2, 1, W2Y, 4, 16.0, 10, 26)


def up_level1(v1, u1, b1, shift, u2, scr):
    def add(p):
        c = spread_rows(u2[p + 10, 10:26, :], 16, scr)
        v1[2 * p] = u1[2 * p] - shift * (4.0 / 3.0) + c
        v1[2 * p + 1] = u1[2 * p + 1] - shift * (4.0 / 3.0) + c

    loop(0, 16, add, 1)
    par1 = row_parity(W1Y, 2)
    for colour in (0, 1):
        half_sweep(v1, lambda i: b1[i] - shift, par1, colour, W1Y, 2, 4.0, 1, W1X - 1)


def up_level0(v0, u0, d, shift, base, v1, scr, lo, hi):
    def add(p):
        c = spread_rows(v1[p], W1Y, scr)[0:W0Y]
        v0[2 * p] = u0[2 * p] - base + c
        v0[2 * p + 1] = u0[2 * p + 1] - base + c

    loop(lo // 2, hi // 2, add, 1)
    par0 = row_parity(W0Y, 1)
    for colour in (0, 1):
        half_sweep(v0, lambda i: d[i] - shift, par0, colour, W0Y, 1, 1.0, lo + 1, hi - 1)


def down_level1(u1, b1, send_ref):
    u1[0] = jnp.zeros((W1Y, NZ), jnp.float32)
    u1[W1X - 1] = jnp.zeros((W1Y, NZ), jnp.float32)
    first_sweep(u1, b1, row_parity(W1Y, 2), W1Y, 2, 4.0, 1, W1X - 1)
    own_coarse(u1, b1, send_ref)


def pre_kernel(pos_ref, x_ref, p1e, p1o, p2a, p2b, p3a, p3b, send_ref, d, u0, b1, u1, scr):
    gy = pos_ref[1]
    d[:, 24:32, :] = x_ref[...]

    def place(first, second, offset):
        d[:, 24 + offset : 32 + offset, :] = first[...]
        d[:, 24 - offset : 32 - offset, :] = second[...]

    even = (gy & 1) == 0
    low = (gy & 3) < 2
    for cond, a, b, offset in ((even, p1e, p1o, 8), (low, p2a, p2b, 16), (even, p3a, p3b, 24)):
        pl.when(cond)(functools.partial(place, a, b, offset))
        pl.when(jnp.logical_not(cond))(functools.partial(place, b, a, offset))
    for i in (0, W0X - 1):
        u0[i] = jnp.zeros((W0Y, NZ), jnp.float32)
    first_sweep(u0, d, row_parity(W0Y, 1), W0Y, 1, 1.0, 1, W0X - 1)
    scr[...] = jnp.zeros(scr.shape, jnp.float32)
    for i in (0, W1X - 1):
        b1[i] = jnp.zeros((W1Y, NZ), jnp.float32)
    restrict_to(b1, u0, lambda i: d[i], W0Y, 1, 1.0, 1, W1X - 1, scr, W1Y)
    down_level1(u1, b1, send_ref)


def own_squares(u, d, shift):
    total = jnp.zeros((CY, NZ), jnp.float32)
    for i in range(24, 40):
        r = residual_at(u, d[i] - shift, i, W0Y, 1, 1.0)[24:32]
        total = total + r * r
    return total


def mid_kernel(pos_ref, ag, d, u0, b1, u1, send_ref, u0n, b1n, u1n, stat_ref, v1, pw, b2, u2, b3, u3, scr):
    total = jnp.sum(jnp.sum(ag[...], axis=0))
    mean = total * (1.0 / COARSE_CELLS)
    coarse_solve(pos_ref, ag, mean, pw, b2, u2, b3, u3, scr)
    up_level1(v1, u1, b1, mean, u2, scr)
    up_level0(u0n, u0, d, mean, mean * (1.0 / 3.0), v1, scr, 0, W0X)
    stat_ref[0:8, :] = own_squares(u0n, d, mean)
    stat_ref[8:16, :] = jnp.full((8, NZ), mean, jnp.float32)
    par0 = row_parity(W0Y, 1)
    for colour in (0, 1):
        half_sweep(u0n, lambda i: d[i] - mean, par0, colour, W0Y, 1, 1.0, 8, 56)
    scr[...] = jnp.zeros(scr.shape, jnp.float32)
    for i in range(W1X):
        if i < 6 or i >= 26:
            b1n[i] = jnp.zeros((W1Y, NZ), jnp.float32)
    restrict_to(b1n, u0n, lambda i: d[i] - mean, W0Y, 1, 1.0, 6, 26, scr, W1Y)
    down_level1(u1n, b1n, send_ref)


def post_kernel(pos_ref, ag, d, u0, b1, u1, stat, pot_ref, res_ref, sums_ref, v0, v1, pw, b2, u2, b3, u3, scr):
    mean = jnp.max(stat[8:16, :])
    coarse_solve(pos_ref, ag, 0.0, pw, b2, u2, b3, u3, scr)
    up_level1(v1, u1, b1, 0.0, u2, scr)
    up_level0(v0, u0, d, mean, 0.0, v1, scr, 16, 48)
    inv = 1.0 / jnp.full((CY, NZ), mean, jnp.float32)
    total = jnp.zeros((CY, NZ), jnp.float32)
    for i in range(16):
        r = residual_at(v0, d[24 + i] - mean, 24 + i, W0Y, 1, 1.0)[24:32] * inv
        total = total + r * r
        res_ref[i] = -r
        pot_ref[i] = v0[24 + i, 24:32, :] * (-coupling * inv)
    first = stat[0:8, :] * (inv * inv)
    lane = lax.broadcasted_iota(jnp.int32, (1, NZ), 1)
    both = jnp.where(lane == 0, jnp.sum(first), 0.0) + jnp.where(lane == 1, jnp.sum(total), 0.0)
    for k in range(sums_ref.shape[0]):
        sums_ref[k] = both


def f32(*shape):
    return jax.ShapeDtypeStruct(shape, jnp.float32)


def vmem(*shape):
    return pltpu.VMEM(shape, jnp.float32)


COARSE_SCRATCH = (vmem(9, W2Y, NZ), vmem(W2X, W2Y, NZ), vmem(W2X, W2Y, NZ), vmem(W3X, W3Y, NZ), vmem(W3X, W3Y, NZ), vmem(64, NZ))
LEVELS_OUT = (f32(W0X, W0Y, NZ), f32(W1X, W1Y, NZ), f32(W1X, W1Y, NZ))


def call(kernel, outs, scratch, *args, pos=None):
    whole = pl.BlockSpec(memory_space=VMEM)
    specs = [whole] * len(args)
    if pos is not None:
        specs = [pl.BlockSpec(memory_space=pltpu.SMEM)] + specs
        args = (pos, *args)
    return pl.pallas_call(
        kernel,
        out_shape=outs,
        in_specs=specs,
        out_specs=jax.tree.map(lambda _: whole, outs),
        scratch_shapes=list(scratch),
    )(*args)


def pairs(count, step, chosen):
    both = []
    for i in range(count):
        if chosen(i):
            both += [(i, (i + step) % count), ((i + step) % count, i)]
    return both


def swap(x, axis, step, chosen):
    return lax.ppermute(x, axis, pairs(lax.axis_size(axis), step, chosen))


def even(i):
    return i % 2 == 0


def odd(i):
    return i % 2 == 1


def gather_all(block):
    ring = lax.all_to_all(block, Z_RING, 0, 0)
    copies = jnp.broadcast_to(ring[None], (32, *ring.shape))
    return lax.all_to_all(copies, PLANE, 0, 0)


def x_window(d):
    first = lax.axis_index("gx_2") == 0
    partner = swap(d, GX, 1, even)
    chip = jnp.where(first, jnp.concatenate([d, partner]), jnp.concatenate([partner, d]))
    far = swap(jnp.where(first, chip[:24], chip[8:]), GX, 1, odd)
    near = swap(jnp.where(first, chip[24:], chip[:8]), GX, 3, even)
    return jnp.where(first, jnp.concatenate([far, chip, near]), jnp.concatenate([near, chip, far]))


def per_device(particle_cell, particle_mass):
    tile_x = lax.axis_index(GX)
    tile_y = lax.axis_index(GY)
    pos = jnp.stack([tile_x, tile_y]).astype(jnp.int32)
    cells = particle_cell.reshape(512, 128)
    masses = particle_mass.reshape(512, 128)
    density = call(deposit_kernel, f32(128, 128), (), cells, masses).reshape(CX, CY, NZ)
    wide = x_window(density)
    strips = (
        swap(wide, GY, 1, even),
        swap(wide, GY, 1, odd),
        swap(wide, GY, 2, lambda i: i % 4 < 2),
        swap(wide, GY, 2, lambda i: i % 4 >= 2),
        swap(wide, GY, 3, even),
        swap(wide, GY, 3, odd),
    )
    send, d, u0, b1, u1 = call(
        pre_kernel, (f32(16, 2, NZ), f32(W0X, W0Y, NZ), *LEVELS_OUT), (vmem(64, NZ),), wide, *strips, pos=pos
    )
    got = gather_all(send).reshape(512, 2, NZ)
    send, u0, b1, u1, stat = call(
        mid_kernel,
        (f32(16, 2, NZ), *LEVELS_OUT, f32(16, NZ)),
        (vmem(W1X, W1Y, NZ), *COARSE_SCRATCH),
        got, d, u0, b1, u1,
        pos=pos,
    )
    got = gather_all(send).reshape(512, 2, NZ)
    potential, residual, sums = call(
        post_kernel,
        (f32(CX, CY, NZ), f32(CX, CY, NZ), f32(16, 1, NZ)),
        (vmem(W0X, W0Y, NZ), vmem(W1X, W1Y, NZ), *COARSE_SCRATCH),
        got, d, u0, b1, u1, stat,
        pos=pos,
    )
    ring = jnp.sum(lax.all_to_all(sums, Z_RING, 0, 0), axis=0)
    total = jnp.sum(lax.all_to_all(jnp.broadcast_to(ring[None], (32, 1, NZ)), PLANE, 0, 0), axis=(0, 1))
    norms = jnp.sqrt(total[:2] / GRID_CELLS + norm_eps)
    return potential, residual, norms


def solution(mesh):
    split = Mesh(mesh.devices.reshape(2, 4, 2, 8, 4), ("gx_0", "gx_1", "gx_2", "gy_0", "gy_1"))
    placed = (P(GX, GY, None), P(GX, GY, None))
    return jax.shard_map(
        per_device,
        mesh=split,
        in_specs=placed,
        out_specs=(P(GX, GY, None), P(GX, GY, None), P()),
        check_vma=False,
    )
```

time: 1510 us -> 262 us (0.17)
  starting transfers between devices: 926 us -> 56.8 us
  other arithmetic: 370 us -> 2.18 us
  Pallas kernels: 0 us -> 90.8 us
  blocking collectives: 138 us -> 96.9 us
  local copies, waits for them, and re-layouts: 32.7 us -> 1.18 us
    ppermute x120 -> x9, starting transfers between devices: 926 us -> 56.8 us  [swap(): return lax.ppermute(x, axis, pairs(lax.axis_size(axis), step, chosen))]
    scatter-add x1 -> x0, other arithmetic: 351 us -> none  [per_device(): jnp.zeros((block_cells + 1,), jnp.float32).at[target].add(masses)]
    psum x10 -> x0, blocking collectives: 138 us -> none  [by_axis(): x = lax.psum(x, axis)]
    all_to_all x0 -> x6, blocking collectives: none -> 96.9 us  [the longest x2 35.1 us: gather_all(): return lax.all_to_all(copies, PLANE, 0, 0)]
    pallas_call x0 -> x4, Pallas kernels: none -> 90.8 us  [call(): pl.pallas_call(kernel, out_shape=outs, in_specs=specs, out_specs=jax.tree...]
    reshape x8 -> x0, local copies, waits for them, and re-layouts: 20.7 us -> none  [the longest x4 12.2 us: restrict(): values.reshape(rows_x // 2, 2, rows_y // 2, 2, rows_z // 2, 2)]
  transfers between devices with their start and end apart: 120 -> 9, of which waited for: 35 -> 5; matrix products, arithmetic and copies ran while one was open for 25% -> 0% of each run, Pallas kernels for 0% -> 0%
where the time goes in v1:
time: 262 us; the launch traced here: 261 us
  blocking collectives  96.9 us (37%)
  Pallas kernels  90.8 us (35%)
  starting transfers between devices  56.8 us (22%)
  waiting for transfers between devices  12.7 us (5%)
    pallas_call x4, Pallas kernels, call(): pl.pallas_call(kernel, out_shape=outs, in_specs=specs, out_specs=jax.tree...  90.8 us
    ppermute x9, starting transfers between devices, swap(): return lax.ppermute(x, axis, pairs(lax.axis_size(axis), step, chosen))  56.8 us
    all_to_all x2, blocking collectives, gather_all(): return lax.all_to_all(copies, PLANE, 0, 0)  35.1 us
    all_to_all x2, blocking collectives, gather_all(): ring = lax.all_to_all(block, Z_RING, 0, 0)  34.9 us
    all_to_all x1, blocking collectives, per_device(): ring = jnp.sum(lax.all_to_all(sums, Z_RING, 0, 0), axis=0)  14.5 us
    ppermute x9, waiting for transfers between devices, swap(): return lax.ppermute(x, axis, pairs(lax.axis_size(axis), step, chosen))  12.7 us
    all_to_all x1, blocking collectives, per_device(): lax.all_to_all(jnp.broadcast_to(ring[None], (32, 1, NZ)), PLANE, 0, 0)  12.4 us
  transfers between devices with their start and end apart: 9, of which 5 were waited for; matrix products, arithmetic and copies ran while one was open for 0% of the time, Pallas kernels for 0%

profile of v1, /device:TPU:1, one launch (start us, length us, event | category | flops | bytes accessed | tf_op | source)
XLA Modules:
  0.0 261.4 jit_solution(12061099259001896105)
XLA Ops:
  0.6 22.4 %shard_map.49 = f32[128,128]{1,0:T(8,128)} custom-call(s32[512,128]{1,0:T(8,128)} %bitcast.10, f32[512,128]{1,0:T(8,128)} %bitcast.11), custom_call_target="tpu_custom_call" | custom-call | tf_op jit(solution)/shard_map/pallas_call | solution.py:300
  23.1 8.7 %collective-permute-start = (f32[16,8,128]{2,1,0:T(8,128)}, f32[16,8,128]{2,1,0:T(8,128)S(1)}, u32[]{:S(2)}, u32[]{:S(2)}) collective-permute-start(f32[16,8,128]{2,1,0:T(8,128)} %bitcast.12), channel_id=1, source_target_pairs={{0,32},{32,0},{64,96},{96,64},{128,160},{160,128},{192,224},{224,1... | collective-permute-start | bytes 196616 | tf_op jit(solution)/shard_map/ppermute | solution.py:318
  31.8 1.1 collective-permute-done
  32.9 0.9 maximum_select_fusion.1
  33.8 1.9 collective-permute-start.1
  35.8 13.3 %collective-permute-start.2 = (f32[8,8,128]{2,1,0:T(8,128)S(1)}, f32[8,8,128]{2,1,0:T(8,128)S(1)}, u32[]{:S(2)}, u32[]{:S(2)}) collective-permute-start(f32[8,8,128]{2,1,0:T(8,128)S(1)} %slice_select_fusion.1), channel_id=1, source_target_pairs={{0,96},{96,0},{64,160},{160,64},{128,224},{224,128},{192,288},{288... | collective-permute-start | bytes 98312 | tf_op jit(solution)/shard_map/ppermute | solution.py:318
  49.1 2.8 %collective-permute-done.2 = f32[8,8,128]{2,1,0:T(8,128)S(1)} collective-permute-done((f32[8,8,128]{2,1,0:T(8,128)S(1)}, f32[8,8,128]{2,1,0:T(8,128)S(1)}, u32[]{:S(2)}, u32[]{:S(2)}) %collective-permute-start.2) | collective-permute-done | bytes 32800 | tf_op jit(solution)/shard_map/ppermute | solution.py:318
  51.8 0.0 collective-permute-done.1
  51.9 0.0 copy-start
  51.9 12.2 %collective-permute-start.8 = (f32[64,8,128]{2,1,0:T(8,128)S(1)}, f32[64,8,128]{2,1,0:T(8,128)S(1)}, u32[]{:S(2)}, u32[]{:S(2)}) collective-permute-start(f32[64,8,128]{2,1,0:T(8,128)S(1)} %maximum_select_fusion.x_ref), channel_id=1, source_target_pairs={{1,4},{4,1},{3,6},{6,3},{5,8},{8,5},{7,10},{10,7},{9,12},{12,9},{1... | collective-permute-start | bytes 786440 | tf_op jit(solution)/shard_map/ppermute | solution.py:318
  64.1 1.9 collective-permute-start.7
  66.0 4.2 %collective-permute-start.6 = (f32[64,8,128]{2,1,0:T(8,128)S(1)}, f32[64,8,128]{2,1,0:T(8,128)S(1)}, u32[]{:S(2)}, u32[]{:S(2)}) collective-permute-start(f32[64,8,128]{2,1,0:T(8,128)S(1)} %maximum_select_fusion.x_ref), channel_id=1, source_target_pairs={{2,4},{4,2},{3,5},{5,3},{6,8},{8,6},{7,9},{9,7},{10,12},{12,10},{1... | collective-permute-start | bytes 786440 | tf_op jit(solution)/shard_map/ppermute | solution.py:318
  70.2 2.1 collective-permute-start.5
  72.3 10.6 %collective-permute-start.4 = (f32[64,8,128]{2,1,0:T(8,128)S(1)}, f32[64,8,128]{2,1,0:T(8,128)S(1)}, u32[]{:S(2)}, u32[]{:S(2)}) collective-permute-start(f32[64,8,128]{2,1,0:T(8,128)S(1)} %maximum_select_fusion.x_ref), channel_id=1, source_target_pairs={{1,2},{2,1},{3,4},{4,3},{5,6},{6,5},{7,8},{8,7},{9,10},{10,9},{11,... | collective-permute-start | bytes 786440 | tf_op jit(solution)/shard_map/ppermute | solution.py:318
  82.9 0.0 collective-permute-done.8.p3b
  82.9 0.0 copy-start.1
  82.9 1.9 collective-permute-start.3
  84.8 0.6 pad_add_fusion.pos_ref
  85.5 0.0 collective-permute-done.7.p3a
  85.5 0.0 copy-start.2
  85.5 0.0 collective-permute-done.6.p2b
  85.5 0.0 copy-start.3
  85.5 3.3 %collective-permute-done.5.p2a = f32[64,8,128]{2,1,0:T(8,128)S(1)} collective-permute-done((f32[64,8,128]{2,1,0:T(8,128)S(1)}, f32[64,8,128]{2,1,0:T(8,128)S(1)}, u32[]{:S(2)}, u32[]{:S(2)}) %collective-permute-start.5) | collective-permute-done | bytes 262176 | tf_op jit(solution)/shard_map/ppermute | solution.py:318
  88.8 0.0 copy-start.4
  88.8 3.8 %collective-permute-done.4.p1o = f32[64,8,128]{2,1,0:T(8,128)S(1)} collective-permute-done((f32[64,8,128]{2,1,0:T(8,128)S(1)}, f32[64,8,128]{2,1,0:T(8,128)S(1)}, u32[]{:S(2)}, u32[]{:S(2)}) %collective-permute-start.4) | collective-permute-done | bytes 262176 | tf_op jit(solution)/shard_map/ppermute | solution.py:318
  92.6 0.0 copy-start.5
  92.6 1.7 collective-permute-done.3.p1e
  94.3 0.0 copy-done
  94.4 0.0 copy-done.1
  94.4 0.0 copy-done.2
  94.4 0.0 copy-done.3
  94.4 0.0 copy-done.4
  94.4 0.0 copy-done.5
  94.4 0.0 copy-start.6
  94.4 0.7 copy-done.6
  95.1 13.8 %shard_map.50 = (f32[16,2,128]{2,1,0:T(2,128)}, f32[64,56,128]{2,1,0:T(8,128)}, f32[64,56,128]{2,1,0:T(8,128)}, f32[32,32,128]{2,1,0:T(8,128)}, f32[32,32,128]{2,1,0:T(8,128)}) custom-call(s32[2]{0:T(128)} %pad_add_fusion.pos_ref, f32[64,8,128]{2,1,0:T(8,128)} %copy-done, f32[64,8,128]{2,1,0:T(8,128)} %copy-done.6, f32[64,8,128]{2,1,0:T(8,128)} %copy-done.5, ...), custom_call_target="tpu_custom_call" | custom-call | tf_op jit(solution)/shard_map/pallas_call | solution.py:300
  108.9 20.2 %all_to_all.30 = f32[16,2,128]{2,1,0:T(2,128)S(1)} all-to-all(f32[16,2,128]{2,1,0:T(2,128)} %get-tuple-element.16), channel_id=1, replica_groups=mesh['gx_0'=2,'gx_1'=4,'gx_2'=2,'gy_0'=8,'gy_1'=4] {'gx_0','gy_0'}, dimensions={0} | all-to-all | bytes 32768 | tf_op jit(solution)/shard_map/all_to_all | solution.py:330
  129.1 0.2 broadcast_in_dim.6
  129.4 18.3 %all_to_all.31 = f32[32,16,2,128]{3,2,1,0:T(2,128)} all-to-all(f32[32,16,2,128]{3,2,1,0:T(2,128)S(1)} %broadcast_in_dim.6), channel_id=1, replica_groups=mesh['gx_0'=2,'gx_1'=4,'gx_2'=2,'gy_0'=8,'gy_1'=4] {'gx_1','gx_2','gy_1'}, dimensions={0} | all-to-all | bytes 1048576 | tf_op jit(solution)/shard_map/all_to_all | solution.py:332
  147.7 34.7 %shard_map.51 = (f32[16,2,128]{2,1,0:T(2,128)}, f32[64,56,128]{2,1,0:T(8,128)}, f32[32,32,128]{2,1,0:T(8,128)}, f32[32,32,128]{2,1,0:T(8,128)}, f32[16,128]{1,0:T(8,128)}) custom-call(s32[2]{0:T(128)} %pad_add_fusion.pos_ref, f32[512,2,128]{2,1,0:T(2,128)} %bitcast.9, f32[64,56,128]{2,1,0:T(8,128)} %get-tuple-element.17.d, ...), custom_call_target="tpu_custom_call" | custom-call | tf_op jit(solution)/shard_map/pallas_call | solution.py:300
  182.3 14.7 %all_to_all.32 = f32[16,2,128]{2,1,0:T(2,128)S(1)} all-to-all(f32[16,2,128]{2,1,0:T(2,128)} %get-tuple-element.21), channel_id=1, replica_groups=mesh['gx_0'=2,'gx_1'=4,'gx_2'=2,'gy_0'=8,'gy_1'=4] {'gx_0','gy_0'}, dimensions={0} | all-to-all | bytes 32768 | tf_op jit(solution)/shard_map/all_to_all | solution.py:330
  197.0 0.2 broadcast_in_dim.7
  197.3 16.8 %all_to_all.33 = f32[32,16,2,128]{3,2,1,0:T(2,128)} all-to-all(f32[32,16,2,128]{3,2,1,0:T(2,128)S(1)} %broadcast_in_dim.7), channel_id=1, replica_groups=mesh['gx_0'=2,'gx_1'=4,'gx_2'=2,'gy_0'=8,'gy_1'=4] {'gx_1','gx_2','gy_1'}, dimensions={0} | all-to-all | bytes 1048576 | tf_op jit(solution)/shard_map/all_to_all | solution.py:332
  214.0 19.9 %shard_map.52 = (f32[16,8,128]{2,1,0:T(8,128)}, f32[16,8,128]{2,1,0:T(8,128)}, f32[16,1,128]{2,1,0:T(1,128)}) custom-call(s32[2]{0:T(128)} %pad_add_fusion.pos_ref, f32[512,2,128]{2,1,0:T(2,128)} %bitcast.8, f32[64,56,128]{2,1,0:T(8,128)} %get-tuple-element.17.d, f32[64,56,128]{2,1,0:T(8,128)} %get-tuple-element.22.u0, f32[32,32,128]{2,1,0:T(8,128)} %get-tuple-element.23.b1, ...), custom_call_target="tpu_custom_call" | custom-call | tf_op jit(solution)/shard_map/pallas_call | solution.py:300
  233.9 14.5 %all_to_all.34 = f32[16,1,128]{2,1,0:T(1,128)S(1)} all-to-all(f32[16,1,128]{2,1,0:T(1,128)} %get-tuple-element.28), channel_id=1, replica_groups=mesh['gx_0'=2,'gx_1'=4,'gx_2'=2,'gy_0'=8,'gy_1'=4] {'gx_0','gy_0'}, dimensions={0} | all-to-all | bytes 16384 | tf_op jit(solution)/shard_map/all_to_all | solution.py:379
  248.4 12.4 %all_to_all.35 = f32[32,1,128]{2,1,0:T(1,128)S(1)} all-to-all(f32[32,1,128]{2,1,0:T(1,128)S(1)} %broadcast_in_dim.8), channel_id=1, replica_groups=mesh['gx_0'=2,'gx_1'=4,'gx_2'=2,'gy_0'=8,'gy_1'=4] {'gx_1','gx_2','gy_1'}, dimensions={0} | all-to-all | bytes 32768 | tf_op jit(solution)/shard_map/all_to_all | solution.py:380
  260.9 0.5 add_sqrt_fusion
  (6 shorter events, 0.1 us)
Async XLA Ops:
  23.1 9.8 %collective-permute-start = (f32[16,8,128]{2,1,0:T(8,128)}, f32[16,8,128]{2,1,0:T(8,128)S(1)}, u32[]{:S(2)}, u32[]{:S(2)}) collective-permute-start(f32[16,8,128]{2,1,0:T(8,128)} %bitcast.12), channel_id=1, source_target_pairs={{0,32},{32,0},{64,96},{96,64},{128,160},{160,128},{192,224},{224,1... | collective-permute-start | bytes 196616 | tf_op jit(solution)/shard_map/ppermute | solution.py:318
  33.8 18.0 %collective-permute-start.1 = (f32[24,8,128]{2,1,0:T(8,128)S(1)}, f32[24,8,128]{2,1,0:T(8,128)S(1)}, u32[]{:S(2)}, u32[]{:S(2)}) collective-permute-start(f32[24,8,128]{2,1,0:T(8,128)S(1)} %slice_select_fusion), channel_id=1, source_target_pairs={{32,64},{64,32},{96,128},{128,96},{160,192},{192,160},{224,256},{2... | collective-permute-start | bytes 294920 | tf_op jit(solution)/shard_map/ppermute | solution.py:318
  35.8 16.1 %collective-permute-start.2 = (f32[8,8,128]{2,1,0:T(8,128)S(1)}, f32[8,8,128]{2,1,0:T(8,128)S(1)}, u32[]{:S(2)}, u32[]{:S(2)}) collective-permute-start(f32[8,8,128]{2,1,0:T(8,128)S(1)} %slice_select_fusion.1), channel_id=1, source_target_pairs={{0,96},{96,0},{64,160},{160,64},{128,224},{224,128},{192,288},{288... | collective-permute-start | bytes 98312 | tf_op jit(solution)/shard_map/ppermute | solution.py:318
  51.9 42.5 %copy-start = (f32[64,8,128]{2,1,0:T(8,128)}, f32[64,8,128]{2,1,0:T(8,128)S(1)}, u32[]{:S(2)}) copy-start(f32[64,8,128]{2,1,0:T(8,128)S(1)} %maximum_select_fusion.x_ref) | copy-start | bytes 786436
  51.9 31.0 %collective-permute-start.8 = (f32[64,8,128]{2,1,0:T(8,128)S(1)}, f32[64,8,128]{2,1,0:T(8,128)S(1)}, u32[]{:S(2)}, u32[]{:S(2)}) collective-permute-start(f32[64,8,128]{2,1,0:T(8,128)S(1)} %maximum_select_fusion.x_ref), channel_id=1, source_target_pairs={{1,4},{4,1},{3,6},{6,3},{5,8},{8,5},{7,10},{10,7},{9,12},{12,9},{1... | collective-permute-start | bytes 786440 | tf_op jit(solution)/shard_map/ppermute | solution.py:318
  64.1 21.4 %collective-permute-start.7 = (f32[64,8,128]{2,1,0:T(8,128)S(1)}, f32[64,8,128]{2,1,0:T(8,128)S(1)}, u32[]{:S(2)}, u32[]{:S(2)}) collective-permute-start(f32[64,8,128]{2,1,0:T(8,128)S(1)} %maximum_select_fusion.x_ref), channel_id=1, source_target_pairs={{0,3},{3,0},{2,5},{5,2},{4,7},{7,4},{6,9},{9,6},{8,11},{11,8},{10,... | collective-permute-start | bytes 786440 | tf_op jit(solution)/shard_map/ppermute | solution.py:318
  66.0 19.5 %collective-permute-start.6 = (f32[64,8,128]{2,1,0:T(8,128)S(1)}, f32[64,8,128]{2,1,0:T(8,128)S(1)}, u32[]{:S(2)}, u32[]{:S(2)}) collective-permute-start(f32[64,8,128]{2,1,0:T(8,128)S(1)} %maximum_select_fusion.x_ref), channel_id=1, source_target_pairs={{2,4},{4,2},{3,5},{5,3},{6,8},{8,6},{7,9},{9,7},{10,12},{12,10},{1... | collective-permute-start | bytes 786440 | tf_op jit(solution)/shard_map/ppermute | solution.py:318
  70.2 18.6 %collective-permute-start.5 = (f32[64,8,128]{2,1,0:T(8,128)S(1)}, f32[64,8,128]{2,1,0:T(8,128)S(1)}, u32[]{:S(2)}, u32[]{:S(2)}) collective-permute-start(f32[64,8,128]{2,1,0:T(8,128)S(1)} %maximum_select_fusion.x_ref), channel_id=1, source_target_pairs={{0,2},{2,0},{1,3},{3,1},{4,6},{6,4},{5,7},{7,5},{8,10},{10,8},{9,1... | collective-permute-start | bytes 786440 | tf_op jit(solution)/shard_map/ppermute | solution.py:318
  72.3 20.3 %collective-permute-start.4 = (f32[64,8,128]{2,1,0:T(8,128)S(1)}, f32[64,8,128]{2,1,0:T(8,128)S(1)}, u32[]{:S(2)}, u32[]{:S(2)}) collective-permute-start(f32[64,8,128]{2,1,0:T(8,128)S(1)} %maximum_select_fusion.x_ref), channel_id=1, source_target_pairs={{1,2},{2,1},{3,4},{4,3},{5,6},{6,5},{7,8},{8,7},{9,10},{10,9},{11,... | collective-permute-start | bytes 786440 | tf_op jit(solution)/shard_map/ppermute | solution.py:318
  82.9 11.5 %copy-start.1 = (f32[64,8,128]{2,1,0:T(8,128)}, f32[64,8,128]{2,1,0:T(8,128)S(1)}, u32[]{:S(2)}) copy-start(f32[64,8,128]{2,1,0:T(8,128)S(1)} %collective-permute-done.8.p3b) | copy-start | bytes 786436
  82.9 11.5 %collective-permute-start.3 = (f32[64,8,128]{2,1,0:T(8,128)S(1)}, f32[64,8,128]{2,1,0:T(8,128)S(1)}, u32[]{:S(2)}, u32[]{:S(2)}) collective-permute-start(f32[64,8,128]{2,1,0:T(8,128)S(1)} %maximum_select_fusion.x_ref), channel_id=1, source_target_pairs={{0,1},{1,0},{2,3},{3,2},{4,5},{5,4},{6,7},{7,6},{8,9},{9,8},{10,11... | collective-permute-start | bytes 786440 | tf_op jit(solution)/shard_map/ppermute | solution.py:318
  85.5 8.9 %copy-start.2 = (f32[64,8,128]{2,1,0:T(8,128)}, f32[64,8,128]{2,1,0:T(8,128)S(1)}, u32[]{:S(2)}) copy-start(f32[64,8,128]{2,1,0:T(8,128)S(1)} %collective-permute-done.7.p3a) | copy-start | bytes 786436
  85.5 8.9 %copy-start.3 = (f32[64,8,128]{2,1,0:T(8,128)}, f32[64,8,128]{2,1,0:T(8,128)S(1)}, u32[]{:S(2)}) copy-start(f32[64,8,128]{2,1,0:T(8,128)S(1)} %collective-permute-done.6.p2b) | copy-start | bytes 786436
  88.8 5.5 %copy-start.4 = (f32[64,8,128]{2,1,0:T(8,128)}, f32[64,8,128]{2,1,0:T(8,128)S(1)}, u32[]{:S(2)}) copy-start(f32[64,8,128]{2,1,0:T(8,128)S(1)} %collective-permute-done.5.p2a) | copy-start | bytes 786436
  92.6 1.8 copy-start.5
  94.4 0.7 copy-start.6

commit v2 on v1

--- a/solution.py
+++ b/solution.py
@@ -27,21 +27,24 @@
 W1X, W1Y = 32, 32
 W2X, W2Y = 36, 40
 W3X, W3Y = 18, 24
+DEPOSIT_ROWS = 32
+KEEP = True
 VMEM = pltpu.VMEM
 
 
 def deposit_kernel(cell_ref, mass_ref, out_ref):
     rows = lax.broadcasted_iota(jnp.int32, (128, 128), 0)
+    batch = DEPOSIT_ROWS
 
     def step(t, acc):
-        cells = cell_ref[pl.ds(pl.multiple_of(t * 8, 8), 8), :]
-        masses = mass_ref[pl.ds(pl.multiple_of(t * 8, 8), 8), :]
+        cells = cell_ref[pl.ds(pl.multiple_of(t * batch, 8), batch), :]
+        masses = mass_ref[pl.ds(pl.multiple_of(t * batch, 8), batch), :]
         high = cells >> 7
         low = cells & 127
         coarse = masses.astype(jnp.bfloat16).astype(jnp.float32)
         fine = masses - coarse
         left, right = [], []
-        for r in range(8):
+        for r in range(batch):
             hit = rows == high[r : r + 1, :]
             first = jnp.where(hit, coarse[r : r + 1, :], 0.0).astype(jnp.bfloat16)
             second = jnp.where(hit, fine[r : r + 1, :], 0.0).astype(jnp.bfloat16)
@@ -51,7 +54,7 @@
         right = jnp.concatenate(right, axis=1)
         return acc + lax.dot_general(left, right, (((1,), (1,)), ((), ())), preferred_element_type=jnp.float32)
 
-    total = lax.fori_loop(0, cell_ref.shape[0] // 8, step, jnp.zeros((256, 128), jnp.float32))
+    total = lax.fori_loop(0, cell_ref.shape[0] // batch, step, jnp.zeros((256, 128), jnp.float32))
     out_ref[...] = total[:128] + total[128:]
 
 
@@ -61,9 +64,10 @@
     return (j + z + extra) & 1
 
 
-def around(ref, i, rows, lanes):
-    c = ref[i]
-    n = ref[i - 1] + ref[i + 1]
+def around(ref, i, rows, lanes, top=0):
+    part = slice(top, top + rows)
+    c = ref[i, part, :]
+    n = ref[i - 1, part, :] + ref[i + 1, part, :]
     n = n + (pltpu.roll(c, 1, 0) + pltpu.roll(c, rows - 1, 0))
     return c, n + (pltpu.roll(c, lanes, 1) + pltpu.roll(c, NZ - lanes, 1))
 
@@ -90,25 +94,25 @@
     loop(lo, hi, body)
 
 
-def half_sweep(u, get_b, parity, colour, rows, lanes, s, lo, hi):
+def half_sweep(u, get_b, parity, colour, rows, lanes, s, lo, hi, top=0):
     def body(i):
-        c, n = around(u, i, rows, lanes)
+        c, n = around(u, i, rows, lanes, top)
         chosen = parity == ((i + colour) & 1)
-        u[i] = jnp.where(chosen, (n + s * get_b(i)) * (1.0 / 6.0), c)
+        u[i, top : top + rows, :] = jnp.where(chosen, (n + s * get_b(i)) * (1.0 / 6.0), c)
 
     loop(lo, hi, body)
 
 
-def residual_at(u, b, i, rows, lanes, s):
-    c, n = around(u, i, rows, lanes)
+def residual_at(u, b, i, rows, lanes, s, top=0):
+    c, n = around(u, i, rows, lanes, top)
     return b - (6.0 * c - n) * (1.0 / s)
 
 
-def restrict_to(out, u, get_b, rows, lanes, s, lo, hi, scr, out_rows):
+def restrict_to(out, u, get_b, rows, lanes, s, lo, hi, scr, out_rows, top=0):
     def body(p):
-        t = residual_at(u, get_b(2 * p), 2 * p, rows, lanes, s)
-        t = t + residual_at(u, get_b(2 * p + 1), 2 * p + 1, rows, lanes, s)
-        scr[0:rows, :] = pair_z(t, lanes)
+        t = residual_at(u, get_b(2 * p), 2 * p, rows, lanes, s, top)
+        t = t + residual_at(u, get_b(2 * p + 1), 2 * p + 1, rows, lanes, s, top)
+        scr[top : top + rows, :] = pair_z(t, lanes)
         out[p] = (scr[pl.ds(0, out_rows, 2), :] + scr[pl.ds(1, out_rows, 2), :]) * 0.125
 
     loop(lo, hi, body, 1)
@@ -179,28 +183,34 @@
     half_sweep(u2, lambda i: b2[i], par2, 1, W2Y, 4, 16.0, 10, 26)
 
 
-def up_level1(v1, u1, b1, shift, u2, scr):
+def up_level1(v1, u1, b1, shift, u2, scr, lo, hi, top, rows):
+    part = slice(top, top + rows)
+    first = 10 + top // 2
+
     def add(p):
-        c = spread_rows(u2[p + 10, 10:26, :], 16, scr)
-        v1[2 * p] = u1[2 * p] - shift * (4.0 / 3.0) + c
-        v1[2 * p + 1] = u1[2 * p + 1] - shift * (4.0 / 3.0) + c
-
-    loop(0, 16, add, 1)
-    par1 = row_parity(W1Y, 2)
+        c = spread_rows(u2[p + 10, first : first + rows // 2, :], rows // 2, scr)
+        v1[2 * p, part, :] = u1[2 * p, part, :] - shift * (4.0 / 3.0) + c
+        v1[2 * p + 1, part, :] = u1[2 * p + 1, part, :] - shift * (4.0 / 3.0) + c
+
+    loop(lo // 2, hi // 2, add, 1)
+    par1 = row_parity(rows, 2)
     for colour in (0, 1):
-        half_sweep(v1, lambda i: b1[i] - shift, par1, colour, W1Y, 2, 4.0, 1, W1X - 1)
-
-
-def up_level0(v0, u0, d, shift, base, v1, scr, lo, hi):
+        half_sweep(v1, lambda i: b1[i, part, :] - shift, par1, colour, rows, 2, 4.0, lo + 1, hi - 1, top)
+
+
+def up_level0(v0, u0, d, shift, base, v1, scr, lo, hi, top, rows):
+    part = slice(top, top + rows)
+    half = (rows // 2 + 7) // 8 * 8
+
     def add(p):
-        c = spread_rows(v1[p], W1Y, scr)[0:W0Y]
-        v0[2 * p] = u0[2 * p] - base + c
-        v0[2 * p + 1] = u0[2 * p + 1] - base + c
+        c = spread_rows(v1[p, top // 2 : top // 2 + half, :], half, scr)[0:rows]
+        v0[2 * p, part, :] = u0[2 * p, part, :] - base + c
+        v0[2 * p + 1, part, :] = u0[2 * p + 1, part, :] - base + c
 
     loop(lo // 2, hi // 2, add, 1)
-    par0 = row_parity(W0Y, 1)
+    par0 = row_parity(rows, 1)
     for colour in (0, 1):
-        half_sweep(v0, lambda i: d[i] - shift, par0, colour, W0Y, 1, 1.0, lo + 1, hi - 1)
+        half_sweep(v0, lambda i: d[i, part, :] - shift, par0, colour, rows, 1, 1.0, lo + 1, hi - 1, top)
 
 
 def down_level1(u1, b1, send_ref):
@@ -233,42 +243,43 @@
     down_level1(u1, b1, send_ref)
 
 
-def own_squares(u, d, shift):
-    total = jnp.zeros((CY, NZ), jnp.float32)
-    for i in range(24, 40):
-        r = residual_at(u, d[i] - shift, i, W0Y, 1, 1.0)[24:32]
-        total = total + r * r
-    return total
+def own_residual(u, d, shift, x):
+    i = 24 + x
+    return residual_at(u, d[i, 16:40, :] - shift, i, 24, 1, 1.0, 16)[8:16]
 
 
 def mid_kernel(pos_ref, ag, d, u0, b1, u1, send_ref, u0n, b1n, u1n, stat_ref, v1, pw, b2, u2, b3, u3, scr):
     total = jnp.sum(jnp.sum(ag[...], axis=0))
     mean = total * (1.0 / COARSE_CELLS)
     coarse_solve(pos_ref, ag, mean, pw, b2, u2, b3, u3, scr)
-    up_level1(v1, u1, b1, mean, u2, scr)
-    up_level0(u0n, u0, d, mean, mean * (1.0 / 3.0), v1, scr, 0, W0X)
-    stat_ref[0:8, :] = own_squares(u0n, d, mean)
+    up_level1(v1, u1, b1, mean, u2, scr, 0, W1X, 0, W1Y)
+    up_level0(u0n, u0, d, mean, mean * (1.0 / 3.0), v1, scr, 8, 56, 8, 40)
+    squares = jnp.zeros((CY, NZ), jnp.float32)
+    for x in range(CX):
+        r = own_residual(u0n, d, mean, x)
+        squares = squares + r * r
+    stat_ref[0:8, :] = squares
     stat_ref[8:16, :] = jnp.full((8, NZ), mean, jnp.float32)
-    par0 = row_parity(W0Y, 1)
+    par0 = row_parity(40, 1)
     for colour in (0, 1):
-        half_sweep(u0n, lambda i: d[i] - mean, par0, colour, W0Y, 1, 1.0, 8, 56)
+        half_sweep(u0n, lambda i: d[i, 8:48, :] - mean, par0, colour, 40, 1, 1.0, 10, 54, 8)
     scr[...] = jnp.zeros(scr.shape, jnp.float32)
     for i in range(W1X):
         if i < 6 or i >= 26:
             b1n[i] = jnp.zeros((W1Y, NZ), jnp.float32)
-    restrict_to(b1n, u0n, lambda i: d[i] - mean, W0Y, 1, 1.0, 6, 26, scr, W1Y)
+    restrict_to(b1n, u0n, lambda i: d[i, 8:48, :] - mean, 40, 1, 1.0, 6, 26, scr, W1Y, 8)
     down_level1(u1n, b1n, send_ref)
 
 
 def post_kernel(pos_ref, ag, d, u0, b1, u1, stat, pot_ref, res_ref, sums_ref, v0, v1, pw, b2, u2, b3, u3, scr):
     mean = jnp.max(stat[8:16, :])
     coarse_solve(pos_ref, ag, 0.0, pw, b2, u2, b3, u3, scr)
-    up_level1(v1, u1, b1, 0.0, u2, scr)
-    up_level0(v0, u0, d, mean, 0.0, v1, scr, 16, 48)
+    up_level1(v1, u1, b1, 0.0, u2, scr, 8, 24, 8, 16)
+    up_level0(v0, u0, d, mean, 0.0, v1, scr, 20, 44, 16, 24)
     inv = 1.0 / jnp.full((CY, NZ), mean, jnp.float32)
     total = jnp.zeros((CY, NZ), jnp.float32)
-    for i in range(16):
-        r = residual_at(v0, d[24 + i] - mean, 24 + i, W0Y, 1, 1.0)[24:32] * inv
+    for i in range(CX):
+        r = own_residual(v0, d, mean, i) * inv
         total = total + r * r
         res_ref[i] = -r
         pot_ref[i] = v0[24 + i, 24:32, :] * (-coupling * inv)
@@ -283,17 +294,26 @@
     return jax.ShapeDtypeStruct(shape, jnp.float32)
 
 
+def kept(*shape):
+    return pltpu.VMEM(shape, jnp.float32) if KEEP else f32(*shape)
+
+
+def resident(x):
+    return pltpu.with_memory_space_constraint(x, pltpu.VMEM) if KEEP else x
+
+
 def vmem(*shape):
     return pltpu.VMEM(shape, jnp.float32)
 
 
 COARSE_SCRATCH = (vmem(9, W2Y, NZ), vmem(W2X, W2Y, NZ), vmem(W2X, W2Y, NZ), vmem(W3X, W3Y, NZ), vmem(W3X, W3Y, NZ), vmem(64, NZ))
-LEVELS_OUT = (f32(W0X, W0Y, NZ), f32(W1X, W1Y, NZ), f32(W1X, W1Y, NZ))
+LEVELS_OUT = (kept(W0X, W0Y, NZ), kept(W1X, W1Y, NZ), kept(W1X, W1Y, NZ))
 
 
 def call(kernel, outs, scratch, *args, pos=None):
     whole = pl.BlockSpec(memory_space=VMEM)
     specs = [whole] * len(args)
+    args = tuple(resident(a) for a in args)
     if pos is not None:
         specs = [pl.BlockSpec(memory_space=pltpu.SMEM)] + specs
         args = (pos, *args)
@@ -303,6 +323,7 @@
         in_specs=specs,
         out_specs=jax.tree.map(lambda _: whole, outs),
         scratch_shapes=list(scratch),
+        compiler_params=pltpu.CompilerParams(vmem_limit_bytes=24 * 1024 * 1024),
     )(*args)
 
 
@@ -347,7 +368,7 @@
     pos = jnp.stack([tile_x, tile_y]).astype(jnp.int32)
     cells = particle_cell.reshape(512, 128)
     masses = particle_mass.reshape(512, 128)
-    density = call(deposit_kernel, f32(128, 128), (), cells, masses).reshape(CX, CY, NZ)
+    density = call(deposit_kernel, kept(128, 128), (), cells, masses).reshape(CX, CY, NZ)
     wide = x_window(density)
     strips = (
         swap(wide, GY, 1, even),
@@ -358,12 +379,12 @@
         swap(wide, GY, 3, odd),
     )
     send, d, u0, b1, u1 = call(
-        pre_kernel, (f32(16, 2, NZ), f32(W0X, W0Y, NZ), *LEVELS_OUT), (vmem(64, NZ),), wide, *strips, pos=pos
+        pre_kernel, (kept(16, 2, NZ), kept(W0X, W0Y, NZ), *LEVELS_OUT), (vmem(64, NZ),), wide, *strips, pos=pos
     )
     got = gather_all(send).reshape(512, 2, NZ)
     send, u0, b1, u1, stat = call(
         mid_kernel,
-        (f32(16, 2, NZ), *LEVELS_OUT, f32(16, NZ)),
+        (kept(16, 2, NZ), *LEVELS_OUT, kept(16, NZ)),
         (vmem(W1X, W1Y, NZ), *COARSE_SCRATCH),
         got, d, u0, b1, u1,
         pos=pos,
@@ -371,7 +392,7 @@
     got = gather_all(send).reshape(512, 2, NZ)
     potential, residual, sums = call(
         post_kernel,
-        (f32(CX, CY, NZ), f32(CX, CY, NZ), f32(16, 1, NZ)),
+        (f32(CX, CY, NZ), f32(CX, CY, NZ), kept(16, 1, NZ)),
         (vmem(W0X, W0Y, NZ), vmem(W1X, W1Y, NZ), *COARSE_SCRATCH),
         got, d, u0, b1, u1, stat,
         pos=pos,

time: 262 us -> 238 us (0.908)
  Pallas kernels: 90.8 us -> 68.5 us
    pallas_call x4, Pallas kernels: 90.8 us -> 68.5 us  [call(): pl.pallas_call(kernel, out_shape=outs, in_specs=specs, out_specs=jax.tree...]
where the time goes in v2:
time: 238 us; the launch traced here: 237 us
  blocking collectives  94.9 us (40%)
  Pallas kernels  68.5 us (29%)
  starting transfers between devices  56.6 us (24%)
  waiting for transfers between devices  13.2 us (6%)
    pallas_call x4, Pallas kernels, call(): pl.pallas_call(kernel, out_shape=outs, in_specs=specs, out_specs=jax.tree...  68.5 us
    ppermute x9, starting transfers between devices, swap(): return lax.ppermute(x, axis, pairs(lax.axis_size(axis), step, chosen))  56.6 us
    all_to_all x2, blocking collectives, gather_all(): return lax.all_to_all(copies, PLANE, 0, 0)  35.4 us
    all_to_all x2, blocking collectives, gather_all(): ring = lax.all_to_all(block, Z_RING, 0, 0)  33.5 us
    all_to_all x1, blocking collectives, per_device(): ring = jnp.sum(lax.all_to_all(sums, Z_RING, 0, 0), axis=0)  13.9 us
    ppermute x9, waiting for transfers between devices, swap(): return lax.ppermute(x, axis, pairs(lax.axis_size(axis), step, chosen))  13.2 us
    all_to_all x1, blocking collectives, per_device(): lax.all_to_all(jnp.broadcast_to(ring[None], (32, 1, NZ)), PLANE, 0, 0)  12.2 us
  transfers between devices with their start and end apart: 9, of which 5 were waited for; matrix products, arithmetic and copies ran while one was open for 0% of the time, Pallas kernels for 0%

profile of v2, /device:TPU:1, one launch (start us, length us, event | category | flops | bytes accessed | tf_op | source)
XLA Modules:
  0.0 237.0 jit_solution(2718098470857018996)
XLA Ops:
  0.6 0.0 copy-start
  0.6 0.9 copy-done
  1.6 0.0 copy-start.1
  1.6 0.9 copy-done.1
  2.5 13.9 %shard_map.49 = f32[128,128]{1,0:T(8,128)S(1)} custom-call(s32[512,128]{1,0:T(8,128)S(1)} %bitcast.10, f32[512,128]{1,0:T(8,128)S(1)} %bitcast.11), custom_call_target="tpu_custom_call" | custom-call | tf_op jit(solution)/shard_map/pallas_call | solution.py:320
  16.4 8.7 %collective-permute-start = (f32[16,8,128]{2,1,0:T(8,128)S(1)}, f32[16,8,128]{2,1,0:T(8,128)S(1)}, u32[]{:S(2)}, u32[]{:S(2)}) collective-permute-start(f32[16,8,128]{2,1,0:T(8,128)S(1)} %bitcast.12), channel_id=1, source_target_pairs={{0,32},{32,0},{64,96},{96,64},{128,160},{160,128},{192,224},{224,1... | collective-permute-start | bytes 196616 | tf_op jit(solution)/shard_map/ppermute | solution.py:339
  25.2 0.9 collective-permute-done
  26.1 1.9 collective-permute-start.1
  28.0 13.2 %collective-permute-start.2 = (f32[8,8,128]{2,1,0:T(8,128)S(1)}, f32[8,8,128]{2,1,0:T(8,128)S(1)}, u32[]{:S(2)}, u32[]{:S(2)}) collective-permute-start(f32[8,8,128]{2,1,0:T(8,128)S(1)} %slice_select_fusion.1), channel_id=1, source_target_pairs={{0,96},{96,0},{64,160},{160,64},{128,224},{224,128},{192,288},{288... | collective-permute-start | bytes 98312 | tf_op jit(solution)/shard_map/ppermute | solution.py:339
  41.2 2.9 %collective-permute-done.2 = f32[8,8,128]{2,1,0:T(8,128)S(1)} collective-permute-done((f32[8,8,128]{2,1,0:T(8,128)S(1)}, f32[8,8,128]{2,1,0:T(8,128)S(1)}, u32[]{:S(2)}, u32[]{:S(2)}) %collective-permute-start.2) | collective-permute-done | bytes 32800 | tf_op jit(solution)/shard_map/ppermute | solution.py:339
  44.1 0.0 collective-permute-done.1
  44.1 12.1 %collective-permute-start.8 = (f32[64,8,128]{2,1,0:T(8,128)S(1)}, f32[64,8,128]{2,1,0:T(8,128)S(1)}, u32[]{:S(2)}, u32[]{:S(2)}) collective-permute-start(f32[64,8,128]{2,1,0:T(8,128)S(1)} %maximum_select_fusion.x_ref), channel_id=1, source_target_pairs={{1,4},{4,1},{3,6},{6,3},{5,8},{8,5},{7,10},{10,7},{9,12},{12,9},{1... | collective-permute-start | bytes 786440 | tf_op jit(solution)/shard_map/ppermute | solution.py:339
  56.2 1.9 collective-permute-start.7
  58.1 4.3 %collective-permute-start.6 = (f32[64,8,128]{2,1,0:T(8,128)S(1)}, f32[64,8,128]{2,1,0:T(8,128)S(1)}, u32[]{:S(2)}, u32[]{:S(2)}) collective-permute-start(f32[64,8,128]{2,1,0:T(8,128)S(1)} %maximum_select_fusion.x_ref), channel_id=1, source_target_pairs={{2,4},{4,2},{3,5},{5,3},{6,8},{8,6},{7,9},{9,7},{10,12},{12,10},{1... | collective-permute-start | bytes 786440 | tf_op jit(solution)/shard_map/ppermute | solution.py:339
  62.4 2.1 collective-permute-start.5
  64.5 10.4 %collective-permute-start.4 = (f32[64,8,128]{2,1,0:T(8,128)S(1)}, f32[64,8,128]{2,1,0:T(8,128)S(1)}, u32[]{:S(2)}, u32[]{:S(2)}) collective-permute-start(f32[64,8,128]{2,1,0:T(8,128)S(1)} %maximum_select_fusion.x_ref), channel_id=1, source_target_pairs={{1,2},{2,1},{3,4},{4,3},{5,6},{6,5},{7,8},{8,7},{9,10},{10,9},{11,... | collective-permute-start | bytes 786440 | tf_op jit(solution)/shard_map/ppermute | solution.py:339
  75.0 0.0 collective-permute-done.8.p3b
  75.0 1.9 collective-permute-start.3
  76.9 0.1 pad_add_fusion.pos_ref
  77.0 0.0 collective-permute-done.7.p3a
  77.0 0.0 collective-permute-done.6.p2b
  77.0 4.5 %collective-permute-done.5.p2a = f32[64,8,128]{2,1,0:T(8,128)S(1)} collective-permute-done((f32[64,8,128]{2,1,0:T(8,128)S(1)}, f32[64,8,128]{2,1,0:T(8,128)S(1)}, u32[]{:S(2)}, u32[]{:S(2)}) %collective-permute-start.5) | collective-permute-done | bytes 262176 | tf_op jit(solution)/shard_map/ppermute | solution.py:339
  81.5 3.5 %collective-permute-done.4.p1o = f32[64,8,128]{2,1,0:T(8,128)S(1)} collective-permute-done((f32[64,8,128]{2,1,0:T(8,128)S(1)}, f32[64,8,128]{2,1,0:T(8,128)S(1)}, u32[]{:S(2)}, u32[]{:S(2)}) %collective-permute-start.4) | collective-permute-done | bytes 262176 | tf_op jit(solution)/shard_map/ppermute | solution.py:339
  85.0 1.4 collective-permute-done.3.p1e
  86.4 11.0 %shard_map.50 = (f32[16,2,128]{2,1,0:T(2,128)S(1)}, f32[64,56,128]{2,1,0:T(8,128)S(1)}, f32[64,56,128]{2,1,0:T(8,128)S(1)}, f32[32,32,128]{2,1,0:T(8,128)S(1)}, f32[32,32,128]{2,1,0:T(8,128)S(1)}) custom-call(s32[2]{0:T(128)S(1)} %pad_add_fusion.pos_ref, f32[64,8,128]{2,1,0:T(8,128)S(1)} %maximum_select_fusion.x_ref, ...), custom_call_target="tpu_custom_call" | custom-call | tf_op jit(solution)/shard_map/pallas_call | solution.py:320
  97.5 19.7 %all_to_all.30 = f32[16,2,128]{2,1,0:T(2,128)S(1)} all-to-all(f32[16,2,128]{2,1,0:T(2,128)S(1)} %get-tuple-element.16), channel_id=1, replica_groups=mesh['gx_0'=2,'gx_1'=4,'gx_2'=2,'gy_0'=8,'gy_1'=4] {'gx_0','gy_0'}, dimensions={0} | all-to-all | bytes 32768 | tf_op jit(solution)/shard_map/all_to_all | solution.py:351
  117.1 0.2 broadcast_in_dim.6
  117.3 18.7 %all_to_all.31 = f32[32,16,2,128]{3,2,1,0:T(2,128)S(1)} all-to-all(f32[32,16,2,128]{3,2,1,0:T(2,128)S(1)} %broadcast_in_dim.6), channel_id=1, replica_groups=mesh['gx_0'=2,'gx_1'=4,'gx_2'=2,'gy_0'=8,'gy_1'=4] {'gx_1','gx_2','gy_1'}, dimensions={0} | all-to-all | bytes 1048576 | tf_op jit(solution)/shard_map/all_to_all | solution.py:353
  136.1 28.5 %shard_map.51 = (f32[16,2,128]{2,1,0:T(2,128)S(1)}, f32[64,56,128]{2,1,0:T(8,128)S(1)}, f32[32,32,128]{2,1,0:T(8,128)S(1)}, f32[32,32,128]{2,1,0:T(8,128)S(1)}, f32[16,128]{1,0:T(8,128)S(1)}) custom-call(s32[2]{0:T(128)S(1)} %pad_add_fusion.pos_ref, f32[512,2,128]{2,1,0:T(2,128)S(1)} %bitcast.9, f32[64,56,128]{2,1,0:T(8,128)S(1)} %get-tuple-element.17.d, ...), custom_call_target="tpu_custom_call" | custom-call | tf_op jit(solution)/shard_map/pallas_call | solution.py:320
  164.6 13.8 %all_to_all.32 = f32[16,2,128]{2,1,0:T(2,128)S(1)} all-to-all(f32[16,2,128]{2,1,0:T(2,128)S(1)} %get-tuple-element.21), channel_id=1, replica_groups=mesh['gx_0'=2,'gx_1'=4,'gx_2'=2,'gy_0'=8,'gy_1'=4] {'gx_0','gy_0'}, dimensions={0} | all-to-all | bytes 32768 | tf_op jit(solution)/shard_map/all_to_all | solution.py:351
  178.4 0.2 broadcast_in_dim.7
  178.7 16.7 %all_to_all.33 = f32[32,16,2,128]{3,2,1,0:T(2,128)S(1)} all-to-all(f32[32,16,2,128]{3,2,1,0:T(2,128)S(1)} %broadcast_in_dim.7), channel_id=1, replica_groups=mesh['gx_0'=2,'gx_1'=4,'gx_2'=2,'gy_0'=8,'gy_1'=4] {'gx_1','gx_2','gy_1'}, dimensions={0} | all-to-all | bytes 1048576 | tf_op jit(solution)/shard_map/all_to_all | solution.py:353
  195.4 15.0 %shard_map.52 = (f32[16,8,128]{2,1,0:T(8,128)}, f32[16,8,128]{2,1,0:T(8,128)}, f32[16,1,128]{2,1,0:T(1,128)S(1)}) custom-call(s32[2]{0:T(128)S(1)} %pad_add_fusion.pos_ref, f32[512,2,128]{2,1,0:T(2,128)S(1)} %bitcast.8, f32[64,56,128]{2,1,0:T(8,128)S(1)} %get-tuple-element.17.d, f32[64,56,128]{2,1,0:T(8,128)S(1)} %get-tuple-element.22.u0, ...), custom_call_target="tpu_custom_call" | custom-call | tf_op jit(solution)/shard_map/pallas_call | solution.py:320
  210.4 13.9 %all_to_all.34 = f32[16,1,128]{2,1,0:T(1,128)S(1)} all-to-all(f32[16,1,128]{2,1,0:T(1,128)S(1)} %get-tuple-element.28), channel_id=1, replica_groups=mesh['gx_0'=2,'gx_1'=4,'gx_2'=2,'gy_0'=8,'gy_1'=4] {'gx_0','gy_0'}, dimensions={0} | all-to-all | bytes 16384 | tf_op jit(solution)/shard_map/all_to_all | solution.py:400
  224.3 12.2 %all_to_all.35 = f32[32,1,128]{2,1,0:T(1,128)S(1)} all-to-all(f32[32,1,128]{2,1,0:T(1,128)S(1)} %broadcast_in_dim.8), channel_id=1, replica_groups=mesh['gx_0'=2,'gx_1'=4,'gx_2'=2,'gy_0'=8,'gy_1'=4] {'gx_1','gx_2','gy_1'}, dimensions={0} | all-to-all | bytes 32768 | tf_op jit(solution)/shard_map/all_to_all | solution.py:401
  236.5 0.5 add_sqrt_fusion
  (7 shorter events, 0.1 us)
Async XLA Ops:
  0.6 1.0 copy-start
  1.6 0.9 copy-start.1
  16.4 9.6 %collective-permute-start = (f32[16,8,128]{2,1,0:T(8,128)S(1)}, f32[16,8,128]{2,1,0:T(8,128)S(1)}, u32[]{:S(2)}, u32[]{:S(2)}) collective-permute-start(f32[16,8,128]{2,1,0:T(8,128)S(1)} %bitcast.12), channel_id=1, source_target_pairs={{0,32},{32,0},{64,96},{96,64},{128,160},{160,128},{192,224},{224,1... | collective-permute-start | bytes 196616 | tf_op jit(solution)/shard_map/ppermute | solution.py:339
  26.1 18.0 %collective-permute-start.1 = (f32[24,8,128]{2,1,0:T(8,128)S(1)}, f32[24,8,128]{2,1,0:T(8,128)S(1)}, u32[]{:S(2)}, u32[]{:S(2)}) collective-permute-start(f32[24,8,128]{2,1,0:T(8,128)S(1)} %slice_select_fusion), channel_id=1, source_target_pairs={{32,64},{64,32},{96,128},{128,96},{160,192},{192,160},{224,256},{2... | collective-permute-start | bytes 294920 | tf_op jit(solution)/shard_map/ppermute | solution.py:339
  28.0 16.1 %collective-permute-start.2 = (f32[8,8,128]{2,1,0:T(8,128)S(1)}, f32[8,8,128]{2,1,0:T(8,128)S(1)}, u32[]{:S(2)}, u32[]{:S(2)}) collective-permute-start(f32[8,8,128]{2,1,0:T(8,128)S(1)} %slice_select_fusion.1), channel_id=1, source_target_pairs={{0,96},{96,0},{64,160},{160,64},{128,224},{224,128},{192,288},{288... | collective-permute-start | bytes 98312 | tf_op jit(solution)/shard_map/ppermute | solution.py:339
  44.1 30.9 %collective-permute-start.8 = (f32[64,8,128]{2,1,0:T(8,128)S(1)}, f32[64,8,128]{2,1,0:T(8,128)S(1)}, u32[]{:S(2)}, u32[]{:S(2)}) collective-permute-start(f32[64,8,128]{2,1,0:T(8,128)S(1)} %maximum_select_fusion.x_ref), channel_id=1, source_target_pairs={{1,4},{4,1},{3,6},{6,3},{5,8},{8,5},{7,10},{10,7},{9,12},{12,9},{1... | collective-permute-start | bytes 786440 | tf_op jit(solution)/shard_map/ppermute | solution.py:339
  56.2 20.8 %collective-permute-start.7 = (f32[64,8,128]{2,1,0:T(8,128)S(1)}, f32[64,8,128]{2,1,0:T(8,128)S(1)}, u32[]{:S(2)}, u32[]{:S(2)}) collective-permute-start(f32[64,8,128]{2,1,0:T(8,128)S(1)} %maximum_select_fusion.x_ref), channel_id=1, source_target_pairs={{0,3},{3,0},{2,5},{5,2},{4,7},{7,4},{6,9},{9,6},{8,11},{11,8},{10,... | collective-permute-start | bytes 786440 | tf_op jit(solution)/shard_map/ppermute | solution.py:339
  58.1 18.9 %collective-permute-start.6 = (f32[64,8,128]{2,1,0:T(8,128)S(1)}, f32[64,8,128]{2,1,0:T(8,128)S(1)}, u32[]{:S(2)}, u32[]{:S(2)}) collective-permute-start(f32[64,8,128]{2,1,0:T(8,128)S(1)} %maximum_select_fusion.x_ref), channel_id=1, source_target_pairs={{2,4},{4,2},{3,5},{5,3},{6,8},{8,6},{7,9},{9,7},{10,12},{12,10},{1... | collective-permute-start | bytes 786440 | tf_op jit(solution)/shard_map/ppermute | solution.py:339
  62.4 19.1 %collective-permute-start.5 = (f32[64,8,128]{2,1,0:T(8,128)S(1)}, f32[64,8,128]{2,1,0:T(8,128)S(1)}, u32[]{:S(2)}, u32[]{:S(2)}) collective-permute-start(f32[64,8,128]{2,1,0:T(8,128)S(1)} %maximum_select_fusion.x_ref), channel_id=1, source_target_pairs={{0,2},{2,0},{1,3},{3,1},{4,6},{6,4},{5,7},{7,5},{8,10},{10,8},{9,1... | collective-permute-start | bytes 786440 | tf_op jit(solution)/shard_map/ppermute | solution.py:339
  64.5 20.4 %collective-permute-start.4 = (f32[64,8,128]{2,1,0:T(8,128)S(1)}, f32[64,8,128]{2,1,0:T(8,128)S(1)}, u32[]{:S(2)}, u32[]{:S(2)}) collective-permute-start(f32[64,8,128]{2,1,0:T(8,128)S(1)} %maximum_select_fusion.x_ref), channel_id=1, source_target_pairs={{1,2},{2,1},{3,4},{4,3},{5,6},{6,5},{7,8},{8,7},{9,10},{10,9},{11,... | collective-permute-start | bytes 786440 | tf_op jit(solution)/shard_map/ppermute | solution.py:339
  75.0 11.4 %collective-permute-start.3 = (f32[64,8,128]{2,1,0:T(8,128)S(1)}, f32[64,8,128]{2,1,0:T(8,128)S(1)}, u32[]{:S(2)}, u32[]{:S(2)}) collective-permute-start(f32[64,8,128]{2,1,0:T(8,128)S(1)} %maximum_select_fusion.x_ref), channel_id=1, source_target_pairs={{0,1},{1,0},{2,3},{3,2},{4,5},{5,4},{6,7},{7,6},{8,9},{9,8},{10,11... | collective-permute-start | bytes 786440 | tf_op jit(solution)/shard_map/ppermute | solution.py:339

commit v3 on v2

v3 whole, which is shorter than its diff:
```python
import functools

import jax
import jax.numpy as jnp
from jax import lax
from jax.experimental import pallas as pl
from jax.experimental.pallas import tpu as pltpu
from jax.sharding import Mesh
from jax.sharding import PartitionSpec as P

CX = 16
CY = 8
NZ = 128
GX = ("gx_0", "gx_1", "gx_2")
GY = ("gy_0", "gy_1")
Z_RING = ("gx_0", "gy_0")
PLANE = ("gx_1", "gx_2", "gy_1")
TILES_X = 16
TILES_Y = 32
GRID_CELLS = 256 * 256 * 128
COARSE_CELLS = 64 * 64 * 32

coupling = 0.03125
norm_eps = 1e-06

W0X, W0Y = 64, 56
W1X, W1Y = 32, 32
W2X, W2Y = 36, 40
W3X, W3Y = 18, 24
DEPOSIT_ROWS = 32
KEEP = True
VMEM = pltpu.VMEM


def deposit_kernel(cell_ref, mass_ref, out_ref):
    rows = lax.broadcasted_iota(jnp.int32, (128, 128), 0)
    batch = DEPOSIT_ROWS

    def step(t, acc):
        cells = cell_ref[pl.ds(pl.multiple_of(t * batch, 8), batch), :]
        masses = mass_ref[pl.ds(pl.multiple_of(t * batch, 8), batch), :]
        high = cells >> 7
        low = cells & 127
        coarse = masses.astype(jnp.bfloat16).astype(jnp.float32)
        fine = masses - coarse
        left, right = [], []
        for r in range(batch):
            hit = rows == high[r : r + 1, :]
            first = jnp.where(hit, coarse[r : r + 1, :], 0.0).astype(jnp.bfloat16)
            second = jnp.where(hit, fine[r : r + 1, :], 0.0).astype(jnp.bfloat16)
            left.append(jnp.concatenate([first, second], axis=0))
            right.append(jnp.where(rows == low[r : r + 1, :], 1.0, 0.0).astype(jnp.bfloat16))
        left = jnp.concatenate(left, axis=1)
        right = jnp.concatenate(right, axis=1)
        return acc + lax.dot_general(left, right, (((1,), (1,)), ((), ())), preferred_element_type=jnp.float32)

    total = lax.fori_loop(0, cell_ref.shape[0] // batch, step, jnp.zeros((256, 128), jnp.float32))
    out_ref[...] = total[:128] + total[128:]


def row_parity(rows, lanes_per_cell, extra=0):
    j = lax.broadcasted_iota(jnp.int32, (rows, NZ), 0)
    z = lax.broadcasted_iota(jnp.int32, (rows, NZ), 1) // lanes_per_cell
    return (j + z + extra) & 1


def batched(lo, hi, size, body):
    whole = (hi - lo) // size

    def step(t, carry):
        body(lo + t * size, size)
        return carry

    if whole:
        lax.fori_loop(0, whole, step, 0)
    if (hi - lo) % size:
        body(lo + whole * size, (hi - lo) % size)


def batch_of(rows):
    return 4 if rows >= 40 else 6 if rows >= 24 else 8


def planes(ref, first, count, part):
    return [ref[first + j, part, :] for j in range(count)]


def neighbours(values, j, lanes):
    c = values[j]
    rows = c.shape[0]
    n = values[j - 1] + values[j + 1]
    n = n + (pltpu.roll(c, 1, 0) + pltpu.roll(c, rows - 1, 0))
    return c, n + (pltpu.roll(c, lanes, 1) + pltpu.roll(c, NZ - lanes, 1))


def pair_z(t, lanes):
    z = lax.broadcasted_iota(jnp.int32, t.shape, 1) // lanes
    return t + jnp.where((z & 1) == 0, pltpu.roll(t, NZ - lanes, 1), pltpu.roll(t, lanes, 1))


def first_sweep(u, b, parity, lanes, s, lo, hi):
    rows = parity.shape[0]
    red = (parity == 0, parity == 1)

    def body(first, count):
        values = planes(b, first - 1, count + 2, slice(0, rows))
        for j in range(count):
            c, n = neighbours(values, j + 1, lanes)
            own = c * (s / 6.0)
            u[first + j, 0:rows, :] = jnp.where(red[(lo + j) & 1], own, n * (s / 36.0) + own)

    batched(lo, hi, batch_of(rows), body)


def half_sweep(u, b, shift, parity, colour, lanes, s, lo, hi, top=0):
    rows = parity.shape[0]
    part = slice(top, top + rows)
    chosen = (parity == (colour & 1), parity == ((1 + colour) & 1))

    def body(first, count):
        values = planes(u, first - 1, count + 2, part)
        made = []
        for j in range(count):
            c, n = neighbours(values, j + 1, lanes)
            rhs = (b[first + j, part, :] - shift) * (s / 6.0)
            made.append(jnp.where(chosen[(lo + j) & 1], n * (1.0 / 6.0) + rhs, c))
        for j in range(count):
            u[first + j, part, :] = made[j]

    batched(lo, hi, batch_of(rows), body)


def residual_of(values, j, b, lanes, s):
    c, n = neighbours(values, j, lanes)
    return b - (6.0 * c - n) * (1.0 / s)


def restrict_to(out, u, b, shift, rows, lanes, s, lo, hi, scr, out_rows, top=0):
    part = slice(top, top + rows)

    def body(first, count):
        values = planes(u, 2 * first - 1, 2 * count + 2, part)
        for k in range(count):
            t = residual_of(values, 2 * k + 1, b[2 * (first + k), part, :] - shift, lanes, s)
            t = t + residual_of(values, 2 * k + 2, b[2 * (first + k) + 1, part, :] - shift, lanes, s)
            scr[k, part, :] = pair_z(t, lanes)
        for k in range(count):
            out[first + k] = (scr.at[k][pl.ds(0, out_rows, 2), :] + scr.at[k][pl.ds(1, out_rows, 2), :]) * 0.125

    batched(lo, hi, 2, body)


def add_coarse(fine, base, shift, coarse, offset, first_row, half, lo, hi, top, rows, scr):
    part = slice(top, top + rows)

    def body(first, count):
        for k in range(count):
            c = coarse[first + k + offset, first_row : first_row + half, :]
            scr.at[k][pl.ds(0, half, 2), :] = c
            scr.at[k][pl.ds(1, half, 2), :] = c
        for k in range(count):
            c = scr[k, 0:rows, :] - shift
            i = 2 * (first + k)
            even, odd = base[i, part, :] + c, base[i + 1, part, :] + c
            fine[i, part, :] = even
            fine[i + 1, part, :] = odd

    batched(lo, hi, 4, body)


def own_coarse(u1, b1, send_ref, rows, plane, row):
    lane = lax.broadcasted_iota(jnp.int32, (rows, NZ), 1) & 3
    packed = jnp.zeros((rows, NZ), jnp.float32)
    values = planes(u1, plane - 1, 10, slice(0, rows))
    for x in range(4):
        i = plane + 2 * x
        t = residual_of(values, 2 * x + 1, b1[i, 0:rows, :], 2, 4.0)
        t = t + residual_of(values, 2 * x + 2, b1[i + 1, 0:rows, :], 2, 4.0)
        t = pair_z(t, 2)
        t = (t + pltpu.roll(t, rows - 1, 0)) * 0.125
        packed = jnp.where(lane == x, t, packed)
    for k in range(send_ref.shape[0]):
        send_ref[k, 0:1, :] = packed[row : row + 1, :]
        send_ref[k, 1:2, :] = packed[row + 2 : row + 3, :]


def clear(ref, *indices):
    for i in indices:
        ref[i] = jnp.zeros(ref.shape[1:], jnp.float32)


def coarse_solve(pos_ref, ag, shift, pw, b2, u2, b3, u3, scr):
    gx, gy = pos_ref[0], pos_ref[1]
    for tx in range(9):
        pw[tx, 32:40, :] = jnp.zeros((8, NZ), jnp.float32)
        x = lax.rem(gx + (tx - 4 + TILES_X), TILES_X)
        for ty in range(17):
            y = lax.rem(gy + (ty - 8 + TILES_Y), TILES_Y)
            plane = (x & 7) * 4 + (y & 3)
            ring = (x >> 3) * 8 + (y >> 2)
            pw[tx, 2 * ty : 2 * ty + 2, :] = ag[plane * 16 + ring]
    lane = lax.broadcasted_iota(jnp.int32, (W2Y, NZ), 1) & 3

    def unpack(tx, count):
        t = pw[tx]
        for j in range(4):
            v = jnp.where(lane == j, t, 0.0)
            v = v + pltpu.roll(v, 1 if j % 2 == 0 else NZ - 1, 1)
            v = v + pltpu.roll(v, 2 if j < 2 else NZ - 2, 1)
            b2[4 * tx + j] = v - shift

    batched(0, 9, 1, unpack)
    par2 = row_parity(W2Y, 4)
    clear(u2, 0, W2X - 1)
    first_sweep(u2, b2, par2, 4, 16.0, 1, W2X - 1)
    clear(scr, 0, 1)
    clear(b3, 0, W3X - 1)
    clear(u3, 0, W3X - 1)
    restrict_to(b3, u2, b2, 0.0, W2Y, 4, 16.0, 1, W3X - 1, scr, W3Y)
    par3 = row_parity(W3Y, 8, gy)
    first_sweep(u3, b3, par3, 8, 64.0, 1, W3X - 1)
    for colour in (0, 1):
        half_sweep(u3, b3, 0.0, par3, colour, 8, 64.0, 2, W3X - 2)
    add_coarse(u2, u2, 0.0, u3, 0, 0, W3Y, 4, 14, 0, W2Y, scr)
    half_sweep(u2, b2, 0.0, par2, 0, 4, 16.0, 9, 27)
    half_sweep(u2, b2, 0.0, par2, 1, 4, 16.0, 10, 26)


def up_level1(v1, u1, b1, shift, u2, scr, lo, hi, top, rows):
    add_coarse(v1, u1, shift * (4.0 / 3.0), u2, 10, 10 + top // 2, rows // 2, lo // 2, hi // 2, top, rows, scr)
    par1 = row_parity(rows, 2)
    for colour in (0, 1):
        half_sweep(v1, b1, shift, par1, colour, 2, 4.0, lo + 1, hi - 1, top)


def up_level0(v0, u0, d, shift, base, v1, scr, lo, hi, top, rows):
    half = (rows // 2 + 7) // 8 * 8
    add_coarse(v0, u0, base, v1, 0, top // 2, half, lo // 2, hi // 2, top, rows, scr)
    par0 = row_parity(rows, 1)
    for colour in (0, 1):
        half_sweep(v0, d, shift, par0, colour, 1, 1.0, lo + 1, hi - 1, top)


def join_rows(d, pos_ref, wide, e, o, first, last, own):
    d[:, own : own + 8, :] = wide[first:last]
    even = (pos_ref[1] & 1) == 0

    def place(e_row, o_row):
        d[:, e_row : e_row + 8, :] = e[first:last]
        d[:, o_row : o_row + 8, :] = o[first:last]

    pl.when(even)(functools.partial(place, own + 8, own - 8))
    pl.when(jnp.logical_not(even))(functools.partial(place, own - 8, own + 8))


def send_kernel(pos_ref, wide, e, o, send_ref, d, u0, b1, u1, scr):
    join_rows(d, pos_ref, wide, e, o, 16, 48, 8)
    clear(u0, 0, 31)
    first_sweep(u0, d, row_parity(24, 1), 1, 1.0, 1, 31)
    clear(scr, 0, 1)
    clear(b1, 0, 15)
    clear(u1, 0, 15)
    restrict_to(b1, u0, d, 0.0, 24, 1, 1.0, 1, 15, scr, 16)
    first_sweep(u1, b1, row_parity(16, 2), 2, 4.0, 1, 15)
    own_coarse(u1, b1, send_ref, 16, 4, 4)


def own_residual(u, d, shift):
    values = planes(u, 23, 18, slice(16, 40))
    return [residual_of(values, x + 1, d[24 + x, 16:40, :] - shift, 1, 1.0)[8:16] for x in range(CX)]


def wide_kernel(pos_ref, wide, e, o, s, t, d, u0, b1, u1, scr):
    for i in range(16):
        d[i] = jnp.zeros((W0Y, NZ), jnp.float32)
        d[48 + i] = jnp.zeros((W0Y, NZ), jnp.float32)
    join_rows(d, pos_ref, wide, e, o, 0, 64, 24)
    even = (pos_ref[1] & 1) == 0

    def place(o_row, s_row, s_far, t_row):
        d[8:56, o_row : o_row + 8, :] = o[64:112]
        d[8:56, s_row : s_row + 8, :] = s[0:48]
        d[16:48, s_far : s_far + 8, :] = s[48:80]
        d[16:48, t_row : t_row + 8, :] = t[...]

    pl.when(even)(functools.partial(place, 8, 40, 48, 0))
    pl.when(jnp.logical_not(even))(functools.partial(place, 40, 8, 0, 48))
    clear(u0, 0, W0X - 1)
    first_sweep(u0, d, row_parity(W0Y, 1), 1, 1.0, 1, W0X - 1)
    clear(scr, 0, 1)
    clear(b1, 0, W1X - 1)
    clear(u1, 0, W1X - 1)
    restrict_to(b1, u0, d, 0.0, W0Y, 1, 1.0, 1, W1X - 1, scr, W1Y)
    first_sweep(u1, b1, row_parity(W1Y, 2), 2, 4.0, 1, W1X - 1)


def mid_kernel(pos_ref, ag, d, u0, b1, u1, send_ref, u0n, b1n, u1n, stat_ref, v1, pw, b2, u2, b3, u3, scr):
    total = jnp.sum(jnp.sum(ag[...], axis=0))
    mean = total * (1.0 / COARSE_CELLS)
    clear(scr, 2, 3)
    coarse_solve(pos_ref, ag, mean, pw, b2, u2, b3, u3, scr)
    up_level1(v1, u1, b1, mean, u2, scr, 0, W1X, 0, W1Y)
    up_level0(u0n, u0, d, mean, mean * (1.0 / 3.0), v1, scr, 8, 56, 8, 40)
    stat_ref[0:8, :] = sum(r * r for r in own_residual(u0n, d, mean))
    stat_ref[8:16, :] = jnp.full((8, NZ), mean, jnp.float32)
    par0 = row_parity(40, 1)
    for colour in (0, 1):
        half_sweep(u0n, d, mean, par0, colour, 1, 1.0, 10, 54, 8)
    clear(scr, 0, 1)
    clear(b1n, *range(6), *range(26, W1X))
    restrict_to(b1n, u0n, d, mean, 40, 1, 1.0, 6, 26, scr, W1Y, 8)
    clear(u1n, 0, W1X - 1)
    first_sweep(u1n, b1n, row_parity(W1Y, 2), 2, 4.0, 1, W1X - 1)
    own_coarse(u1n, b1n, send_ref, W1Y, 12, 12)


def post_kernel(pos_ref, ag, d, u0, b1, u1, stat, pot_ref, res_ref, sums_ref, v0, v1, pw, b2, u2, b3, u3, scr):
    mean = jnp.max(stat[8:16, :])
    coarse_solve(pos_ref, ag, 0.0, pw, b2, u2, b3, u3, scr)
    up_level1(v1, u1, b1, 0.0, u2, scr, 8, 24, 8, 16)
    up_level0(v0, u0, d, mean, 0.0, v1, scr, 20, 44, 16, 24)
    inv = 1.0 / jnp.full((CY, NZ), mean, jnp.float32)
    total = jnp.zeros((CY, NZ), jnp.float32)
    for i, r in enumerate(own_residual(v0, d, mean)):
        r = r * inv
        total = total + r * r
        res_ref[i] = -r
        pot_ref[i] = v0[24 + i, 24:32, :] * (-coupling * inv)
    first = stat[0:8, :] * (inv * inv)
    lane = lax.broadcasted_iota(jnp.int32, (1, NZ), 1)
    both = jnp.where(lane == 0, jnp.sum(first), 0.0) + jnp.where(lane == 1, jnp.sum(total), 0.0)
    for k in range(sums_ref.shape[0]):
        sums_ref[k] = both


def f32(*shape):
    return jax.ShapeDtypeStruct(shape, jnp.float32)


def kept(*shape):
    return pltpu.VMEM(shape, jnp.float32) if KEEP else f32(*shape)


def resident(x):
    return pltpu.with_memory_space_constraint(x, pltpu.VMEM) if KEEP else x


def vmem(*shape):
    return pltpu.VMEM(shape, jnp.float32)


COARSE_SCRATCH = (vmem(9, W2Y, NZ), vmem(W2X, W2Y, NZ), vmem(W2X, W2Y, NZ), vmem(W3X, W3Y, NZ), vmem(W3X, W3Y, NZ), vmem(4, 64, NZ))
LEVELS_OUT = (kept(W0X, W0Y, NZ), kept(W1X, W1Y, NZ), kept(W1X, W1Y, NZ))


def call(kernel, outs, scratch, *args, pos=None, cost=None):
    whole = pl.BlockSpec(memory_space=VMEM)
    specs = [whole] * len(args)
    args = tuple(resident(a) for a in args)
    if pos is not None:
        specs = [pl.BlockSpec(memory_space=pltpu.SMEM)] + specs
        args = (pos, *args)
    return pl.pallas_call(
        kernel,
        out_shape=outs,
        in_specs=specs,
        out_specs=jax.tree.map(lambda _: whole, outs),
        scratch_shapes=list(scratch),
        cost_estimate=cost and pl.CostEstimate(flops=cost, transcendentals=0, bytes_accessed=0),
        compiler_params=pltpu.CompilerParams(vmem_limit_bytes=24 * 1024 * 1024),
    )(*args)


def pairs(count, step, chosen):
    both = []
    for i in range(count):
        if chosen(i):
            both += [(i, (i + step) % count), ((i + step) % count, i)]
    return both


def swap(x, axis, step, chosen):
    return lax.ppermute(x, axis, pairs(lax.axis_size(axis), step, chosen))


def even(i):
    return i % 2 == 0


def odd(i):
    return i % 2 == 1


def gather_all(block):
    ring = lax.all_to_all(block, Z_RING, 0, 0)
    copies = jnp.broadcast_to(ring[None], (32, *ring.shape))
    return lax.all_to_all(copies, PLANE, 0, 0)


def x_window(d):
    first = lax.axis_index("gx_2") == 0
    partner = swap(d, GX, 1, even)
    chip = jnp.where(first, jnp.concatenate([d, partner]), jnp.concatenate([partner, d]))
    far = swap(jnp.where(first, chip[:24], chip[8:]), GX, 1, odd)
    near = swap(jnp.where(first, chip[24:], chip[:8]), GX, 3, even)
    return jnp.where(first, jnp.concatenate([far, chip, near]), jnp.concatenate([near, chip, far]))


def per_device(particle_cell, particle_mass):
    tile_x = lax.axis_index(GX)
    tile_y = lax.axis_index(GY)
    pos = jnp.stack([tile_x, tile_y]).astype(jnp.int32)
    cells = particle_cell.reshape(512, 128)
    masses = particle_mass.reshape(512, 128)
    density = call(deposit_kernel, kept(128, 128), (), cells, masses).reshape(CX, CY, NZ)
    wide = x_window(density)
    e = swap(wide, GY, 1, even)
    t = swap(wide[16:48], GY, 3, odd)
    o = swap(jnp.concatenate([wide, e[8:56]]), GY, 1, odd)
    s = swap(jnp.concatenate([e[8:56], wide[16:48]]), GY, 3, even)
    send = call(
        send_kernel,
        kept(16, 2, NZ),
        (vmem(32, 24, NZ), vmem(32, 24, NZ), vmem(16, 16, NZ), vmem(16, 16, NZ), vmem(4, 64, NZ)),
        wide, e, o,
        pos=pos,
    )
    got = gather_all(send).reshape(512, 2, NZ)
    d, u0, b1, u1 = call(
        wide_kernel, (kept(W0X, W0Y, NZ), *LEVELS_OUT), (vmem(4, 64, NZ),), wide, e, o, s, t, pos=pos, cost=20_000_000
    )
    send, u0, b1, u1, stat = call(
        mid_kernel,
        (kept(16, 2, NZ), *LEVELS_OUT, kept(16, NZ)),
        (vmem(W1X, W1Y, NZ), *COARSE_SCRATCH),
        got, d, u0, b1, u1,
        pos=pos,
    )
    got = gather_all(send).reshape(512, 2, NZ)
    potential, residual, sums = call(
        post_kernel,
        (f32(CX, CY, NZ), f32(CX, CY, NZ), kept(16, 1, NZ)),
        (vmem(W0X, W0Y, NZ), vmem(W1X, W1Y, NZ), *COARSE_SCRATCH),
        got, d, u0, b1, u1, stat,
        pos=pos,
    )
    ring = jnp.sum(lax.all_to_all(sums, Z_RING, 0, 0), axis=0)
    total = jnp.sum(lax.all_to_all(jnp.broadcast_to(ring[None], (32, 1, NZ)), PLANE, 0, 0), axis=(0, 1))
    norms = jnp.sqrt(total[:2] / GRID_CELLS + norm_eps)
    return potential, residual, norms


def solution(mesh):
    split = Mesh(mesh.devices.reshape(2, 4, 2, 8, 4), ("gx_0", "gx_1", "gx_2", "gy_0", "gy_1"))
    placed = (P(GX, GY, None), P(GX, GY, None))
    return jax.shard_map(
        per_device,
        mesh=split,
        in_specs=placed,
        out_specs=(P(GX, GY, None), P(GX, GY, None), P()),
        check_vma=False,
    )
```

time: 238 us -> 232 us (0.975)
  waiting for transfers between devices: 13.2 us -> 33.1 us
  Pallas kernels: 68.5 us -> 49.3 us
  blocking collectives: 94.9 us -> 86.2 us
  local copies, waits for them, and re-layouts: 2.36 us -> 9.64 us
  starting transfers between devices: 56.6 us -> 51 us
    ppermute x9 -> x7, waiting for transfers between devices: 13.2 us -> 33.1 us  [swap(): return lax.ppermute(x, axis, pairs(lax.axis_size(axis), step, chosen))]
    pallas_call x4 -> x5, Pallas kernels: 68.5 us -> 49.3 us  [call(): pl.pallas_call(kernel, out_shape=outs, in_specs=specs, out_specs=jax.tree...]
    all_to_all x2 -> x1, blocking collectives: 35.4 us -> 20 us  [gather_all(): return lax.all_to_all(copies, PLANE, 0, 0)]
    ppermute x9 -> x7, starting transfers between devices: 56.6 us -> 44 us  [swap(): return lax.ppermute(x, axis, pairs(lax.axis_size(axis), step, chosen))]
    all_to_all x0 -> x1, starting transfers between devices: none -> 7 us  [gather_all(): return lax.all_to_all(copies, PLANE, 0, 0)]
    all_to_all x2, blocking collectives: 33.5 us -> 40.1 us  [gather_all(): ring = lax.all_to_all(block, Z_RING, 0, 0)]
    unnamed x4 -> x16, local copies, waits for them, and re-layouts: 1.89 us -> 8.35 us
  transfers between devices with their start and end apart: 9 -> 8, of which waited for: 5 -> 5; matrix products, arithmetic and copies ran while one was open for 0% -> 0% of each run, Pallas kernels for 0% -> 3%
where the time goes in v3:
time: 232 us; the launch traced here: 231 us
  blocking collectives  86.2 us (37%)
  starting transfers between devices  51 us (22%)
  Pallas kernels  49.3 us (21%)
  waiting for transfers between devices  33.1 us (14%)
  local copies, waits for them, and re-layouts  9.64 us (4%)
    pallas_call x5, Pallas kernels, call(): pl.pallas_call(kernel, out_shape=outs, in_specs=specs, out_specs=jax.tree...  49.3 us
    ppermute x7, starting transfers between devices, swap(): return lax.ppermute(x, axis, pairs(lax.axis_size(axis), step, chosen))  44 us
    all_to_all x2, blocking collectives, gather_all(): ring = lax.all_to_all(block, Z_RING, 0, 0)  40.1 us
    ppermute x7, waiting for transfers between devices, swap(): return lax.ppermute(x, axis, pairs(lax.axis_size(axis), step, chosen))  33.1 us
    all_to_all x1, blocking collectives, gather_all(): return lax.all_to_all(copies, PLANE, 0, 0)  20 us
    all_to_all x1, blocking collectives, per_device(): ring = jnp.sum(lax.all_to_all(sums, Z_RING, 0, 0), axis=0)  13.9 us
    all_to_all x1, blocking collectives, per_device(): lax.all_to_all(jnp.broadcast_to(ring[None], (32, 1, NZ)), PLANE, 0, 0)  12.2 us
    unnamed x16, local copies, waits for them, and re-layouts  8.35 us
  transfers between devices with their start and end apart: 8, of which 5 were waited for; matrix products, arithmetic and copies ran while one was open for 0% of the time, Pallas kernels for 3%

profile of v3, /device:TPU:1, one launch (start us, length us, event | category | flops | bytes accessed | tf_op | source)
XLA Modules:
  0.0 230.9 jit_solution(15513553684277338248)
XLA Ops:
  0.6 0.0 copy-start.6
  0.6 0.9 copy-done.6
  1.6 0.0 copy-start.7
  1.6 0.9 copy-done.7
  2.5 13.9 %shard_map.49 = f32[128,128]{1,0:T(8,128)S(1)} custom-call(s32[512,128]{1,0:T(8,128)S(1)} %bitcast.10, f32[512,128]{1,0:T(8,128)S(1)} %bitcast.11), custom_call_target="tpu_custom_call" | custom-call | tf_op jit(solution)/shard_map/pallas_call | solution.py:363
  16.4 8.7 %collective-permute-start = (f32[16,8,128]{2,1,0:T(8,128)S(1)}, f32[16,8,128]{2,1,0:T(8,128)S(1)}, u32[]{:S(2)}, u32[]{:S(2)}) collective-permute-start(f32[16,8,128]{2,1,0:T(8,128)S(1)} %bitcast.12), channel_id=1, source_target_pairs={{0,32},{32,0},{64,96},{96,64},{128,160},{160,128},{192,224},{224,1... | collective-permute-start | bytes 196616 | tf_op jit(solution)/shard_map/ppermute | solution.py:383
  25.2 0.9 collective-permute-done
  26.1 1.9 collective-permute-start.1
  28.0 13.2 %collective-permute-start.2 = (f32[8,8,128]{2,1,0:T(8,128)S(1)}, f32[8,8,128]{2,1,0:T(8,128)S(1)}, u32[]{:S(2)}, u32[]{:S(2)}) collective-permute-start(f32[8,8,128]{2,1,0:T(8,128)S(1)} %slice_select_fusion.1), channel_id=1, source_target_pairs={{0,96},{96,0},{64,160},{160,64},{128,224},{224,128},{192,288},{288... | collective-permute-start | bytes 98312 | tf_op jit(solution)/shard_map/ppermute | solution.py:383
  41.2 2.9 %collective-permute-done.2 = f32[8,8,128]{2,1,0:T(8,128)S(1)} collective-permute-done((f32[8,8,128]{2,1,0:T(8,128)S(1)}, f32[8,8,128]{2,1,0:T(8,128)S(1)}, u32[]{:S(2)}, u32[]{:S(2)}) %collective-permute-start.2) | collective-permute-done | bytes 32800 | tf_op jit(solution)/shard_map/ppermute | solution.py:383
  44.1 0.0 collective-permute-done.1
  44.1 2.0 collective-permute-start.3
  46.1 7.7 %collective-permute-done.3.e = f32[64,8,128]{2,1,0:T(8,128)S(1)} collective-permute-done((f32[64,8,128]{2,1,0:T(8,128)S(1)}, f32[64,8,128]{2,1,0:T(8,128)S(1)}, u32[]{:S(2)}, u32[]{:S(2)}) %collective-permute-start.3) | collective-permute-done | bytes 262176 | tf_op jit(solution)/shard_map/ppermute | solution.py:383
  53.9 10.9 %collective-permute-start.4 = (f32[112,8,128]{2,1,0:T(8,128)S(1)}, f32[112,8,128]{2,1,0:T(8,128)S(1)}, u32[]{:S(2)}, u32[]{:S(2)}) collective-permute-start(f32[112,8,128]{2,1,0:T(8,128)S(1)} %pad_maximum_fusion), channel_id=1, source_target_pairs={{1,2},{2,1},{3,4},{4,3},{5,6},{6,5},{7,8},{8,7},{9,10},{10,9},{11,... | collective-permute-start | bytes 1376264 | tf_op jit(solution)/shard_map/ppermute | solution.py:383
  64.8 0.1 pad_add_fusion.pos_ref
  64.8 10.8 %collective-permute-done.4.o = f32[112,8,128]{2,1,0:T(8,128)S(1)} collective-permute-done((f32[112,8,128]{2,1,0:T(8,128)S(1)}, f32[112,8,128]{2,1,0:T(8,128)S(1)}, u32[]{:S(2)}, u32[]{:S(2)}) %collective-permute-start.4) | collective-permute-done | bytes 458784 | tf_op jit(solution)/shard_map/ppermute | solution.py:383
  75.6 2.6 %shard_map.50 = f32[16,2,128]{2,1,0:T(2,128)S(1)} custom-call(s32[2]{0:T(128)S(1)} %pad_add_fusion.pos_ref, f32[64,8,128]{2,1,0:T(8,128)S(1)} %maximum_select_fusion.wide, f32[64,8,128]{2,1,0:T(8,128)S(1)} %collective-permute-done.3.e, f32[112,8,128]{2,1,0:T(8,128)S(1)} %collective-permute-done.4.o), custom_call_target="tpu_custom_call" | custom-call | tf_op jit(solution)/shard_map/pallas_call | solution.py:363
  78.3 22.8 %all_to_all.30 = f32[16,2,128]{2,1,0:T(2,128)S(1)} all-to-all(f32[16,2,128]{2,1,0:T(2,128)S(1)} %shard_map.50), channel_id=1, replica_groups=mesh['gx_0'=2,'gx_1'=4,'gx_2'=2,'gy_0'=8,'gy_1'=4] {'gx_0','gy_0'}, dimensions={0} | all-to-all | bytes 32768 | tf_op jit(solution)/shard_map/all_to_all | solution.py:395
  101.0 1.0 broadcast_in_dim.6
  102.1 7.0 %all-to-all-start.1 = ((f32[32,16,2,128]{3,2,1,0:T(2,128)}), f32[32,16,2,128]{3,2,1,0:T(2,128)S(1)}, u32[]{:S(2)}, u32[]{:S(2)}) async-start(f32[32,16,2,128]{3,2,1,0:T(2,128)} %broadcast_in_dim.6), calls=%async_computation.1 | async-start | bytes 1048576 | tf_op jit(solution)/shard_map/all_to_all | solution.py:397
  109.1 4.5 %collective-permute-start.5 = (f32[80,8,128]{2,1,0:T(8,128)S(1)}, f32[80,8,128]{2,1,0:T(8,128)S(1)}, u32[]{:S(2)}, u32[]{:S(2)}) collective-permute-start(f32[80,8,128]{2,1,0:T(8,128)S(1)} %pad_maximum_fusion.1), channel_id=1, source_target_pairs={{0,3},{3,0},{2,5},{5,2},{4,7},{7,4},{6,9},{9,6},{8,11},{11,8},{10,... | collective-permute-start | bytes 983048 | tf_op jit(solution)/shard_map/ppermute | solution.py:383
  113.6 2.9 %collective-permute-start.6 = (f32[32,8,128]{2,1,0:T(8,128)S(1)}, f32[32,8,128]{2,1,0:T(8,128)S(1)}, u32[]{:S(2)}, u32[]{:S(2)}) collective-permute-start(f32[32,8,128]{2,1,0:T(8,128)S(1)} %slice.35), channel_id=1, source_target_pairs={{1,4},{4,1},{3,6},{6,3},{5,8},{8,5},{7,10},{10,7},{9,12},{12,9},{1... | collective-permute-start | bytes 393224 | tf_op jit(solution)/shard_map/ppermute | solution.py:383
  116.5 10.9 %collective-permute-done.6.t = f32[32,8,128]{2,1,0:T(8,128)S(1)} collective-permute-done((f32[32,8,128]{2,1,0:T(8,128)S(1)}, f32[32,8,128]{2,1,0:T(8,128)S(1)}, u32[]{:S(2)}, u32[]{:S(2)}) %collective-permute-start.6) | collective-permute-done | bytes 131104 | tf_op jit(solution)/shard_map/ppermute | solution.py:383
  127.4 0.0 collective-permute-done.5.s
  127.4 6.6 %shard_map.51 = (f32[64,56,128]{2,1,0:T(8,128)S(1)}, f32[64,56,128]{2,1,0:T(8,128)S(1)}, f32[32,32,128]{2,1,0:T(8,128)S(1)}, f32[32,32,128]{2,1,0:T(8,128)S(1)}) custom-call(s32[2]{0:T(128)S(1)} %pad_add_fusion.pos_ref, f32[64,8,128]{2,1,0:T(8,128)S(1)} %maximum_select_fusion.wide, f32[64,8,128]{2,1,0:T(8,128)S(1)} %collective-permute-done.3.e, ...), custom_call_target="tpu_custom_call" | custom-call | flops 20000000 | tf_op jit(solution)/shard_map/pallas_call | solution.py:363
  134.1 0.0 copy-start
  134.1 1.3 copy-done
  135.3 0.0 copy-start.2
  135.3 0.8 copy-done.2
  136.2 0.0 copy-start.4
  136.2 0.8 copy-done.4
  136.9 0.0 all-to-all-done.1
  136.9 0.0 copy-start.1
  136.9 1.5 copy-done.1
  138.4 0.0 copy-start.3
  138.4 1.0 copy-done.3
  139.5 0.0 copy-start.5
  139.5 1.0 copy-done.5
  140.5 17.3 %shard_map.52 = (f32[16,2,128]{2,1,0:T(2,128)S(1)}, f32[64,56,128]{2,1,0:T(8,128)S(1)}, f32[32,32,128]{2,1,0:T(8,128)S(1)}, f32[32,32,128]{2,1,0:T(8,128)S(1)}, f32[16,128]{1,0:T(8,128)S(1)}) custom-call(s32[2]{0:T(128)S(1)} %pad_add_fusion.pos_ref, f32[512,2,128]{2,1,0:T(2,128)S(1)} %bitcast.8, f32[64,56,128]{2,1,0:T(8,128)S(1)} %get-tuple-element.15.d, ...), custom_call_target="tpu_custom_call" | custom-call | tf_op jit(solution)/shard_map/pallas_call | solution.py:363
  157.8 17.4 %all_to_all.31 = f32[16,2,128]{2,1,0:T(2,128)S(1)} all-to-all(f32[16,2,128]{2,1,0:T(2,128)S(1)} %get-tuple-element.19), channel_id=1, replica_groups=mesh['gx_0'=2,'gx_1'=4,'gx_2'=2,'gy_0'=8,'gy_1'=4] {'gx_0','gy_0'}, dimensions={0} | all-to-all | bytes 32768 | tf_op jit(solution)/shard_map/all_to_all | solution.py:395
  175.2 0.2 broadcast_in_dim.7
  175.4 20.0 %all_to_all.32 = f32[32,16,2,128]{3,2,1,0:T(2,128)S(1)} all-to-all(f32[32,16,2,128]{3,2,1,0:T(2,128)S(1)} %broadcast_in_dim.7), channel_id=1, replica_groups=mesh['gx_0'=2,'gx_1'=4,'gx_2'=2,'gy_0'=8,'gy_1'=4] {'gx_1','gx_2','gy_1'}, dimensions={0} | all-to-all | bytes 1048576 | tf_op jit(solution)/shard_map/all_to_all | solution.py:397
  195.4 8.9 %shard_map.53 = (f32[16,8,128]{2,1,0:T(8,128)}, f32[16,8,128]{2,1,0:T(8,128)}, f32[16,1,128]{2,1,0:T(1,128)S(1)}) custom-call(s32[2]{0:T(128)S(1)} %pad_add_fusion.pos_ref, f32[512,2,128]{2,1,0:T(2,128)S(1)} %bitcast.9, f32[64,56,128]{2,1,0:T(8,128)S(1)} %get-tuple-element.15.d, f32[64,56,128]{2,1,0:T(8,128)S(1)} %get-tuple-element.20.u0, ...), custom_call_target="tpu_custom_call" | custom-call | tf_op jit(solution)/shard_map/pallas_call | solution.py:363
  204.3 13.9 %all_to_all.33 = f32[16,1,128]{2,1,0:T(1,128)S(1)} all-to-all(f32[16,1,128]{2,1,0:T(1,128)S(1)} %get-tuple-element.26), channel_id=1, replica_groups=mesh['gx_0'=2,'gx_1'=4,'gx_2'=2,'gy_0'=8,'gy_1'=4] {'gx_0','gy_0'}, dimensions={0} | all-to-all | bytes 16384 | tf_op jit(solution)/shard_map/all_to_all | solution.py:447
  218.2 12.2 %all_to_all.34 = f32[32,1,128]{2,1,0:T(1,128)S(1)} all-to-all(f32[32,1,128]{2,1,0:T(1,128)S(1)} %broadcast_in_dim.8), channel_id=1, replica_groups=mesh['gx_0'=2,'gx_1'=4,'gx_2'=2,'gy_0'=8,'gy_1'=4] {'gx_1','gx_2','gy_1'}, dimensions={0} | all-to-all | bytes 32768 | tf_op jit(solution)/shard_map/all_to_all | solution.py:448
  230.4 0.5 add_sqrt_fusion
  (11 shorter events, 0.2 us)
Async XLA Ops:
  0.6 1.0 copy-start.6
  1.6 0.9 copy-start.7
  16.4 9.6 %collective-permute-start = (f32[16,8,128]{2,1,0:T(8,128)S(1)}, f32[16,8,128]{2,1,0:T(8,128)S(1)}, u32[]{:S(2)}, u32[]{:S(2)}) collective-permute-start(f32[16,8,128]{2,1,0:T(8,128)S(1)} %bitcast.12), channel_id=1, source_target_pairs={{0,32},{32,0},{64,96},{96,64},{128,160},{160,128},{192,224},{224,1... | collective-permute-start | bytes 196616 | tf_op jit(solution)/shard_map/ppermute | solution.py:383
  26.1 18.0 %collective-permute-start.1 = (f32[24,8,128]{2,1,0:T(8,128)S(1)}, f32[24,8,128]{2,1,0:T(8,128)S(1)}, u32[]{:S(2)}, u32[]{:S(2)}) collective-permute-start(f32[24,8,128]{2,1,0:T(8,128)S(1)} %slice_select_fusion), channel_id=1, source_target_pairs={{32,64},{64,32},{96,128},{128,96},{160,192},{192,160},{224,256},{2... | collective-permute-start | bytes 294920 | tf_op jit(solution)/shard_map/ppermute | solution.py:383
  28.0 16.1 %collective-permute-start.2 = (f32[8,8,128]{2,1,0:T(8,128)S(1)}, f32[8,8,128]{2,1,0:T(8,128)S(1)}, u32[]{:S(2)}, u32[]{:S(2)}) collective-permute-start(f32[8,8,128]{2,1,0:T(8,128)S(1)} %slice_select_fusion.1), channel_id=1, source_target_pairs={{0,96},{96,0},{64,160},{160,64},{128,224},{224,128},{192,288},{288... | collective-permute-start | bytes 98312 | tf_op jit(solution)/shard_map/ppermute | solution.py:383
  44.1 9.7 %collective-permute-start.3 = (f32[64,8,128]{2,1,0:T(8,128)S(1)}, f32[64,8,128]{2,1,0:T(8,128)S(1)}, u32[]{:S(2)}, u32[]{:S(2)}) collective-permute-start(f32[64,8,128]{2,1,0:T(8,128)S(1)} %maximum_select_fusion.wide), channel_id=1, source_target_pairs={{0,1},{1,0},{2,3},{3,2},{4,5},{5,4},{6,7},{7,6},{8,9},{9,8},{10,11... | collective-permute-start | bytes 786440 | tf_op jit(solution)/shard_map/ppermute | solution.py:383
  53.9 21.8 %collective-permute-start.4 = (f32[112,8,128]{2,1,0:T(8,128)S(1)}, f32[112,8,128]{2,1,0:T(8,128)S(1)}, u32[]{:S(2)}, u32[]{:S(2)}) collective-permute-start(f32[112,8,128]{2,1,0:T(8,128)S(1)} %pad_maximum_fusion), channel_id=1, source_target_pairs={{1,2},{2,1},{3,4},{4,3},{5,6},{6,5},{7,8},{8,7},{9,10},{10,9},{11,... | collective-permute-start | bytes 1376264 | tf_op jit(solution)/shard_map/ppermute | solution.py:383
  102.1 34.9 %all-to-all-start.1 = ((f32[32,16,2,128]{3,2,1,0:T(2,128)}), f32[32,16,2,128]{3,2,1,0:T(2,128)S(1)}, u32[]{:S(2)}, u32[]{:S(2)}) async-start(f32[32,16,2,128]{3,2,1,0:T(2,128)} %broadcast_in_dim.6), calls=%async_computation.1 | async-start | bytes 1048576 | tf_op jit(solution)/shard_map/all_to_all | solution.py:397
  109.1 18.3 %collective-permute-start.5 = (f32[80,8,128]{2,1,0:T(8,128)S(1)}, f32[80,8,128]{2,1,0:T(8,128)S(1)}, u32[]{:S(2)}, u32[]{:S(2)}) collective-permute-start(f32[80,8,128]{2,1,0:T(8,128)S(1)} %pad_maximum_fusion.1), channel_id=1, source_target_pairs={{0,3},{3,0},{2,5},{5,2},{4,7},{7,4},{6,9},{9,6},{8,11},{11,8},{10,... | collective-permute-start | bytes 983048 | tf_op jit(solution)/shard_map/ppermute | solution.py:383
  113.6 13.8 %collective-permute-start.6 = (f32[32,8,128]{2,1,0:T(8,128)S(1)}, f32[32,8,128]{2,1,0:T(8,128)S(1)}, u32[]{:S(2)}, u32[]{:S(2)}) collective-permute-start(f32[32,8,128]{2,1,0:T(8,128)S(1)} %slice.35), channel_id=1, source_target_pairs={{1,4},{4,1},{3,6},{6,3},{5,8},{8,5},{7,10},{10,7},{9,12},{12,9},{1... | collective-permute-start | bytes 393224 | tf_op jit(solution)/shard_map/ppermute | solution.py:383
  134.1 1.3 copy-start
  135.3 0.8 copy-start.2
  136.2 0.8 copy-start.4
  136.9 1.5 copy-start.1
  138.4 1.0 copy-start.3
  139.5 1.0 copy-start.5

commit v4 on v3

--- a/solution.py
+++ b/solution.py
@@ -29,6 +29,9 @@
 W3X, W3Y = 18, 24
 DEPOSIT_ROWS = 32
 KEEP = True
+RESTRICT = 4
+ADD = 4
+SIZES = (6, 8, 10, 16, 16)
 VMEM = pltpu.VMEM
 
 
@@ -65,20 +68,21 @@
 
 
 def batched(lo, hi, size, body):
-    whole = (hi - lo) // size
+    size = min(size, hi - lo)
+    runs = -(-(hi - lo) // size)
+    if runs == 1:
+        body(lo, size)
+        return
 
     def step(t, carry):
-        body(lo + t * size, size)
+        body(jnp.minimum(lo + t * size, hi - size), size)
         return carry
 
-    if whole:
-        lax.fori_loop(0, whole, step, 0)
-    if (hi - lo) % size:
-        body(lo + whole * size, (hi - lo) % size)
+    lax.fori_loop(0, runs, step, 0)
 
 
 def batch_of(rows):
-    return 4 if rows >= 40 else 6 if rows >= 24 else 8
+    return {56: SIZES[0], 40: SIZES[1], 32: SIZES[2], 24: SIZES[3], 16: SIZES[4]}[rows]
 
 
 def planes(ref, first, count, part):
@@ -147,7 +151,7 @@
         for k in range(count):
             out[first + k] = (scr.at[k][pl.ds(0, out_rows, 2), :] + scr.at[k][pl.ds(1, out_rows, 2), :]) * 0.125
 
-    batched(lo, hi, 2, body)
+    batched(lo, hi, RESTRICT, body)
 
 
 def add_coarse(fine, base, shift, coarse, offset, first_row, half, lo, hi, top, rows, scr):
@@ -165,7 +169,7 @@
             fine[i, part, :] = even
             fine[i + 1, part, :] = odd
 
-    batched(lo, hi, 4, body)
+    batched(lo, hi, (hi - lo) // 2 if base is fine else ADD, body)
 
 
 def own_coarse(u1, b1, send_ref, rows, plane, row):
@@ -201,19 +205,20 @@
             pw[tx, 2 * ty : 2 * ty + 2, :] = ag[plane * 16 + ring]
     lane = lax.broadcasted_iota(jnp.int32, (W2Y, NZ), 1) & 3
 
-    def unpack(tx, count):
-        t = pw[tx]
-        for j in range(4):
-            v = jnp.where(lane == j, t, 0.0)
-            v = v + pltpu.roll(v, 1 if j % 2 == 0 else NZ - 1, 1)
-            v = v + pltpu.roll(v, 2 if j < 2 else NZ - 2, 1)
-            b2[4 * tx + j] = v - shift
-
-    batched(0, 9, 1, unpack)
+    def unpack(first, count):
+        for k in range(count):
+            t = pw[first + k]
+            for j in range(4):
+                v = jnp.where(lane == j, t, 0.0)
+                v = v + pltpu.roll(v, 1 if j % 2 == 0 else NZ - 1, 1)
+                v = v + pltpu.roll(v, 2 if j < 2 else NZ - 2, 1)
+                b2[4 * (first + k) + j] = v - shift
+
+    batched(0, 9, 3, unpack)
     par2 = row_parity(W2Y, 4)
     clear(u2, 0, W2X - 1)
     first_sweep(u2, b2, par2, 4, 16.0, 1, W2X - 1)
-    clear(scr, 0, 1)
+    clear(scr, *range(RESTRICT))
     clear(b3, 0, W3X - 1)
     clear(u3, 0, W3X - 1)
     restrict_to(b3, u2, b2, 0.0, W2Y, 4, 16.0, 1, W3X - 1, scr, W3Y)
@@ -241,23 +246,23 @@
         half_sweep(v0, d, shift, par0, colour, 1, 1.0, lo + 1, hi - 1, top)
 
 
-def join_rows(d, pos_ref, wide, e, o, first, last, own):
-    d[:, own : own + 8, :] = wide[first:last]
+def beside(pos_ref, place, own):
     even = (pos_ref[1] & 1) == 0
-
-    def place(e_row, o_row):
-        d[:, e_row : e_row + 8, :] = e[first:last]
-        d[:, o_row : o_row + 8, :] = o[first:last]
-
     pl.when(even)(functools.partial(place, own + 8, own - 8))
     pl.when(jnp.logical_not(even))(functools.partial(place, own - 8, own + 8))
 
 
-def send_kernel(pos_ref, wide, e, o, send_ref, d, u0, b1, u1, scr):
-    join_rows(d, pos_ref, wide, e, o, 16, 48, 8)
+def send_kernel(pos_ref, wide, e, near, send_ref, d, u0, b1, u1, scr):
+    d[:, 8:16, :] = wide[16:48]
+
+    def place(e_row, o_row):
+        d[:, e_row : e_row + 8, :] = e[16:48]
+        d[:, o_row : o_row + 8, :] = near[...]
+
+    beside(pos_ref, place, 8)
     clear(u0, 0, 31)
     first_sweep(u0, d, row_parity(24, 1), 1, 1.0, 1, 31)
-    clear(scr, 0, 1)
+    clear(scr, *range(RESTRICT))
     clear(b1, 0, 15)
     clear(u1, 0, 15)
     restrict_to(b1, u0, d, 0.0, 24, 1, 1.0, 1, 15, scr, 16)
@@ -270,34 +275,39 @@
     return [residual_of(values, x + 1, d[24 + x, 16:40, :] - shift, 1, 1.0)[8:16] for x in range(CX)]
 
 
-def wide_kernel(pos_ref, wide, e, o, s, t, d, u0, b1, u1, scr):
+def mid_kernel(pos_ref, ag, wide, e, near, o, s, t, send_ref, d, u0n, b1n, u1n, stat_ref, u0, b1, u1, v1, pw, b2, u2, b3, u3, scr):
+    total = jnp.sum(jnp.sum(ag[...], axis=0))
+    mean = total * (1.0 / COARSE_CELLS)
     for i in range(16):
         d[i] = jnp.zeros((W0Y, NZ), jnp.float32)
         d[48 + i] = jnp.zeros((W0Y, NZ), jnp.float32)
-    join_rows(d, pos_ref, wide, e, o, 0, 64, 24)
+    d[:, 24:32, :] = wide[...]
+
+    def place_first(e_row, o_row):
+        d[:, e_row : e_row + 8, :] = e[...]
+        d[0:16, o_row : o_row + 8, :] = o[0:16]
+        d[16:48, o_row : o_row + 8, :] = near[...]
+        d[48:64, o_row : o_row + 8, :] = o[16:32]
+
+    def place_second(s_row, o_row):
+        d[8:56, s_row : s_row + 8, :] = s[0:48]
+        d[8:56, o_row : o_row + 8, :] = o[32:80]
+
+    def place_third(s_row, t_row):
+        d[16:48, s_row : s_row + 8, :] = s[48:80]
+        d[16:48, t_row : t_row + 8, :] = t[...]
+
     even = (pos_ref[1] & 1) == 0
-
-    def place(o_row, s_row, s_far, t_row):
-        d[8:56, o_row : o_row + 8, :] = o[64:112]
-        d[8:56, s_row : s_row + 8, :] = s[0:48]
-        d[16:48, s_far : s_far + 8, :] = s[48:80]
-        d[16:48, t_row : t_row + 8, :] = t[...]
-
-    pl.when(even)(functools.partial(place, 8, 40, 48, 0))
-    pl.when(jnp.logical_not(even))(functools.partial(place, 40, 8, 0, 48))
+    for offset, place in ((8, place_first), (16, place_second), (24, place_third)):
+        pl.when(even)(functools.partial(place, 24 + offset, 24 - offset))
+        pl.when(jnp.logical_not(even))(functools.partial(place, 24 - offset, 24 + offset))
     clear(u0, 0, W0X - 1)
     first_sweep(u0, d, row_parity(W0Y, 1), 1, 1.0, 1, W0X - 1)
-    clear(scr, 0, 1)
+    clear(scr, *range(8))
     clear(b1, 0, W1X - 1)
     clear(u1, 0, W1X - 1)
     restrict_to(b1, u0, d, 0.0, W0Y, 1, 1.0, 1, W1X - 1, scr, W1Y)
     first_sweep(u1, b1, row_parity(W1Y, 2), 2, 4.0, 1, W1X - 1)
-
-
-def mid_kernel(pos_ref, ag, d, u0, b1, u1, send_ref, u0n, b1n, u1n, stat_ref, v1, pw, b2, u2, b3, u3, scr):
-    total = jnp.sum(jnp.sum(ag[...], axis=0))
-    mean = total * (1.0 / COARSE_CELLS)
-    clear(scr, 2, 3)
     coarse_solve(pos_ref, ag, mean, pw, b2, u2, b3, u3, scr)
     up_level1(v1, u1, b1, mean, u2, scr, 0, W1X, 0, W1Y)
     up_level0(u0n, u0, d, mean, mean * (1.0 / 3.0), v1, scr, 8, 56, 8, 40)
@@ -306,7 +316,7 @@
     par0 = row_parity(40, 1)
     for colour in (0, 1):
         half_sweep(u0n, d, mean, par0, colour, 1, 1.0, 10, 54, 8)
-    clear(scr, 0, 1)
+    clear(scr, *range(RESTRICT))
     clear(b1n, *range(6), *range(26, W1X))
     restrict_to(b1n, u0n, d, mean, 40, 1, 1.0, 6, 26, scr, W1Y, 8)
     clear(u1n, 0, W1X - 1)
@@ -349,11 +359,11 @@
     return pltpu.VMEM(shape, jnp.float32)
 
 
-COARSE_SCRATCH = (vmem(9, W2Y, NZ), vmem(W2X, W2Y, NZ), vmem(W2X, W2Y, NZ), vmem(W3X, W3Y, NZ), vmem(W3X, W3Y, NZ), vmem(4, 64, NZ))
+COARSE_SCRATCH = (vmem(9, W2Y, NZ), vmem(W2X, W2Y, NZ), vmem(W2X, W2Y, NZ), vmem(W3X, W3Y, NZ), vmem(W3X, W3Y, NZ), vmem(8, 64, NZ))
 LEVELS_OUT = (kept(W0X, W0Y, NZ), kept(W1X, W1Y, NZ), kept(W1X, W1Y, NZ))
 
 
-def call(kernel, outs, scratch, *args, pos=None, cost=None):
+def call(kernel, outs, scratch, *args, pos=None):
     whole = pl.BlockSpec(memory_space=VMEM)
     specs = [whole] * len(args)
     args = tuple(resident(a) for a in args)
@@ -366,7 +376,6 @@
         in_specs=specs,
         out_specs=jax.tree.map(lambda _: whole, outs),
         scratch_shapes=list(scratch),
-        cost_estimate=cost and pl.CostEstimate(flops=cost, transcendentals=0, bytes_accessed=0),
         compiler_params=pltpu.CompilerParams(vmem_limit_bytes=24 * 1024 * 1024),
     )(*args)
 
@@ -415,25 +424,25 @@
     density = call(deposit_kernel, kept(128, 128), (), cells, masses).reshape(CX, CY, NZ)
     wide = x_window(density)
     e = swap(wide, GY, 1, even)
-    t = swap(wide[16:48], GY, 3, odd)
-    o = swap(jnp.concatenate([wide, e[8:56]]), GY, 1, odd)
-    s = swap(jnp.concatenate([e[8:56], wide[16:48]]), GY, 3, even)
+    near = swap(wide[16:48], GY, 1, odd)
+    outer = jnp.concatenate([wide[:16], wide[48:], e[8:56]])
+    reach = jnp.concatenate([e[8:56], wide[16:48]])
     send = call(
         send_kernel,
         kept(16, 2, NZ),
-        (vmem(32, 24, NZ), vmem(32, 24, NZ), vmem(16, 16, NZ), vmem(16, 16, NZ), vmem(4, 64, NZ)),
-        wide, e, o,
+        (vmem(32, 24, NZ), vmem(32, 24, NZ), vmem(16, 16, NZ), vmem(16, 16, NZ), vmem(8, 64, NZ)),
+        wide, e, near,
         pos=pos,
     )
     got = gather_all(send).reshape(512, 2, NZ)
-    d, u0, b1, u1 = call(
-        wide_kernel, (kept(W0X, W0Y, NZ), *LEVELS_OUT), (vmem(4, 64, NZ),), wide, e, o, s, t, pos=pos, cost=20_000_000
-    )
-    send, u0, b1, u1, stat = call(
+    o = swap(outer, GY, 1, odd)
+    s = swap(reach, GY, 3, even)
+    t = swap(wide[16:48], GY, 3, odd)
+    send, d, u0, b1, u1, stat = call(
         mid_kernel,
-        (kept(16, 2, NZ), *LEVELS_OUT, kept(16, NZ)),
-        (vmem(W1X, W1Y, NZ), *COARSE_SCRATCH),
-        got, d, u0, b1, u1,
+        (kept(16, 2, NZ), kept(W0X, W0Y, NZ), *LEVELS_OUT, kept(16, NZ)),
+        (vmem(W0X, W0Y, NZ), vmem(W1X, W1Y, NZ), vmem(W1X, W1Y, NZ), vmem(W1X, W1Y, NZ), *COARSE_SCRATCH),
+        got, wide, e, near, o, s, t,
         pos=pos,
     )
     got = gather_all(send).reshape(512, 2, NZ)

time: 232 us -> 209 us (0.901)
  waiting for transfers between devices: 33.1 us -> 15 us
  starting transfers between devices: 51 us -> 63.2 us
  Pallas kernels: 49.3 us -> 40.4 us
  local copies, waits for them, and re-layouts: 9.64 us -> 3.2 us
    ppermute x7 -> x8, waiting for transfers between devices: 33.1 us -> 15 us  [swap(): return lax.ppermute(x, axis, pairs(lax.axis_size(axis), step, chosen))]
    ppermute x7 -> x8, starting transfers between devices: 44 us -> 55.7 us  [swap(): return lax.ppermute(x, axis, pairs(lax.axis_size(axis), step, chosen))]
    pallas_call x5 -> x4, Pallas kernels: 49.3 us -> 40.4 us  [call(): pl.pallas_call(kernel, out_shape=outs, in_specs=specs, out_specs=jax.tree...]
    unnamed x16 -> x4, local copies, waits for them, and re-layouts: 8.35 us -> 1.89 us
    all_to_all x2, blocking collectives: 40.1 us -> 37.8 us  [gather_all(): ring = lax.all_to_all(block, Z_RING, 0, 0)]
  transfers between devices with their start and end apart: 8 -> 9, of which waited for: 5 -> 5; matrix products, arithmetic and copies ran while one was open for 0% -> 0% of each run, Pallas kernels for 3% -> 0%
where the time goes in v4:
time: 209 us; the launch traced here: 208 us
  blocking collectives  84.7 us (41%)
  starting transfers between devices  63.2 us (30%)
  Pallas kernels  40.4 us (19%)
  waiting for transfers between devices  15 us (7%)
  local copies, waits for them, and re-layouts  3.2 us (2%)
    ppermute x8, starting transfers between devices, swap(): return lax.ppermute(x, axis, pairs(lax.axis_size(axis), step, chosen))  55.7 us
    pallas_call x4, Pallas kernels, call(): pl.pallas_call(kernel, out_shape=outs, in_specs=specs, out_specs=jax.tree...  40.4 us
    all_to_all x2, blocking collectives, gather_all(): ring = lax.all_to_all(block, Z_RING, 0, 0)  37.8 us
    all_to_all x1, blocking collectives, gather_all(): return lax.all_to_all(copies, PLANE, 0, 0)  20.9 us
    ppermute x8, waiting for transfers between devices, swap(): return lax.ppermute(x, axis, pairs(lax.axis_size(axis), step, chosen))  15 us
    all_to_all x1, blocking collectives, per_device(): ring = jnp.sum(lax.all_to_all(sums, Z_RING, 0, 0), axis=0)  13.9 us
    all_to_all x1, blocking collectives, per_device(): lax.all_to_all(jnp.broadcast_to(ring[None], (32, 1, NZ)), PLANE, 0, 0)  12.2 us
    all_to_all x1, starting transfers between devices, gather_all(): return lax.all_to_all(copies, PLANE, 0, 0)  7.53 us
  transfers between devices with their start and end apart: 9, of which 5 were waited for; matrix products, arithmetic and copies ran while one was open for 0% of the time, Pallas kernels for 0%

profile of v4, /device:TPU:1, one launch (start us, length us, event | category | flops | bytes accessed | tf_op | source)
XLA Modules:
  0.0 208.0 jit_solution(7017717988579157793)
XLA Ops:
  0.6 0.0 copy-start
  0.6 0.9 copy-done
  1.6 0.0 copy-start.1
  1.6 0.9 copy-done.1
  2.5 13.9 %shard_map.49 = f32[128,128]{1,0:T(8,128)S(1)} custom-call(s32[512,128]{1,0:T(8,128)S(1)} %bitcast.10, f32[512,128]{1,0:T(8,128)S(1)} %bitcast.11), custom_call_target="tpu_custom_call" | custom-call | tf_op jit(solution)/shard_map/pallas_call | solution.py:373
  16.4 8.7 %collective-permute-start = (f32[16,8,128]{2,1,0:T(8,128)S(1)}, f32[16,8,128]{2,1,0:T(8,128)S(1)}, u32[]{:S(2)}, u32[]{:S(2)}) collective-permute-start(f32[16,8,128]{2,1,0:T(8,128)S(1)} %bitcast.12), channel_id=1, source_target_pairs={{0,32},{32,0},{64,96},{96,64},{128,160},{160,128},{192,224},{224,1... | collective-permute-start | bytes 196616 | tf_op jit(solution)/shard_map/ppermute | solution.py:392
  25.2 0.9 collective-permute-done
  26.1 1.9 collective-permute-start.1
  28.0 13.2 %collective-permute-start.2 = (f32[8,8,128]{2,1,0:T(8,128)S(1)}, f32[8,8,128]{2,1,0:T(8,128)S(1)}, u32[]{:S(2)}, u32[]{:S(2)}) collective-permute-start(f32[8,8,128]{2,1,0:T(8,128)S(1)} %slice_select_fusion.1), channel_id=1, source_target_pairs={{0,96},{96,0},{64,160},{160,64},{128,224},{224,128},{192,288},{288... | collective-permute-start | bytes 98312 | tf_op jit(solution)/shard_map/ppermute | solution.py:392
  41.2 2.9 %collective-permute-done.2 = f32[8,8,128]{2,1,0:T(8,128)S(1)} collective-permute-done((f32[8,8,128]{2,1,0:T(8,128)S(1)}, f32[8,8,128]{2,1,0:T(8,128)S(1)}, u32[]{:S(2)}, u32[]{:S(2)}) %collective-permute-start.2) | collective-permute-done | bytes 32800 | tf_op jit(solution)/shard_map/ppermute | solution.py:392
  44.1 0.0 collective-permute-done.1
  44.1 2.0 collective-permute-start.3
  46.2 13.8 %collective-permute-start.4 = (f32[32,8,128]{2,1,0:T(8,128)S(1)}, f32[32,8,128]{2,1,0:T(8,128)S(1)}, u32[]{:S(2)}, u32[]{:S(2)}) collective-permute-start(f32[32,8,128]{2,1,0:T(8,128)S(1)} %slice.43), channel_id=1, source_target_pairs={{1,2},{2,1},{3,4},{4,3},{5,6},{6,5},{7,8},{8,7},{9,10},{10,9},{11,... | collective-permute-start | bytes 393224 | tf_op jit(solution)/shard_map/ppermute | solution.py:392
  60.0 0.1 pad_add_fusion.pos_ref
  60.0 3.6 %collective-permute-done.4.near = f32[32,8,128]{2,1,0:T(8,128)S(1)} collective-permute-done((f32[32,8,128]{2,1,0:T(8,128)S(1)}, f32[32,8,128]{2,1,0:T(8,128)S(1)}, u32[]{:S(2)}, u32[]{:S(2)}) %collective-permute-start.4) | collective-permute-done | bytes 131104 | tf_op jit(solution)/shard_map/ppermute | solution.py:392
  63.6 0.0 collective-permute-done.3.e
  63.6 2.0 shard_map.50
  65.7 20.7 %all_to_all.30 = f32[16,2,128]{2,1,0:T(2,128)S(1)} all-to-all(f32[16,2,128]{2,1,0:T(2,128)S(1)} %shard_map.50), channel_id=1, replica_groups=mesh['gx_0'=2,'gx_1'=4,'gx_2'=2,'gy_0'=8,'gy_1'=4] {'gx_0','gy_0'}, dimensions={0} | all-to-all | bytes 32768 | tf_op jit(solution)/shard_map/all_to_all | solution.py:404
  86.4 1.0 broadcast_in_dim.6
  87.4 7.5 %all-to-all-start.1 = ((f32[32,16,2,128]{3,2,1,0:T(2,128)}), f32[32,16,2,128]{3,2,1,0:T(2,128)S(1)}, u32[]{:S(2)}, u32[]{:S(2)}) async-start(f32[32,16,2,128]{3,2,1,0:T(2,128)} %broadcast_in_dim.6), calls=%async_computation.1 | async-start | bytes 1048576 | tf_op jit(solution)/shard_map/all_to_all | solution.py:406
  95.1 4.5 %collective-permute-start.6 = (f32[80,8,128]{2,1,0:T(8,128)S(1)}, f32[80,8,128]{2,1,0:T(8,128)S(1)}, u32[]{:S(2)}, u32[]{:S(2)}) collective-permute-start(f32[80,8,128]{2,1,0:T(8,128)S(1)} %get-tuple-element.23), channel_id=1, source_target_pairs={{0,3},{3,0},{2,5},{5,2},{4,7},{7,4},{6,9},{9,6},{8,11},{11,8},{10,... | collective-permute-start | bytes 983048 | tf_op jit(solution)/shard_map/ppermute | solution.py:392
  99.6 2.2 %collective-permute-start.5 = (f32[80,8,128]{2,1,0:T(8,128)S(1)}, f32[80,8,128]{2,1,0:T(8,128)S(1)}, u32[]{:S(2)}, u32[]{:S(2)}) collective-permute-start(f32[80,8,128]{2,1,0:T(8,128)S(1)} %get-tuple-element.24), channel_id=1, source_target_pairs={{1,2},{2,1},{3,4},{4,3},{5,6},{6,5},{7,8},{8,7},{9,10},{10,9},{11,... | collective-permute-start | bytes 983048 | tf_op jit(solution)/shard_map/ppermute | solution.py:392
  101.8 9.4 %collective-permute-start.7 = (f32[32,8,128]{2,1,0:T(8,128)S(1)}, f32[32,8,128]{2,1,0:T(8,128)S(1)}, u32[]{:S(2)}, u32[]{:S(2)}) collective-permute-start(f32[32,8,128]{2,1,0:T(8,128)S(1)} %slice.43), channel_id=1, source_target_pairs={{1,4},{4,1},{3,6},{6,3},{5,8},{8,5},{7,10},{10,7},{9,12},{12,9},{1... | collective-permute-start | bytes 393224 | tf_op jit(solution)/shard_map/ppermute | solution.py:392
  111.1 4.3 %collective-permute-done.7.t = f32[32,8,128]{2,1,0:T(8,128)S(1)} collective-permute-done((f32[32,8,128]{2,1,0:T(8,128)S(1)}, f32[32,8,128]{2,1,0:T(8,128)S(1)}, u32[]{:S(2)}, u32[]{:S(2)}) %collective-permute-start.7) | collective-permute-done | bytes 131104 | tf_op jit(solution)/shard_map/ppermute | solution.py:392
  115.4 0.0 collective-permute-done.6.s
  115.4 3.3 %collective-permute-done.5.o = f32[80,8,128]{2,1,0:T(8,128)S(1)} collective-permute-done((f32[80,8,128]{2,1,0:T(8,128)S(1)}, f32[80,8,128]{2,1,0:T(8,128)S(1)}, u32[]{:S(2)}, u32[]{:S(2)}) %collective-permute-start.5) | collective-permute-done | bytes 327712 | tf_op jit(solution)/shard_map/ppermute | solution.py:392
  118.8 0.0 all-to-all-done.1
  118.8 17.9 %shard_map.51 = (f32[16,2,128]{2,1,0:T(2,128)S(1)}, f32[64,56,128]{2,1,0:T(8,128)S(1)}, f32[64,56,128]{2,1,0:T(8,128)S(1)}, f32[32,32,128]{2,1,0:T(8,128)S(1)}, ...) custom-call(s32[2]{0:T(128)S(1)} %pad_add_fusion.pos_ref, f32[512,2,128]{2,1,0:T(2,128)S(1)} %bitcast.8, ...), custom_call_target="tpu_custom_call" | custom-call | tf_op jit(solution)/shard_map/pallas_call | solution.py:373
  136.7 17.0 %all_to_all.31 = f32[16,2,128]{2,1,0:T(2,128)S(1)} all-to-all(f32[16,2,128]{2,1,0:T(2,128)S(1)} %get-tuple-element.12), channel_id=1, replica_groups=mesh['gx_0'=2,'gx_1'=4,'gx_2'=2,'gy_0'=8,'gy_1'=4] {'gx_0','gy_0'}, dimensions={0} | all-to-all | bytes 32768 | tf_op jit(solution)/shard_map/all_to_all | solution.py:404
  153.7 0.2 broadcast_in_dim.7
  154.0 20.9 %all_to_all.32 = f32[32,16,2,128]{3,2,1,0:T(2,128)S(1)} all-to-all(f32[32,16,2,128]{3,2,1,0:T(2,128)S(1)} %broadcast_in_dim.7), channel_id=1, replica_groups=mesh['gx_0'=2,'gx_1'=4,'gx_2'=2,'gy_0'=8,'gy_1'=4] {'gx_1','gx_2','gy_1'}, dimensions={0} | all-to-all | bytes 1048576 | tf_op jit(solution)/shard_map/all_to_all | solution.py:406
  174.8 6.6 %shard_map.52 = (f32[16,8,128]{2,1,0:T(8,128)}, f32[16,8,128]{2,1,0:T(8,128)}, f32[16,1,128]{2,1,0:T(1,128)S(1)}) custom-call(s32[2]{0:T(128)S(1)} %pad_add_fusion.pos_ref, f32[512,2,128]{2,1,0:T(2,128)S(1)} %bitcast.9, f32[64,56,128]{2,1,0:T(8,128)S(1)} %get-tuple-element.13.d, f32[64,56,128]{2,1,0:T(8,128)S(1)} %get-tuple-element.14.u0, ...), custom_call_target="tpu_custom_call" | custom-call | tf_op jit(solution)/shard_map/pallas_call | solution.py:373
  181.4 13.9 %all_to_all.33 = f32[16,1,128]{2,1,0:T(1,128)S(1)} all-to-all(f32[16,1,128]{2,1,0:T(1,128)S(1)} %get-tuple-element.20), channel_id=1, replica_groups=mesh['gx_0'=2,'gx_1'=4,'gx_2'=2,'gy_0'=8,'gy_1'=4] {'gx_0','gy_0'}, dimensions={0} | all-to-all | bytes 16384 | tf_op jit(solution)/shard_map/all_to_all | solution.py:456
  195.3 12.2 %all_to_all.34 = f32[32,1,128]{2,1,0:T(1,128)S(1)} all-to-all(f32[32,1,128]{2,1,0:T(1,128)S(1)} %broadcast_in_dim.8), channel_id=1, replica_groups=mesh['gx_0'=2,'gx_1'=4,'gx_2'=2,'gy_0'=8,'gy_1'=4] {'gx_1','gx_2','gy_1'}, dimensions={0} | all-to-all | bytes 32768 | tf_op jit(solution)/shard_map/all_to_all | solution.py:457
  207.5 0.5 add_sqrt_fusion
  (11 shorter events, 0.2 us)
Async XLA Ops:
  0.6 1.0 copy-start
  1.6 0.9 copy-start.1
  16.4 9.6 %collective-permute-start = (f32[16,8,128]{2,1,0:T(8,128)S(1)}, f32[16,8,128]{2,1,0:T(8,128)S(1)}, u32[]{:S(2)}, u32[]{:S(2)}) collective-permute-start(f32[16,8,128]{2,1,0:T(8,128)S(1)} %bitcast.12), channel_id=1, source_target_pairs={{0,32},{32,0},{64,96},{96,64},{128,160},{160,128},{192,224},{224,1... | collective-permute-start | bytes 196616 | tf_op jit(solution)/shard_map/ppermute | solution.py:392
  26.1 18.0 %collective-permute-start.1 = (f32[24,8,128]{2,1,0:T(8,128)S(1)}, f32[24,8,128]{2,1,0:T(8,128)S(1)}, u32[]{:S(2)}, u32[]{:S(2)}) collective-permute-start(f32[24,8,128]{2,1,0:T(8,128)S(1)} %slice_select_fusion), channel_id=1, source_target_pairs={{32,64},{64,32},{96,128},{128,96},{160,192},{192,160},{224,256},{2... | collective-permute-start | bytes 294920 | tf_op jit(solution)/shard_map/ppermute | solution.py:392
  28.0 16.1 %collective-permute-start.2 = (f32[8,8,128]{2,1,0:T(8,128)S(1)}, f32[8,8,128]{2,1,0:T(8,128)S(1)}, u32[]{:S(2)}, u32[]{:S(2)}) collective-permute-start(f32[8,8,128]{2,1,0:T(8,128)S(1)} %slice_select_fusion.1), channel_id=1, source_target_pairs={{0,96},{96,0},{64,160},{160,64},{128,224},{224,128},{192,288},{288... | collective-permute-start | bytes 98312 | tf_op jit(solution)/shard_map/ppermute | solution.py:392
  44.1 19.5 %collective-permute-start.3 = (f32[64,8,128]{2,1,0:T(8,128)S(1)}, f32[64,8,128]{2,1,0:T(8,128)S(1)}, u32[]{:S(2)}, u32[]{:S(2)}) collective-permute-start(f32[64,8,128]{2,1,0:T(8,128)S(1)} %maximum_select_fusion.wide), channel_id=1, source_target_pairs={{0,1},{1,0},{2,3},{3,2},{4,5},{5,4},{6,7},{7,6},{8,9},{9,8},{10,11... | collective-permute-start | bytes 786440 | tf_op jit(solution)/shard_map/ppermute | solution.py:392
  46.2 17.5 %collective-permute-start.4 = (f32[32,8,128]{2,1,0:T(8,128)S(1)}, f32[32,8,128]{2,1,0:T(8,128)S(1)}, u32[]{:S(2)}, u32[]{:S(2)}) collective-permute-start(f32[32,8,128]{2,1,0:T(8,128)S(1)} %slice.43), channel_id=1, source_target_pairs={{1,2},{2,1},{3,4},{4,3},{5,6},{6,5},{7,8},{8,7},{9,10},{10,9},{11,... | collective-permute-start | bytes 393224 | tf_op jit(solution)/shard_map/ppermute | solution.py:392
  87.4 31.3 %all-to-all-start.1 = ((f32[32,16,2,128]{3,2,1,0:T(2,128)}), f32[32,16,2,128]{3,2,1,0:T(2,128)S(1)}, u32[]{:S(2)}, u32[]{:S(2)}) async-start(f32[32,16,2,128]{3,2,1,0:T(2,128)} %broadcast_in_dim.6), calls=%async_computation.1 | async-start | bytes 1048576 | tf_op jit(solution)/shard_map/all_to_all | solution.py:406
  95.1 20.4 %collective-permute-start.6 = (f32[80,8,128]{2,1,0:T(8,128)S(1)}, f32[80,8,128]{2,1,0:T(8,128)S(1)}, u32[]{:S(2)}, u32[]{:S(2)}) collective-permute-start(f32[80,8,128]{2,1,0:T(8,128)S(1)} %get-tuple-element.23), channel_id=1, source_target_pairs={{0,3},{3,0},{2,5},{5,2},{4,7},{7,4},{6,9},{9,6},{8,11},{11,8},{10,... | collective-permute-start | bytes 983048 | tf_op jit(solution)/shard_map/ppermute | solution.py:392
  99.6 19.2 %collective-permute-start.5 = (f32[80,8,128]{2,1,0:T(8,128)S(1)}, f32[80,8,128]{2,1,0:T(8,128)S(1)}, u32[]{:S(2)}, u32[]{:S(2)}) collective-permute-start(f32[80,8,128]{2,1,0:T(8,128)S(1)} %get-tuple-element.24), channel_id=1, source_target_pairs={{1,2},{2,1},{3,4},{4,3},{5,6},{6,5},{7,8},{8,7},{9,10},{10,9},{11,... | collective-permute-start | bytes 983048 | tf_op jit(solution)/shard_map/ppermute | solution.py:392
  101.8 13.7 %collective-permute-start.7 = (f32[32,8,128]{2,1,0:T(8,128)S(1)}, f32[32,8,128]{2,1,0:T(8,128)S(1)}, u32[]{:S(2)}, u32[]{:S(2)}) collective-permute-start(f32[32,8,128]{2,1,0:T(8,128)S(1)} %slice.43), channel_id=1, source_target_pairs={{1,4},{4,1},{3,6},{6,3},{5,8},{8,5},{7,10},{10,7},{9,12},{12,9},{1... | collective-permute-start | bytes 393224 | tf_op jit(solution)/shard_map/ppermute | solution.py:392

commit v5 on v4

--- a/solution.py
+++ b/solution.py
@@ -201,7 +201,7 @@
         for ty in range(17):
             y = lax.rem(gy + (ty - 8 + TILES_Y), TILES_Y)
             plane = (x & 7) * 4 + (y & 3)
-            ring = (x >> 3) * 8 + (y >> 2)
+            ring = (y >> 2) * 2 + (x >> 3)
             pw[tx, 2 * ty : 2 * ty + 2, :] = ag[plane * 16 + ring]
     lane = lax.broadcasted_iota(jnp.int32, (W2Y, NZ), 1) & 3
 
@@ -380,16 +380,28 @@
     )(*args)
 
 
-def pairs(count, step, chosen):
+def place_of(tile_x, tile_y):
+    z = (tile_y // 4) * 2 + tile_x // 8
+    return (((z // 8) * 8 + tile_x % 8) * 8 + z % 8) * 4 + tile_y % 4
+
+
+def every_tile():
+    return [(i, j) for i in range(TILES_X) for j in range(TILES_Y)]
+
+
+def move(x, forth):
+    moves = [(i * TILES_Y + j, place_of(i, j)) for i, j in every_tile()]
+    return lax.ppermute(x, GX + GY, moves if forth else [(b, a) for a, b in moves])
+
+
+def swap(x, axis, step, chosen):
     both = []
-    for i in range(count):
-        if chosen(i):
-            both += [(i, (i + step) % count), ((i + step) % count, i)]
-    return both
-
-
-def swap(x, axis, step, chosen):
-    return lax.ppermute(x, axis, pairs(lax.axis_size(axis), step, chosen))
+    for i, j in every_tile():
+        if chosen(i if axis is GX else j):
+            other = ((i + step) % TILES_X, j) if axis is GX else (i, (j + step) % TILES_Y)
+            a, b = place_of(i, j), place_of(*other)
+            both += [(a, b), (b, a)]
+    return lax.ppermute(x, GX + GY, both)
 
 
 def even(i):
@@ -416,13 +428,14 @@
 
 
 def per_device(particle_cell, particle_mass):
-    tile_x = lax.axis_index(GX)
-    tile_y = lax.axis_index(GY)
+    z = lax.axis_index(Z_RING)
+    tile_x = (z % 2) * 8 + lax.axis_index(("gx_1", "gx_2"))
+    tile_y = (z // 2) * 4 + lax.axis_index("gy_1")
     pos = jnp.stack([tile_x, tile_y]).astype(jnp.int32)
     cells = particle_cell.reshape(512, 128)
     masses = particle_mass.reshape(512, 128)
     density = call(deposit_kernel, kept(128, 128), (), cells, masses).reshape(CX, CY, NZ)
-    wide = x_window(density)
+    wide = x_window(move(density, True))
     e = swap(wide, GY, 1, even)
     near = swap(wide[16:48], GY, 1, odd)
     outer = jnp.concatenate([wide[:16], wide[48:], e[8:56]])
@@ -456,7 +469,7 @@
     ring = jnp.sum(lax.all_to_all(sums, Z_RING, 0, 0), axis=0)
     total = jnp.sum(lax.all_to_all(jnp.broadcast_to(ring[None], (32, 1, NZ)), PLANE, 0, 0), axis=(0, 1))
     norms = jnp.sqrt(total[:2] / GRID_CELLS + norm_eps)
-    return potential, residual, norms
+    return move(potential, False), move(residual, False), norms
 
 
 def solution(mesh):

time: 209 us -> 218 us (1.043)
  blocking collectives: 84.7 us -> 67.3 us
  waiting for transfers between devices: 15 us -> 27.2 us
  starting transfers between devices: 63.2 us -> 73.8 us
    all_to_all x1 -> x0, blocking collectives: 12.2 us -> none  [per_device(): lax.all_to_all(jnp.broadcast_to(ring[None], (32, 1, NZ)), PLANE, 0, 0)]
    ppermute x8 -> x11, waiting for transfers between devices: 15 us -> 21.6 us  [the longest x8 21.6 us: swap(): return lax.ppermute(x, GX + GY, both)]
    all_to_all x2, blocking collectives: 37.8 us -> 31.7 us  [gather_all(): ring = lax.all_to_all(block, Z_RING, 0, 0)]
    all_to_all x0 -> x1, waiting for transfers between devices: none -> 5.53 us  [per_device(): lax.all_to_all(jnp.broadcast_to(ring[None], (32, 1, NZ)), PLANE, 0, 0)]
    all_to_all x0 -> x1, starting transfers between devices: none -> 5.42 us  [per_device(): lax.all_to_all(jnp.broadcast_to(ring[None], (32, 1, NZ)), PLANE, 0, 0)]
    ppermute x8 -> x11, starting transfers between devices: 55.7 us -> 59.3 us  [the longest x8 57.3 us: swap(): return lax.ppermute(x, GX + GY, both)]
  transfers between devices with their start and end apart: 9 -> 13, of which waited for: 5 -> 5; matrix products, arithmetic and copies ran while one was open for 0% -> 0% of each run, Pallas kernels for 0% -> 0%
where the time goes in v5:
time: 218 us; the launch traced here: 215 us
  starting transfers between devices  73.8 us (34%)
  blocking collectives  67.3 us (31%)
  Pallas kernels  39.9 us (18%)
  waiting for transfers between devices  27.2 us (12%)
  local copies, waits for them, and re-layouts  5.06 us (2%)
    ppermute x8, starting transfers between devices, swap(): return lax.ppermute(x, GX + GY, both)  57.3 us
    pallas_call x4, Pallas kernels, call(): pl.pallas_call(kernel, out_shape=outs, in_specs=specs, out_specs=jax.tree...  39.9 us
    all_to_all x2, blocking collectives, gather_all(): ring = lax.all_to_all(block, Z_RING, 0, 0)  31.7 us
    all_to_all x1, blocking collectives, gather_all(): return lax.all_to_all(copies, PLANE, 0, 0)  21.8 us
    ppermute x8, waiting for transfers between devices, swap(): return lax.ppermute(x, GX + GY, both)  21.6 us
    all_to_all x1, blocking collectives, per_device(): ring = jnp.sum(lax.all_to_all(sums, Z_RING, 0, 0), axis=0)  13.9 us
    all_to_all x1, starting transfers between devices, gather_all(): return lax.all_to_all(copies, PLANE, 0, 0)  9.12 us
    all_to_all x1, waiting for transfers between devices, per_device(): lax.all_to_all(jnp.broadcast_to(ring[None], (32, 1, NZ)), PLANE, 0, 0)  5.53 us
  transfers between devices with their start and end apart: 13, of which 5 were waited for; matrix products, arithmetic and copies ran while one was open for 0% of the time, Pallas kernels for 0%

profile of v5, /device:TPU:1, one launch (start us, length us, event | category | flops | bytes accessed | tf_op | source)
XLA Modules:
  0.0 214.9 jit_solution(16713163566706269084)
XLA Ops:
  0.6 0.0 copy-start
  0.6 0.9 copy-done
  1.6 0.0 copy-start.1
  1.6 0.9 copy-done.1
  2.5 13.9 %shard_map.49 = f32[128,128]{1,0:T(8,128)S(1)} custom-call(s32[512,128]{1,0:T(8,128)S(1)} %bitcast.10, f32[512,128]{1,0:T(8,128)S(1)} %bitcast.11), custom_call_target="tpu_custom_call" | custom-call | tf_op jit(solution)/shard_map/pallas_call | solution.py:373
  16.4 0.7 collective-permute-start
  17.1 0.0 collective-permute-done
  17.1 8.7 %collective-permute-start.1 = (f32[16,8,128]{2,1,0:T(8,128)S(1)}, f32[16,8,128]{2,1,0:T(8,128)S(1)}, u32[]{:S(2)}, u32[]{:S(2)}) collective-permute-start(f32[16,8,128]{2,1,0:T(8,128)S(1)} %collective-permute-done), channel_id=1, source_target_pairs={{0,32},{32,0},{1,33},{33,1},{2,34},{34,2},{3,35},{35,3},{8,40},{40... | collective-permute-start | bytes 196616 | tf_op jit(solution)/shard_map/ppermute | solution.py:404
  25.9 0.9 collective-permute-done.1
  26.8 1.9 collective-permute-start.2
  28.7 21.3 %collective-permute-start.3 = (f32[8,8,128]{2,1,0:T(8,128)S(1)}, f32[8,8,128]{2,1,0:T(8,128)S(1)}, u32[]{:S(2)}, u32[]{:S(2)}) collective-permute-start(f32[8,8,128]{2,1,0:T(8,128)S(1)} %slice_select_fusion.1), channel_id=1, source_target_pairs={{0,96},{96,0},{1,97},{97,1},{2,98},{98,2},{3,99},{99,3},{8,104},{1... | collective-permute-start | bytes 98312 | tf_op jit(solution)/shard_map/ppermute | solution.py:404
  50.1 1.6 collective-permute-done.3
  51.7 0.0 collective-permute-done.2
  51.7 3.1 %collective-permute-start.4 = (f32[64,8,128]{2,1,0:T(8,128)S(1)}, f32[64,8,128]{2,1,0:T(8,128)S(1)}, u32[]{:S(2)}, u32[]{:S(2)}) collective-permute-start(f32[64,8,128]{2,1,0:T(8,128)S(1)} %maximum_select_fusion.wide), channel_id=1, source_target_pairs={{0,1},{1,0},{2,3},{3,2},{8,9},{9,8},{10,11},{11,10},{16,17},{17,16... | collective-permute-start | bytes 786440 | tf_op jit(solution)/shard_map/ppermute | solution.py:404
  54.8 10.6 %collective-permute-start.5 = (f32[32,8,128]{2,1,0:T(8,128)S(1)}, f32[32,8,128]{2,1,0:T(8,128)S(1)}, u32[]{:S(2)}, u32[]{:S(2)}) collective-permute-start(f32[32,8,128]{2,1,0:T(8,128)S(1)} %slice.43), channel_id=1, source_target_pairs={{1,2},{2,1},{3,8},{8,3},{9,10},{10,9},{11,16},{16,11},{17,18},{18,... | collective-permute-start | bytes 393224 | tf_op jit(solution)/shard_map/ppermute | solution.py:404
  65.5 0.1 pad_add_fusion.pos_ref
  65.6 4.9 %collective-permute-done.5.near = f32[32,8,128]{2,1,0:T(8,128)S(1)} collective-permute-done((f32[32,8,128]{2,1,0:T(8,128)S(1)}, f32[32,8,128]{2,1,0:T(8,128)S(1)}, u32[]{:S(2)}, u32[]{:S(2)}) %collective-permute-start.5) | collective-permute-done | bytes 131104 | tf_op jit(solution)/shard_map/ppermute | solution.py:404
  70.4 0.0 collective-permute-done.4.e
  70.4 2.0 shard_map.50
  72.5 14.4 %all_to_all.30 = f32[16,2,128]{2,1,0:T(2,128)S(1)} all-to-all(f32[16,2,128]{2,1,0:T(2,128)S(1)} %shard_map.50), channel_id=1, replica_groups=mesh['gx_0'=2,'gx_1'=4,'gx_2'=2,'gy_0'=8,'gy_1'=4] {'gx_0','gy_0'}, dimensions={0} | all-to-all | bytes 32768 | tf_op jit(solution)/shard_map/all_to_all | solution.py:416
  86.9 1.0 broadcast_in_dim.6
  87.9 9.1 %all-to-all-start.1 = ((f32[32,16,2,128]{3,2,1,0:T(2,128)}), f32[32,16,2,128]{3,2,1,0:T(2,128)S(1)}, u32[]{:S(2)}, u32[]{:S(2)}) async-start(f32[32,16,2,128]{3,2,1,0:T(2,128)} %broadcast_in_dim.6), calls=%async_computation.1 | async-start | bytes 1048576 | tf_op jit(solution)/shard_map/all_to_all | solution.py:418
  97.2 4.5 %collective-permute-start.7 = (f32[80,8,128]{2,1,0:T(8,128)S(1)}, f32[80,8,128]{2,1,0:T(8,128)S(1)}, u32[]{:S(2)}, u32[]{:S(2)}) collective-permute-start(f32[80,8,128]{2,1,0:T(8,128)S(1)} %get-tuple-element.23), channel_id=1, source_target_pairs={{0,3},{3,0},{2,9},{9,2},{8,11},{11,8},{10,17},{17,10},{16,19},{19,... | collective-permute-start | bytes 983048 | tf_op jit(solution)/shard_map/ppermute | solution.py:404
  101.6 2.2 %collective-permute-start.6 = (f32[80,8,128]{2,1,0:T(8,128)S(1)}, f32[80,8,128]{2,1,0:T(8,128)S(1)}, u32[]{:S(2)}, u32[]{:S(2)}) collective-permute-start(f32[80,8,128]{2,1,0:T(8,128)S(1)} %get-tuple-element.24), channel_id=1, source_target_pairs={{1,2},{2,1},{3,8},{8,3},{9,10},{10,9},{11,16},{16,11},{17,18},{18,... | collective-permute-start | bytes 983048 | tf_op jit(solution)/shard_map/ppermute | solution.py:404
  103.8 4.9 %collective-permute-start.8 = (f32[32,8,128]{2,1,0:T(8,128)S(1)}, f32[32,8,128]{2,1,0:T(8,128)S(1)}, u32[]{:S(2)}, u32[]{:S(2)}) collective-permute-start(f32[32,8,128]{2,1,0:T(8,128)S(1)} %slice.43), channel_id=1, source_target_pairs={{1,8},{8,1},{3,10},{10,3},{9,16},{16,9},{11,18},{18,11},{17,24},{2... | collective-permute-start | bytes 393224 | tf_op jit(solution)/shard_map/ppermute | solution.py:404
  108.7 14.2 %collective-permute-done.8.t = f32[32,8,128]{2,1,0:T(8,128)S(1)} collective-permute-done((f32[32,8,128]{2,1,0:T(8,128)S(1)}, f32[32,8,128]{2,1,0:T(8,128)S(1)}, u32[]{:S(2)}, u32[]{:S(2)}) %collective-permute-start.8) | collective-permute-done | bytes 131104 | tf_op jit(solution)/shard_map/ppermute | solution.py:404
  123.0 0.0 collective-permute-done.7.s
  123.0 0.0 collective-permute-done.6.o
  123.0 0.0 all-to-all-done.1
  123.0 17.9 %shard_map.51 = (f32[16,2,128]{2,1,0:T(2,128)S(1)}, f32[64,56,128]{2,1,0:T(8,128)S(1)}, f32[64,56,128]{2,1,0:T(8,128)S(1)}, f32[32,32,128]{2,1,0:T(8,128)S(1)}, ...) custom-call(s32[2]{0:T(128)S(1)} %pad_add_fusion.pos_ref, f32[512,2,128]{2,1,0:T(2,128)S(1)} %bitcast.8, ...), custom_call_target="tpu_custom_call" | custom-call | tf_op jit(solution)/shard_map/pallas_call | solution.py:373
  140.9 17.3 %all_to_all.31 = f32[16,2,128]{2,1,0:T(2,128)S(1)} all-to-all(f32[16,2,128]{2,1,0:T(2,128)S(1)} %get-tuple-element.12), channel_id=1, replica_groups=mesh['gx_0'=2,'gx_1'=4,'gx_2'=2,'gy_0'=8,'gy_1'=4] {'gx_0','gy_0'}, dimensions={0} | all-to-all | bytes 32768 | tf_op jit(solution)/shard_map/all_to_all | solution.py:416
  158.2 0.2 broadcast_in_dim.7
  158.4 21.8 %all_to_all.32 = f32[32,16,2,128]{3,2,1,0:T(2,128)S(1)} all-to-all(f32[32,16,2,128]{3,2,1,0:T(2,128)S(1)} %broadcast_in_dim.7), channel_id=1, replica_groups=mesh['gx_0'=2,'gx_1'=4,'gx_2'=2,'gy_0'=8,'gy_1'=4] {'gx_1','gx_2','gy_1'}, dimensions={0} | all-to-all | bytes 1048576 | tf_op jit(solution)/shard_map/all_to_all | solution.py:418
  180.2 6.0 %shard_map.52 = (f32[16,8,128]{2,1,0:T(8,128)S(1)}, f32[16,8,128]{2,1,0:T(8,128)S(1)}, f32[16,1,128]{2,1,0:T(1,128)S(1)}) custom-call(s32[2]{0:T(128)S(1)} %pad_add_fusion.pos_ref, f32[512,2,128]{2,1,0:T(2,128)S(1)} %bitcast.9, f32[64,56,128]{2,1,0:T(8,128)S(1)} %get-tuple-element.13.d, f32[64,56,128]{2,1,0:T(8,128)S(1)} %get-tuple-element.14.u0, ...), custom_call_target="tpu_custom_call" | custom-call | tf_op jit(solution)/shard_map/pallas_call | solution.py:373
  186.2 13.9 %all_to_all.33 = f32[16,1,128]{2,1,0:T(1,128)S(1)} all-to-all(f32[16,1,128]{2,1,0:T(1,128)S(1)} %get-tuple-element.20), channel_id=1, replica_groups=mesh['gx_0'=2,'gx_1'=4,'gx_2'=2,'gy_0'=8,'gy_1'=4] {'gx_0','gy_0'}, dimensions={0} | all-to-all | bytes 16384 | tf_op jit(solution)/shard_map/all_to_all | solution.py:469
  200.1 0.6 broadcast_in_dim.8
  200.7 5.4 %all-to-all-start.5 = ((f32[32,1,128]{2,1,0:T(1,128)}), f32[32,1,128]{2,1,0:T(1,128)S(1)}, u32[]{:S(2)}, u32[]{:S(2)}) async-start(f32[32,1,128]{2,1,0:T(1,128)} %broadcast_in_dim.8), calls=%async_computation.5 | async-start | bytes 32768 | tf_op jit(solution)/shard_map/all_to_all | solution.py:470
  206.2 0.7 collective-permute-start.9
  206.8 0.7 collective-permute-start.10
  207.5 5.5 %all-to-all-done.5 = f32[32,1,128]{2,1,0:T(1,128)S(1)} async-done(((f32[32,1,128]{2,1,0:T(1,128)}), f32[32,1,128]{2,1,0:T(1,128)S(1)}, u32[]{:S(2)}, u32[]{:S(2)}) %all-to-all-start.5) | async-done | bytes 16416 | tf_op jit(solution)/shard_map/all_to_all | solution.py:470
  213.1 0.5 add_sqrt_fusion
  213.6 0.0 collective-permute-done.9
  213.6 0.0 collective-permute-done.10
  213.6 0.6 copy.8
  214.2 0.6 copy.9
  (10 shorter events, 0.2 us)
Async XLA Ops:
  0.6 1.0 copy-start
  1.6 0.9 copy-start.1
  16.4 0.7 collective-permute-start
  17.1 9.6 %collective-permute-start.1 = (f32[16,8,128]{2,1,0:T(8,128)S(1)}, f32[16,8,128]{2,1,0:T(8,128)S(1)}, u32[]{:S(2)}, u32[]{:S(2)}) collective-permute-start(f32[16,8,128]{2,1,0:T(8,128)S(1)} %collective-permute-done), channel_id=1, source_target_pairs={{0,32},{32,0},{1,33},{33,1},{2,34},{34,2},{3,35},{35,3},{8,40},{40... | collective-permute-start | bytes 196616 | tf_op jit(solution)/shard_map/ppermute | solution.py:404
  26.8 24.9 %collective-permute-start.2 = (f32[24,8,128]{2,1,0:T(8,128)S(1)}, f32[24,8,128]{2,1,0:T(8,128)S(1)}, u32[]{:S(2)}, u32[]{:S(2)}) collective-permute-start(f32[24,8,128]{2,1,0:T(8,128)S(1)} %slice_select_fusion), channel_id=1, source_target_pairs={{32,64},{64,32},{33,65},{65,33},{34,66},{66,34},{35,67},{67,35},{4... | collective-permute-start | bytes 294920 | tf_op jit(solution)/shard_map/ppermute | solution.py:404
  28.7 22.9 %collective-permute-start.3 = (f32[8,8,128]{2,1,0:T(8,128)S(1)}, f32[8,8,128]{2,1,0:T(8,128)S(1)}, u32[]{:S(2)}, u32[]{:S(2)}) collective-permute-start(f32[8,8,128]{2,1,0:T(8,128)S(1)} %slice_select_fusion.1), channel_id=1, source_target_pairs={{0,96},{96,0},{1,97},{97,1},{2,98},{98,2},{3,99},{99,3},{8,104},{1... | collective-permute-start | bytes 98312 | tf_op jit(solution)/shard_map/ppermute | solution.py:404
  51.7 18.8 %collective-permute-start.4 = (f32[64,8,128]{2,1,0:T(8,128)S(1)}, f32[64,8,128]{2,1,0:T(8,128)S(1)}, u32[]{:S(2)}, u32[]{:S(2)}) collective-permute-start(f32[64,8,128]{2,1,0:T(8,128)S(1)} %maximum_select_fusion.wide), channel_id=1, source_target_pairs={{0,1},{1,0},{2,3},{3,2},{8,9},{9,8},{10,11},{11,10},{16,17},{17,16... | collective-permute-start | bytes 786440 | tf_op jit(solution)/shard_map/ppermute | solution.py:404
  54.8 15.6 %collective-permute-start.5 = (f32[32,8,128]{2,1,0:T(8,128)S(1)}, f32[32,8,128]{2,1,0:T(8,128)S(1)}, u32[]{:S(2)}, u32[]{:S(2)}) collective-permute-start(f32[32,8,128]{2,1,0:T(8,128)S(1)} %slice.43), channel_id=1, source_target_pairs={{1,2},{2,1},{3,8},{8,3},{9,10},{10,9},{11,16},{16,11},{17,18},{18,... | collective-permute-start | bytes 393224 | tf_op jit(solution)/shard_map/ppermute | solution.py:404
  87.9 35.1 %all-to-all-start.1 = ((f32[32,16,2,128]{3,2,1,0:T(2,128)}), f32[32,16,2,128]{3,2,1,0:T(2,128)S(1)}, u32[]{:S(2)}, u32[]{:S(2)}) async-start(f32[32,16,2,128]{3,2,1,0:T(2,128)} %broadcast_in_dim.6), calls=%async_computation.1 | async-start | bytes 1048576 | tf_op jit(solution)/shard_map/all_to_all | solution.py:418
  97.2 25.8 %collective-permute-start.7 = (f32[80,8,128]{2,1,0:T(8,128)S(1)}, f32[80,8,128]{2,1,0:T(8,128)S(1)}, u32[]{:S(2)}, u32[]{:S(2)}) collective-permute-start(f32[80,8,128]{2,1,0:T(8,128)S(1)} %get-tuple-element.23), channel_id=1, source_target_pairs={{0,3},{3,0},{2,9},{9,2},{8,11},{11,8},{10,17},{17,10},{16,19},{19,... | collective-permute-start | bytes 983048 | tf_op jit(solution)/shard_map/ppermute | solution.py:404
  101.6 21.3 %collective-permute-start.6 = (f32[80,8,128]{2,1,0:T(8,128)S(1)}, f32[80,8,128]{2,1,0:T(8,128)S(1)}, u32[]{:S(2)}, u32[]{:S(2)}) collective-permute-start(f32[80,8,128]{2,1,0:T(8,128)S(1)} %get-tuple-element.24), channel_id=1, source_target_pairs={{1,2},{2,1},{3,8},{8,3},{9,10},{10,9},{11,16},{16,11},{17,18},{18,... | collective-permute-start | bytes 983048 | tf_op jit(solution)/shard_map/ppermute | solution.py:404
  103.8 19.2 %collective-permute-start.8 = (f32[32,8,128]{2,1,0:T(8,128)S(1)}, f32[32,8,128]{2,1,0:T(8,128)S(1)}, u32[]{:S(2)}, u32[]{:S(2)}) collective-permute-start(f32[32,8,128]{2,1,0:T(8,128)S(1)} %slice.43), channel_id=1, source_target_pairs={{1,8},{8,1},{3,10},{10,3},{9,16},{16,9},{11,18},{18,11},{17,24},{2... | collective-permute-start | bytes 393224 | tf_op jit(solution)/shard_map/ppermute | solution.py:404
  200.7 12.3 %all-to-all-start.5 = ((f32[32,1,128]{2,1,0:T(1,128)}), f32[32,1,128]{2,1,0:T(1,128)S(1)}, u32[]{:S(2)}, u32[]{:S(2)}) async-start(f32[32,1,128]{2,1,0:T(1,128)} %broadcast_in_dim.8), calls=%async_computation.5 | async-start | bytes 32768 | tf_op jit(solution)/shard_map/all_to_all | solution.py:470
  206.2 7.4 %collective-permute-start.9 = (f32[16,8,128]{2,1,0:T(8,128)S(1)}, f32[16,8,128]{2,1,0:T(8,128)S(1)}, u32[]{:S(2)}, u32[]{:S(2)}) collective-permute-start(f32[16,8,128]{2,1,0:T(8,128)S(1)} %get-tuple-element.18), channel_id=1, source_target_pairs={{0,0},{1,1},{2,2},{3,3},{8,4},{9,5},{10,6},{11,7},{16,8},{17,9},{1... | collective-permute-start | bytes 196616 | tf_op jit(solution)/shard_map/ppermute | solution.py:394
  206.8 6.8 %collective-permute-start.10 = (f32[16,8,128]{2,1,0:T(8,128)S(1)}, f32[16,8,128]{2,1,0:T(8,128)S(1)}, u32[]{:S(2)}, u32[]{:S(2)}) collective-permute-start(f32[16,8,128]{2,1,0:T(8,128)S(1)} %get-tuple-element.19), channel_id=1, source_target_pairs={{0,0},{1,1},{2,2},{3,3},{8,4},{9,5},{10,6},{11,7},{16,8},{17,9},{1... | collective-permute-start | bytes 196616 | tf_op jit(solution)/shard_map/ppermute | solution.py:394

commit v6 on v4

--- a/solution.py
+++ b/solution.py
@@ -27,8 +27,9 @@
 W1X, W1Y = 32, 32
 W2X, W2Y = 36, 40
 W3X, W3Y = 18, 24
-DEPOSIT_ROWS = 32
+DEPOSIT_ROWS = 64
 KEEP = True
+RING = 10
 RESTRICT = 4
 ADD = 4
 SIZES = (6, 8, 10, 16, 16)
@@ -36,23 +37,24 @@
 
 
 def deposit_kernel(cell_ref, mass_ref, out_ref):
-    rows = lax.broadcasted_iota(jnp.int32, (128, 128), 0)
+    rows = lax.broadcasted_iota(jnp.int32, (128, 128), 0).astype(jnp.bfloat16)
     batch = DEPOSIT_ROWS
 
     def step(t, acc):
         cells = cell_ref[pl.ds(pl.multiple_of(t * batch, 8), batch), :]
         masses = mass_ref[pl.ds(pl.multiple_of(t * batch, 8), batch), :]
-        high = cells >> 7
-        low = cells & 127
-        coarse = masses.astype(jnp.bfloat16).astype(jnp.float32)
-        fine = masses - coarse
+        high = (cells >> 7).astype(jnp.bfloat16)
+        low = (cells & 127).astype(jnp.bfloat16)
+        coarse = masses.astype(jnp.bfloat16)
+        fine = (masses - coarse.astype(jnp.float32)).astype(jnp.bfloat16)
+        zero = jnp.zeros((128, 128), jnp.bfloat16)
+        one = jnp.ones((128, 128), jnp.bfloat16)
         left, right = [], []
         for r in range(batch):
-            hit = rows == high[r : r + 1, :]
-            first = jnp.where(hit, coarse[r : r + 1, :], 0.0).astype(jnp.bfloat16)
-            second = jnp.where(hit, fine[r : r + 1, :], 0.0).astype(jnp.bfloat16)
-            left.append(jnp.concatenate([first, second], axis=0))
-            right.append(jnp.where(rows == low[r : r + 1, :], 1.0, 0.0).astype(jnp.bfloat16))
+            line = lambda x: jnp.broadcast_to(x[r : r + 1, :], (128, 128))
+            hit = rows == line(high)
+            left.append(jnp.concatenate([jnp.where(hit, line(coarse), zero), jnp.where(hit, line(fine), zero)], axis=0))
+            right.append(jnp.where(rows == line(low), one, zero))
         left = jnp.concatenate(left, axis=1)
         right = jnp.concatenate(right, axis=1)
         return acc + lax.dot_general(left, right, (((1,), (1,)), ((), ())), preferred_element_type=jnp.float32)
@@ -193,6 +195,15 @@
         ref[i] = jnp.zeros(ref.shape[1:], jnp.float32)
 
 
+def fan_kernel(pos_ref, ring, out):
+    block = lax.shift_right_logical(pos_ref[1], 2)
+    parts = [ring[8 * h + ((block + (j + 6)) & 7)] for h in range(2) for j in range(5)]
+    parts.append(jnp.sum(ring[...], axis=0))
+    for n in range(32):
+        for j in range(RING + 1):
+            out[n, j] = parts[j]
+
+
 def coarse_solve(pos_ref, ag, shift, pw, b2, u2, b3, u3, scr):
     gx, gy = pos_ref[0], pos_ref[1]
     for tx in range(9):
@@ -201,8 +212,8 @@
         for ty in range(17):
             y = lax.rem(gy + (ty - 8 + TILES_Y), TILES_Y)
             plane = (x & 7) * 4 + (y & 3)
-            ring = (x >> 3) * 8 + (y >> 2)
-            pw[tx, 2 * ty : 2 * ty + 2, :] = ag[plane * 16 + ring]
+            ring = (x >> 3) * 5 + (((y >> 2) - (gy >> 2) + 2) & 7)
+            pw[tx, 2 * ty : 2 * ty + 2, :] = ag[plane * (RING + 1) + ring]
     lane = lax.broadcasted_iota(jnp.int32, (W2Y, NZ), 1) & 3
 
     def unpack(first, count):
@@ -276,7 +287,10 @@
 
 
 def mid_kernel(pos_ref, ag, wide, e, near, o, s, t, send_ref, d, u0n, b1n, u1n, stat_ref, u0, b1, u1, v1, pw, b2, u2, b3, u3, scr):
-    total = jnp.sum(jnp.sum(ag[...], axis=0))
+    total = ag[RING]
+    for n in range(1, 32):
+        total = total + ag[n * (RING + 1) + RING]
+    total = jnp.sum(total)
     mean = total * (1.0 / COARSE_CELLS)
     for i in range(16):
         d[i] = jnp.zeros((W0Y, NZ), jnp.float32)
@@ -400,10 +414,10 @@
     return i % 2 == 1
 
 
-def gather_all(block):
-    ring = lax.all_to_all(block, Z_RING, 0, 0)
-    copies = jnp.broadcast_to(ring[None], (32, *ring.shape))
-    return lax.all_to_all(copies, PLANE, 0, 0)
+def gather_all(block, pos):
+    ring = resident(lax.all_to_all(block, Z_RING, 0, 0))
+    copies = call(fan_kernel, kept(32, RING + 1, 2, NZ), (), ring, pos=pos)
+    return lax.all_to_all(copies, PLANE, 0, 0).reshape(32 * (RING + 1), 2, NZ)
 
 
 def x_window(d):
@@ -434,7 +448,7 @@
         wide, e, near,
         pos=pos,
     )
-    got = gather_all(send).reshape(512, 2, NZ)
+    got = gather_all(send, pos)
     o = swap(outer, GY, 1, odd)
     s = swap(reach, GY, 3, even)
     t = swap(wide[16:48], GY, 3, odd)
@@ -445,7 +459,7 @@
         got, wide, e, near, o, s, t,
         pos=pos,
     )
-    got = gather_all(send).reshape(512, 2, NZ)
+    got = gather_all(send, pos)
     potential, residual, sums = call(
         post_kernel,
         (f32(CX, CY, NZ), f32(CX, CY, NZ), kept(16, 1, NZ)),

time: 209 us -> 205 us (0.981)
  blocking collectives: 84.7 us -> 62.2 us
  waiting for transfers between devices: 15 us -> 26.7 us
  starting transfers between devices: 63.2 us -> 72.6 us
    all_to_all x3 -> x2, blocking collectives: 58.7 us -> 36.3 us  [the longest x1 19.3 us: gather_all(): return lax.all_to_all(copies, PLANE, 0, 0).reshape(32 * (RING + 1), 2, NZ)]
    all_to_all x1 -> x2, waiting for transfers between devices: 0.01 us -> 11.7 us  [the longest x1 11.7 us: gather_all(): ring = resident(lax.all_to_all(block, Z_RING, 0, 0))]
    all_to_all x1 -> x2, starting transfers between devices: 7.53 us -> 16.7 us  [the longest x1 8.9 us: gather_all(): ring = resident(lax.all_to_all(block, Z_RING, 0, 0))]
    pallas_call x4 -> x6, Pallas kernels: 40.4 us -> 38.8 us  [call(): pl.pallas_call(kernel, out_shape=outs, in_specs=specs, out_specs=jax.tree...]
  transfers between devices with their start and end apart: 9 -> 10, of which waited for: 5 -> 6; matrix products, arithmetic and copies ran while one was open for 0% -> 0% of each run, Pallas kernels for 0% -> 0%
where the time goes in v6:
time: 205 us; the launch traced here: 204 us
  starting transfers between devices  72.6 us (35%)
  blocking collectives  62.2 us (30%)
  Pallas kernels  38.8 us (19%)
  waiting for transfers between devices  26.7 us (13%)
    ppermute x8, starting transfers between devices, swap(): return lax.ppermute(x, axis, pairs(lax.axis_size(axis), step, chosen))  55.9 us
    pallas_call x6, Pallas kernels, call(): pl.pallas_call(kernel, out_shape=outs, in_specs=specs, out_specs=jax.tree...  38.8 us
    all_to_all x1, blocking collectives, gather_all(): return lax.all_to_all(copies, PLANE, 0, 0).reshape(32 * (RING + 1), 2, NZ)  19.3 us
    all_to_all x1, blocking collectives, gather_all(): ring = resident(lax.all_to_all(block, Z_RING, 0, 0))  17 us
    ppermute x8, waiting for transfers between devices, swap(): return lax.ppermute(x, axis, pairs(lax.axis_size(axis), step, chosen))  15 us
    all_to_all x1, blocking collectives, per_device(): ring = jnp.sum(lax.all_to_all(sums, Z_RING, 0, 0), axis=0)  13.8 us
    all_to_all x1, blocking collectives, per_device(): lax.all_to_all(jnp.broadcast_to(ring[None], (32, 1, NZ)), PLANE, 0, 0)  12.1 us
    all_to_all x1, waiting for transfers between devices, gather_all(): ring = resident(lax.all_to_all(block, Z_RING, 0, 0))  11.7 us
  transfers between devices with their start and end apart: 10, of which 6 were waited for; matrix products, arithmetic and copies ran while one was open for 0% of the time, Pallas kernels for 0%

profile of v6, /device:TPU:1, one launch (start us, length us, event | category | flops | bytes accessed | tf_op | source)
XLA Modules:
  0.0 203.9 jit_solution(10422384165216410113)
XLA Ops:
  0.6 0.0 copy-start
  0.6 0.9 copy-done
  1.6 0.0 copy-start.1
  1.6 0.9 copy-done.1
  2.5 10.1 %shard_map.49 = f32[128,128]{1,0:T(8,128)S(1)} custom-call(s32[512,128]{1,0:T(8,128)S(1)} %bitcast.10, f32[512,128]{1,0:T(8,128)S(1)} %bitcast.11), custom_call_target="tpu_custom_call" | custom-call | tf_op jit(solution)/shard_map/pallas_call | solution.py:387
  12.7 8.7 %collective-permute-start = (f32[16,8,128]{2,1,0:T(8,128)S(1)}, f32[16,8,128]{2,1,0:T(8,128)S(1)}, u32[]{:S(2)}, u32[]{:S(2)}) collective-permute-start(f32[16,8,128]{2,1,0:T(8,128)S(1)} %bitcast.12), channel_id=1, source_target_pairs={{0,32},{32,0},{64,96},{96,64},{128,160},{160,128},{192,224},{224,1... | collective-permute-start | bytes 196616 | tf_op jit(solution)/shard_map/ppermute | solution.py:406
  21.4 0.9 collective-permute-done
  22.4 1.9 collective-permute-start.1
  24.3 13.3 %collective-permute-start.2 = (f32[8,8,128]{2,1,0:T(8,128)S(1)}, f32[8,8,128]{2,1,0:T(8,128)S(1)}, u32[]{:S(2)}, u32[]{:S(2)}) collective-permute-start(f32[8,8,128]{2,1,0:T(8,128)S(1)} %slice_select_fusion.1), channel_id=1, source_target_pairs={{0,96},{96,0},{64,160},{160,64},{128,224},{224,128},{192,288},{288... | collective-permute-start | bytes 98312 | tf_op jit(solution)/shard_map/ppermute | solution.py:406
  37.6 2.8 %collective-permute-done.2 = f32[8,8,128]{2,1,0:T(8,128)S(1)} collective-permute-done((f32[8,8,128]{2,1,0:T(8,128)S(1)}, f32[8,8,128]{2,1,0:T(8,128)S(1)}, u32[]{:S(2)}, u32[]{:S(2)}) %collective-permute-start.2) | collective-permute-done | bytes 32800 | tf_op jit(solution)/shard_map/ppermute | solution.py:406
  40.4 0.0 collective-permute-done.1
  40.4 2.1 %collective-permute-start.3 = (f32[64,8,128]{2,1,0:T(8,128)S(1)}, f32[64,8,128]{2,1,0:T(8,128)S(1)}, u32[]{:S(2)}, u32[]{:S(2)}) collective-permute-start(f32[64,8,128]{2,1,0:T(8,128)S(1)} %maximum_select_fusion.wide), channel_id=1, source_target_pairs={{0,1},{1,0},{2,3},{3,2},{4,5},{5,4},{6,7},{7,6},{8,9},{9,8},{10,11... | collective-permute-start | bytes 786440 | tf_op jit(solution)/shard_map/ppermute | solution.py:406
  42.5 13.8 %collective-permute-start.4 = (f32[32,8,128]{2,1,0:T(8,128)S(1)}, f32[32,8,128]{2,1,0:T(8,128)S(1)}, u32[]{:S(2)}, u32[]{:S(2)}) collective-permute-start(f32[32,8,128]{2,1,0:T(8,128)S(1)} %slice.43), channel_id=1, source_target_pairs={{1,2},{2,1},{3,4},{4,3},{5,6},{6,5},{7,8},{8,7},{9,10},{10,9},{11,... | collective-permute-start | bytes 393224 | tf_op jit(solution)/shard_map/ppermute | solution.py:406
  56.3 0.1 pad_add_fusion.pos_ref
  56.4 3.7 %collective-permute-done.4.near = f32[32,8,128]{2,1,0:T(8,128)S(1)} collective-permute-done((f32[32,8,128]{2,1,0:T(8,128)S(1)}, f32[32,8,128]{2,1,0:T(8,128)S(1)}, u32[]{:S(2)}, u32[]{:S(2)}) %collective-permute-start.4) | collective-permute-done | bytes 131104 | tf_op jit(solution)/shard_map/ppermute | solution.py:406
  60.1 0.0 collective-permute-done.3.e
  60.1 2.6 %shard_map.50 = f32[16,2,128]{2,1,0:T(2,128)} custom-call(s32[2]{0:T(128)S(1)} %pad_add_fusion.pos_ref, f32[64,8,128]{2,1,0:T(8,128)S(1)} %maximum_select_fusion.wide, f32[64,8,128]{2,1,0:T(8,128)S(1)} %collective-permute-done.3.e, f32[32,8,128]{2,1,0:T(8,128)S(1)} %collective-permute-done.4.near), custom_call_target="tpu_custom_call" | custom-call | tf_op jit(solution)/shard_map/pallas_call | solution.py:387
  62.8 8.9 %all-to-all-start = ((f32[16,2,128]{2,1,0:T(2,128)}), f32[16,2,128]{2,1,0:T(2,128)S(1)}, u32[]{:S(2)}, u32[]{:S(2)}) async-start(f32[16,2,128]{2,1,0:T(2,128)} %shard_map.50), calls=%async_computation | async-start | bytes 32768 | tf_op jit(solution)/shard_map/all_to_all | solution.py:418
  71.7 11.7 %all-to-all-done.ring = f32[16,2,128]{2,1,0:T(2,128)S(1)} async-done(((f32[16,2,128]{2,1,0:T(2,128)}), f32[16,2,128]{2,1,0:T(2,128)S(1)}, u32[]{:S(2)}, u32[]{:S(2)}) %all-to-all-start) | async-done | bytes 16416 | tf_op jit(solution)/shard_map/all_to_all | solution.py:418
  83.4 1.4 shard_map.51
  84.8 7.8 %all-to-all-start.1 = ((f32[32,11,2,128]{3,2,1,0:T(2,128)}), f32[32,11,2,128]{3,2,1,0:T(2,128)S(1)}, u32[]{:S(2)}, u32[]{:S(2)}) async-start(f32[32,11,2,128]{3,2,1,0:T(2,128)} %shard_map.51), calls=%async_computation.1 | async-start | bytes 720896 | tf_op jit(solution)/shard_map/all_to_all | solution.py:420
  92.7 4.5 %collective-permute-start.6 = (f32[80,8,128]{2,1,0:T(8,128)S(1)}, f32[80,8,128]{2,1,0:T(8,128)S(1)}, u32[]{:S(2)}, u32[]{:S(2)}) collective-permute-start(f32[80,8,128]{2,1,0:T(8,128)S(1)} %get-tuple-element.23), channel_id=1, source_target_pairs={{0,3},{3,0},{2,5},{5,2},{4,7},{7,4},{6,9},{9,6},{8,11},{11,8},{10,... | collective-permute-start | bytes 983048 | tf_op jit(solution)/shard_map/ppermute | solution.py:406
  97.1 2.2 %collective-permute-start.5 = (f32[80,8,128]{2,1,0:T(8,128)S(1)}, f32[80,8,128]{2,1,0:T(8,128)S(1)}, u32[]{:S(2)}, u32[]{:S(2)}) collective-permute-start(f32[80,8,128]{2,1,0:T(8,128)S(1)} %get-tuple-element.24), channel_id=1, source_target_pairs={{1,2},{2,1},{3,4},{4,3},{5,6},{6,5},{7,8},{8,7},{9,10},{10,9},{11,... | collective-permute-start | bytes 983048 | tf_op jit(solution)/shard_map/ppermute | solution.py:406
  99.4 9.4 %collective-permute-start.7 = (f32[32,8,128]{2,1,0:T(8,128)S(1)}, f32[32,8,128]{2,1,0:T(8,128)S(1)}, u32[]{:S(2)}, u32[]{:S(2)}) collective-permute-start(f32[32,8,128]{2,1,0:T(8,128)S(1)} %slice.43), channel_id=1, source_target_pairs={{1,4},{4,1},{3,6},{6,3},{5,8},{8,5},{7,10},{10,7},{9,12},{12,9},{1... | collective-permute-start | bytes 393224 | tf_op jit(solution)/shard_map/ppermute | solution.py:406
  108.7 4.3 %collective-permute-done.7.t = f32[32,8,128]{2,1,0:T(8,128)S(1)} collective-permute-done((f32[32,8,128]{2,1,0:T(8,128)S(1)}, f32[32,8,128]{2,1,0:T(8,128)S(1)}, u32[]{:S(2)}, u32[]{:S(2)}) %collective-permute-start.7) | collective-permute-done | bytes 131104 | tf_op jit(solution)/shard_map/ppermute | solution.py:406
  113.0 0.0 collective-permute-done.6.s
  113.0 3.3 %collective-permute-done.5.o = f32[80,8,128]{2,1,0:T(8,128)S(1)} collective-permute-done((f32[80,8,128]{2,1,0:T(8,128)S(1)}, f32[80,8,128]{2,1,0:T(8,128)S(1)}, u32[]{:S(2)}, u32[]{:S(2)}) %collective-permute-start.5) | collective-permute-done | bytes 327712 | tf_op jit(solution)/shard_map/ppermute | solution.py:406
  116.4 0.0 all-to-all-done.1
  116.4 17.4 %shard_map.52 = (f32[16,2,128]{2,1,0:T(2,128)S(1)}, f32[64,56,128]{2,1,0:T(8,128)S(1)}, f32[64,56,128]{2,1,0:T(8,128)S(1)}, f32[32,32,128]{2,1,0:T(8,128)S(1)}, ...) custom-call(s32[2]{0:T(128)S(1)} %pad_add_fusion.pos_ref, f32[352,2,128]{2,1,0:T(2,128)S(1)} %bitcast.8, ...), custom_call_target="tpu_custom_call" | custom-call | tf_op jit(solution)/shard_map/pallas_call | solution.py:387
  133.8 17.0 %all_to_all.30.ring = f32[16,2,128]{2,1,0:T(2,128)S(1)} all-to-all(f32[16,2,128]{2,1,0:T(2,128)S(1)} %get-tuple-element.12), channel_id=1, replica_groups=mesh['gx_0'=2,'gx_1'=4,'gx_2'=2,'gy_0'=8,'gy_1'=4] {'gx_0','gy_0'}, dimensions={0} | all-to-all | bytes 32768 | tf_op jit(solution)/shard_map/all_to_all | solution.py:418
  150.9 0.6 shard_map.53
  151.5 19.3 %all_to_all.31 = f32[32,11,2,128]{3,2,1,0:T(2,128)S(1)} all-to-all(f32[32,11,2,128]{3,2,1,0:T(2,128)S(1)} %shard_map.53), channel_id=1, replica_groups=mesh['gx_0'=2,'gx_1'=4,'gx_2'=2,'gy_0'=8,'gy_1'=4] {'gx_1','gx_2','gy_1'}, dimensions={0} | all-to-all | bytes 720896 | tf_op jit(solution)/shard_map/all_to_all | solution.py:420
  170.8 6.6 %shard_map.54 = (f32[16,8,128]{2,1,0:T(8,128)}, f32[16,8,128]{2,1,0:T(8,128)}, f32[16,1,128]{2,1,0:T(1,128)S(1)}) custom-call(s32[2]{0:T(128)S(1)} %pad_add_fusion.pos_ref, f32[352,2,128]{2,1,0:T(2,128)S(1)} %bitcast.9, f32[64,56,128]{2,1,0:T(8,128)S(1)} %get-tuple-element.13.d, f32[64,56,128]{2,1,0:T(8,128)S(1)} %get-tuple-element.14.u0, ...), custom_call_target="tpu_custom_call" | custom-call | tf_op jit(solution)/shard_map/pallas_call | solution.py:387
  177.4 13.8 %all_to_all.32 = f32[16,1,128]{2,1,0:T(1,128)S(1)} all-to-all(f32[16,1,128]{2,1,0:T(1,128)S(1)} %get-tuple-element.20), channel_id=1, replica_groups=mesh['gx_0'=2,'gx_1'=4,'gx_2'=2,'gy_0'=8,'gy_1'=4] {'gx_0','gy_0'}, dimensions={0} | all-to-all | bytes 16384 | tf_op jit(solution)/shard_map/all_to_all | solution.py:470
  191.2 12.1 %all_to_all.33 = f32[32,1,128]{2,1,0:T(1,128)S(1)} all-to-all(f32[32,1,128]{2,1,0:T(1,128)S(1)} %broadcast_in_dim.2), channel_id=1, replica_groups=mesh['gx_0'=2,'gx_1'=4,'gx_2'=2,'gy_0'=8,'gy_1'=4] {'gx_1','gx_2','gy_1'}, dimensions={0} | all-to-all | bytes 32768 | tf_op jit(solution)/shard_map/all_to_all | solution.py:471
  203.3 0.5 add_sqrt_fusion
  (11 shorter events, 0.2 us)
Async XLA Ops:
  0.6 1.0 copy-start
  1.6 0.9 copy-start.1
  12.7 9.6 %collective-permute-start = (f32[16,8,128]{2,1,0:T(8,128)S(1)}, f32[16,8,128]{2,1,0:T(8,128)S(1)}, u32[]{:S(2)}, u32[]{:S(2)}) collective-permute-start(f32[16,8,128]{2,1,0:T(8,128)S(1)} %bitcast.12), channel_id=1, source_target_pairs={{0,32},{32,0},{64,96},{96,64},{128,160},{160,128},{192,224},{224,1... | collective-permute-start | bytes 196616 | tf_op jit(solution)/shard_map/ppermute | solution.py:406
  22.4 18.0 %collective-permute-start.1 = (f32[24,8,128]{2,1,0:T(8,128)S(1)}, f32[24,8,128]{2,1,0:T(8,128)S(1)}, u32[]{:S(2)}, u32[]{:S(2)}) collective-permute-start(f32[24,8,128]{2,1,0:T(8,128)S(1)} %slice_select_fusion), channel_id=1, source_target_pairs={{32,64},{64,32},{96,128},{128,96},{160,192},{192,160},{224,256},{2... | collective-permute-start | bytes 294920 | tf_op jit(solution)/shard_map/ppermute | solution.py:406
  24.3 16.1 %collective-permute-start.2 = (f32[8,8,128]{2,1,0:T(8,128)S(1)}, f32[8,8,128]{2,1,0:T(8,128)S(1)}, u32[]{:S(2)}, u32[]{:S(2)}) collective-permute-start(f32[8,8,128]{2,1,0:T(8,128)S(1)} %slice_select_fusion.1), channel_id=1, source_target_pairs={{0,96},{96,0},{64,160},{160,64},{128,224},{224,128},{192,288},{288... | collective-permute-start | bytes 98312 | tf_op jit(solution)/shard_map/ppermute | solution.py:406
  40.4 19.8 %collective-permute-start.3 = (f32[64,8,128]{2,1,0:T(8,128)S(1)}, f32[64,8,128]{2,1,0:T(8,128)S(1)}, u32[]{:S(2)}, u32[]{:S(2)}) collective-permute-start(f32[64,8,128]{2,1,0:T(8,128)S(1)} %maximum_select_fusion.wide), channel_id=1, source_target_pairs={{0,1},{1,0},{2,3},{3,2},{4,5},{5,4},{6,7},{7,6},{8,9},{9,8},{10,11... | collective-permute-start | bytes 786440 | tf_op jit(solution)/shard_map/ppermute | solution.py:406
  42.5 17.6 %collective-permute-start.4 = (f32[32,8,128]{2,1,0:T(8,128)S(1)}, f32[32,8,128]{2,1,0:T(8,128)S(1)}, u32[]{:S(2)}, u32[]{:S(2)}) collective-permute-start(f32[32,8,128]{2,1,0:T(8,128)S(1)} %slice.43), channel_id=1, source_target_pairs={{1,2},{2,1},{3,4},{4,3},{5,6},{6,5},{7,8},{8,7},{9,10},{10,9},{11,... | collective-permute-start | bytes 393224 | tf_op jit(solution)/shard_map/ppermute | solution.py:406
  62.8 20.7 %all-to-all-start = ((f32[16,2,128]{2,1,0:T(2,128)}), f32[16,2,128]{2,1,0:T(2,128)S(1)}, u32[]{:S(2)}, u32[]{:S(2)}) async-start(f32[16,2,128]{2,1,0:T(2,128)} %shard_map.50), calls=%async_computation | async-start | bytes 32768 | tf_op jit(solution)/shard_map/all_to_all | solution.py:418
  84.8 31.5 %all-to-all-start.1 = ((f32[32,11,2,128]{3,2,1,0:T(2,128)}), f32[32,11,2,128]{3,2,1,0:T(2,128)S(1)}, u32[]{:S(2)}, u32[]{:S(2)}) async-start(f32[32,11,2,128]{3,2,1,0:T(2,128)} %shard_map.51), calls=%async_computation.1 | async-start | bytes 720896 | tf_op jit(solution)/shard_map/all_to_all | solution.py:420
  92.7 20.4 %collective-permute-start.6 = (f32[80,8,128]{2,1,0:T(8,128)S(1)}, f32[80,8,128]{2,1,0:T(8,128)S(1)}, u32[]{:S(2)}, u32[]{:S(2)}) collective-permute-start(f32[80,8,128]{2,1,0:T(8,128)S(1)} %get-tuple-element.23), channel_id=1, source_target_pairs={{0,3},{3,0},{2,5},{5,2},{4,7},{7,4},{6,9},{9,6},{8,11},{11,8},{10,... | collective-permute-start | bytes 983048 | tf_op jit(solution)/shard_map/ppermute | solution.py:406
  97.1 19.2 %collective-permute-start.5 = (f32[80,8,128]{2,1,0:T(8,128)S(1)}, f32[80,8,128]{2,1,0:T(8,128)S(1)}, u32[]{:S(2)}, u32[]{:S(2)}) collective-permute-start(f32[80,8,128]{2,1,0:T(8,128)S(1)} %get-tuple-element.24), channel_id=1, source_target_pairs={{1,2},{2,1},{3,4},{4,3},{5,6},{6,5},{7,8},{8,7},{9,10},{10,9},{11,... | collective-permute-start | bytes 983048 | tf_op jit(solution)/shard_map/ppermute | solution.py:406
  99.4 13.7 %collective-permute-start.7 = (f32[32,8,128]{2,1,0:T(8,128)S(1)}, f32[32,8,128]{2,1,0:T(8,128)S(1)}, u32[]{:S(2)}, u32[]{:S(2)}) collective-permute-start(f32[32,8,128]{2,1,0:T(8,128)S(1)} %slice.43), channel_id=1, source_target_pairs={{1,4},{4,1},{3,6},{6,3},{5,8},{8,5},{7,10},{10,7},{9,12},{12,9},{1... | collective-permute-start | bytes 393224 | tf_op jit(solution)/shard_map/ppermute | solution.py:406

commit v7 on v6

--- a/solution.py
+++ b/solution.py
@@ -7,6 +7,7 @@
 from jax.experimental.pallas import tpu as pltpu
 from jax.sharding import Mesh
 from jax.sharding import PartitionSpec as P
+
 
 CX = 16
 CY = 8
@@ -195,7 +196,8 @@
         ref[i] = jnp.zeros(ref.shape[1:], jnp.float32)
 
 
-def fan_kernel(pos_ref, ring, out):
+def fan_kernel(pos_ref, ring, *rest):
+    out = rest[-1]
     block = lax.shift_right_logical(pos_ref[1], 2)
     parts = [ring[8 * h + ((block + (j + 6)) & 7)] for h in range(2) for j in range(5)]
     parts.append(jnp.sum(ring[...], axis=0))
@@ -414,9 +416,9 @@
     return i % 2 == 1
 
 
-def gather_all(block, pos):
+def gather_all(block, pos, *held):
     ring = resident(lax.all_to_all(block, Z_RING, 0, 0))
-    copies = call(fan_kernel, kept(32, RING + 1, 2, NZ), (), ring, pos=pos)
+    copies = call(fan_kernel, kept(32, RING + 1, 2, NZ), (), ring, *held, pos=pos)
     return lax.all_to_all(copies, PLANE, 0, 0).reshape(32 * (RING + 1), 2, NZ)
 
 
@@ -437,8 +439,8 @@
     masses = particle_mass.reshape(512, 128)
     density = call(deposit_kernel, kept(128, 128), (), cells, masses).reshape(CX, CY, NZ)
     wide = x_window(density)
+    near = swap(wide[16:48], GY, 1, odd)
     e = swap(wide, GY, 1, even)
-    near = swap(wide[16:48], GY, 1, odd)
     outer = jnp.concatenate([wide[:16], wide[48:], e[8:56]])
     reach = jnp.concatenate([e[8:56], wide[16:48]])
     send = call(
@@ -448,10 +450,10 @@
         wide, e, near,
         pos=pos,
     )
-    got = gather_all(send, pos)
-    o = swap(outer, GY, 1, odd)
     s = swap(reach, GY, 3, even)
     t = swap(wide[16:48], GY, 3, odd)
+    got = gather_all(send, pos, s, t)
+    o = swap(outer, GY, 1, odd)
     send, d, u0, b1, u1, stat = call(
         mid_kernel,
         (kept(16, 2, NZ), kept(W0X, W0Y, NZ), *LEVELS_OUT, kept(16, NZ)),

time: 205 us -> 209 us (1.020)
  waiting for transfers between devices: 26.7 us -> 39 us
  blocking collectives: 62.2 us -> 57.9 us
  starting transfers between devices: 72.6 us -> 68.8 us
    ppermute x8, waiting for transfers between devices: 15 us -> 27.7 us  [swap(): return lax.ppermute(x, axis, pairs(lax.axis_size(axis), step, chosen))]
    ppermute x8, starting transfers between devices: 55.9 us -> 45.9 us  [swap(): return lax.ppermute(x, axis, pairs(lax.axis_size(axis), step, chosen))]
    all_to_all x1, starting transfers between devices: 8.9 us -> 12.8 us  [gather_all(): ring = resident(lax.all_to_all(block, Z_RING, 0, 0))]
    all_to_all x1, blocking collectives: 17 us -> 13.8 us  [gather_all(): ring = resident(lax.all_to_all(block, Z_RING, 0, 0))]
    all_to_all x1, starting transfers between devices: 7.78 us -> 10.2 us  [gather_all(): return lax.all_to_all(copies, PLANE, 0, 0).reshape(32 * (RING + 1), 2, NZ)]
  transfers between devices with their start and end apart: 10 -> 10, of which waited for: 6 -> 6; matrix products, arithmetic and copies ran while one was open for 0% -> 0% of each run, Pallas kernels for 0% -> 1%
where the time goes in v7:
time: 209 us; the launch traced here: 208 us
  starting transfers between devices  68.8 us (33%)
  blocking collectives  57.9 us (28%)
  waiting for transfers between devices  39 us (19%)
  Pallas kernels  38.8 us (19%)
    ppermute x8, starting transfers between devices, swap(): return lax.ppermute(x, axis, pairs(lax.axis_size(axis), step, chosen))  45.9 us
    pallas_call x6, Pallas kernels, call(): pl.pallas_call(kernel, out_shape=outs, in_specs=specs, out_specs=jax.tree...  38.8 us
    ppermute x8, waiting for transfers between devices, swap(): return lax.ppermute(x, axis, pairs(lax.axis_size(axis), step, chosen))  27.7 us
    all_to_all x1, blocking collectives, gather_all(): return lax.all_to_all(copies, PLANE, 0, 0).reshape(32 * (RING + 1), 2, NZ)  18.1 us
    all_to_all x1, blocking collectives, per_device(): ring = jnp.sum(lax.all_to_all(sums, Z_RING, 0, 0), axis=0)  13.8 us
    all_to_all x1, blocking collectives, gather_all(): ring = resident(lax.all_to_all(block, Z_RING, 0, 0))  13.8 us
    all_to_all x1, starting transfers between devices, gather_all(): ring = resident(lax.all_to_all(block, Z_RING, 0, 0))  12.8 us
    all_to_all x1, blocking collectives, per_device(): lax.all_to_all(jnp.broadcast_to(ring[None], (32, 1, NZ)), PLANE, 0, 0)  12.1 us
  transfers between devices with their start and end apart: 10, of which 6 were waited for; matrix products, arithmetic and copies ran while one was open for 0% of the time, Pallas kernels for 1%

profile of v7, /device:TPU:1, one launch (start us, length us, event | category | flops | bytes accessed | tf_op | source)
XLA Modules:
  0.0 208.1 jit_solution(8532157623192773672)
XLA Ops:
  0.6 0.0 copy-start
  0.6 0.9 copy-done
  1.6 0.0 copy-start.1
  1.6 0.9 copy-done.1
  2.5 10.1 %shard_map.49 = f32[128,128]{1,0:T(8,128)S(1)} custom-call(s32[512,128]{1,0:T(8,128)S(1)} %bitcast.10, f32[512,128]{1,0:T(8,128)S(1)} %bitcast.11), custom_call_target="tpu_custom_call" | custom-call | tf_op jit(solution)/shard_map/pallas_call | solution.py:389
  12.7 8.7 %collective-permute-start = (f32[16,8,128]{2,1,0:T(8,128)S(1)}, f32[16,8,128]{2,1,0:T(8,128)S(1)}, u32[]{:S(2)}, u32[]{:S(2)}) collective-permute-start(f32[16,8,128]{2,1,0:T(8,128)S(1)} %bitcast.12), channel_id=1, source_target_pairs={{0,32},{32,0},{64,96},{96,64},{128,160},{160,128},{192,224},{224,1... | collective-permute-start | bytes 196616 | tf_op jit(solution)/shard_map/ppermute | solution.py:408
  21.4 0.9 collective-permute-done
  22.4 1.9 collective-permute-start.1
  24.3 13.3 %collective-permute-start.2 = (f32[8,8,128]{2,1,0:T(8,128)S(1)}, f32[8,8,128]{2,1,0:T(8,128)S(1)}, u32[]{:S(2)}, u32[]{:S(2)}) collective-permute-start(f32[8,8,128]{2,1,0:T(8,128)S(1)} %slice_select_fusion.1), channel_id=1, source_target_pairs={{0,96},{96,0},{64,160},{160,64},{128,224},{224,128},{192,288},{288... | collective-permute-start | bytes 98312 | tf_op jit(solution)/shard_map/ppermute | solution.py:408
  37.6 2.8 %collective-permute-done.2 = f32[8,8,128]{2,1,0:T(8,128)S(1)} collective-permute-done((f32[8,8,128]{2,1,0:T(8,128)S(1)}, f32[8,8,128]{2,1,0:T(8,128)S(1)}, u32[]{:S(2)}, u32[]{:S(2)}) %collective-permute-start.2) | collective-permute-done | bytes 32800 | tf_op jit(solution)/shard_map/ppermute | solution.py:408
  40.4 0.0 collective-permute-done.1
  40.4 2.1 %collective-permute-start.3 = (f32[64,8,128]{2,1,0:T(8,128)S(1)}, f32[64,8,128]{2,1,0:T(8,128)S(1)}, u32[]{:S(2)}, u32[]{:S(2)}) collective-permute-start(f32[64,8,128]{2,1,0:T(8,128)S(1)} %maximum_select_fusion.wide), channel_id=1, source_target_pairs={{0,1},{1,0},{2,3},{3,2},{4,5},{5,4},{6,7},{7,6},{8,9},{9,8},{10,11... | collective-permute-start | bytes 786440 | tf_op jit(solution)/shard_map/ppermute | solution.py:408
  42.6 7.4 %collective-permute-done.3.e = f32[64,8,128]{2,1,0:T(8,128)S(1)} collective-permute-done((f32[64,8,128]{2,1,0:T(8,128)S(1)}, f32[64,8,128]{2,1,0:T(8,128)S(1)}, u32[]{:S(2)}, u32[]{:S(2)}) %collective-permute-start.3) | collective-permute-done | bytes 262176 | tf_op jit(solution)/shard_map/ppermute | solution.py:408
  50.0 2.4 %collective-permute-start.5 = (f32[80,8,128]{2,1,0:T(8,128)S(1)}, f32[80,8,128]{2,1,0:T(8,128)S(1)}, u32[]{:S(2)}, u32[]{:S(2)}) collective-permute-start(f32[80,8,128]{2,1,0:T(8,128)S(1)} %get-tuple-element.24), channel_id=1, source_target_pairs={{0,3},{3,0},{2,5},{5,2},{4,7},{7,4},{6,9},{9,6},{8,11},{11,8},{10,... | collective-permute-start | bytes 983048 | tf_op jit(solution)/shard_map/ppermute | solution.py:408
  52.5 10.7 %collective-permute-start.4 = (f32[32,8,128]{2,1,0:T(8,128)S(1)}, f32[32,8,128]{2,1,0:T(8,128)S(1)}, u32[]{:S(2)}, u32[]{:S(2)}) collective-permute-start(f32[32,8,128]{2,1,0:T(8,128)S(1)} %slice.43), channel_id=1, source_target_pairs={{1,2},{2,1},{3,4},{4,3},{5,6},{6,5},{7,8},{8,7},{9,10},{10,9},{11,... | collective-permute-start | bytes 393224 | tf_op jit(solution)/shard_map/ppermute | solution.py:408
  63.2 2.0 collective-permute-start.6
  65.2 0.1 pad_add_fusion.pos_ref
  65.3 1.6 collective-permute-done.4.near
  66.9 2.6 %shard_map.50 = f32[16,2,128]{2,1,0:T(2,128)} custom-call(s32[2]{0:T(128)S(1)} %pad_add_fusion.pos_ref, f32[64,8,128]{2,1,0:T(8,128)S(1)} %maximum_select_fusion.wide, f32[64,8,128]{2,1,0:T(8,128)S(1)} %collective-permute-done.3.e, f32[32,8,128]{2,1,0:T(8,128)S(1)} %collective-permute-done.4.near), custom_call_target="tpu_custom_call" | custom-call | tf_op jit(solution)/shard_map/pallas_call | solution.py:389
  69.5 12.8 %all-to-all-start = ((f32[16,2,128]{2,1,0:T(2,128)}), f32[16,2,128]{2,1,0:T(2,128)S(1)}, u32[]{:S(2)}, u32[]{:S(2)}) async-start(f32[16,2,128]{2,1,0:T(2,128)} %shard_map.50), calls=%async_computation | async-start | bytes 32768 | tf_op jit(solution)/shard_map/all_to_all | solution.py:420
  82.3 0.0 collective-permute-done.6.rest_1_.t
  82.3 11.4 %all-to-all-done.ring = f32[16,2,128]{2,1,0:T(2,128)S(1)} async-done(((f32[16,2,128]{2,1,0:T(2,128)}), f32[16,2,128]{2,1,0:T(2,128)S(1)}, u32[]{:S(2)}, u32[]{:S(2)}) %all-to-all-start) | async-done | bytes 16416 | tf_op jit(solution)/shard_map/all_to_all | solution.py:420
  93.7 0.0 collective-permute-done.5.rest_0_.s
  93.7 1.4 shard_map.51
  95.1 10.2 %all-to-all-start.1 = ((f32[32,11,2,128]{3,2,1,0:T(2,128)}), f32[32,11,2,128]{3,2,1,0:T(2,128)S(1)}, u32[]{:S(2)}, u32[]{:S(2)}) async-start(f32[32,11,2,128]{3,2,1,0:T(2,128)} %shard_map.51), calls=%async_computation.1 | async-start | bytes 720896 | tf_op jit(solution)/shard_map/all_to_all | solution.py:422
  105.3 4.7 %collective-permute-start.7 = (f32[80,8,128]{2,1,0:T(8,128)S(1)}, f32[80,8,128]{2,1,0:T(8,128)S(1)}, u32[]{:S(2)}, u32[]{:S(2)}) collective-permute-start(f32[80,8,128]{2,1,0:T(8,128)S(1)} %get-tuple-element.23), channel_id=1, source_target_pairs={{1,2},{2,1},{3,4},{4,3},{5,6},{6,5},{7,8},{8,7},{9,10},{10,9},{11,... | collective-permute-start | bytes 983048 | tf_op jit(solution)/shard_map/ppermute | solution.py:408
  110.0 15.0 %collective-permute-done.7.o = f32[80,8,128]{2,1,0:T(8,128)S(1)} collective-permute-done((f32[80,8,128]{2,1,0:T(8,128)S(1)}, f32[80,8,128]{2,1,0:T(8,128)S(1)}, u32[]{:S(2)}, u32[]{:S(2)}) %collective-permute-start.7) | collective-permute-done | bytes 327712 | tf_op jit(solution)/shard_map/ppermute | solution.py:408
  124.9 0.0 all-to-all-done.1
  124.9 17.4 %shard_map.52 = (f32[16,2,128]{2,1,0:T(2,128)S(1)}, f32[64,56,128]{2,1,0:T(8,128)S(1)}, f32[64,56,128]{2,1,0:T(8,128)S(1)}, f32[32,32,128]{2,1,0:T(8,128)S(1)}, ...) custom-call(s32[2]{0:T(128)S(1)} %pad_add_fusion.pos_ref, f32[352,2,128]{2,1,0:T(2,128)S(1)} %bitcast.8, ...), custom_call_target="tpu_custom_call" | custom-call | tf_op jit(solution)/shard_map/pallas_call | solution.py:389
  142.4 13.8 %all_to_all.30.ring = f32[16,2,128]{2,1,0:T(2,128)S(1)} all-to-all(f32[16,2,128]{2,1,0:T(2,128)S(1)} %get-tuple-element.12), channel_id=1, replica_groups=mesh['gx_0'=2,'gx_1'=4,'gx_2'=2,'gy_0'=8,'gy_1'=4] {'gx_0','gy_0'}, dimensions={0} | all-to-all | bytes 32768 | tf_op jit(solution)/shard_map/all_to_all | solution.py:420
  156.2 0.6 shard_map.53
  156.9 18.1 %all_to_all.31 = f32[32,11,2,128]{3,2,1,0:T(2,128)S(1)} all-to-all(f32[32,11,2,128]{3,2,1,0:T(2,128)S(1)} %shard_map.53), channel_id=1, replica_groups=mesh['gx_0'=2,'gx_1'=4,'gx_2'=2,'gy_0'=8,'gy_1'=4] {'gx_1','gx_2','gy_1'}, dimensions={0} | all-to-all | bytes 720896 | tf_op jit(solution)/shard_map/all_to_all | solution.py:422
  175.0 6.6 %shard_map.54 = (f32[16,8,128]{2,1,0:T(8,128)}, f32[16,8,128]{2,1,0:T(8,128)}, f32[16,1,128]{2,1,0:T(1,128)S(1)}) custom-call(s32[2]{0:T(128)S(1)} %pad_add_fusion.pos_ref, f32[352,2,128]{2,1,0:T(2,128)S(1)} %bitcast.9, f32[64,56,128]{2,1,0:T(8,128)S(1)} %get-tuple-element.13.d, f32[64,56,128]{2,1,0:T(8,128)S(1)} %get-tuple-element.14.u0, ...), custom_call_target="tpu_custom_call" | custom-call | tf_op jit(solution)/shard_map/pallas_call | solution.py:389
  181.6 13.8 %all_to_all.32 = f32[16,1,128]{2,1,0:T(1,128)S(1)} all-to-all(f32[16,1,128]{2,1,0:T(1,128)S(1)} %get-tuple-element.20), channel_id=1, replica_groups=mesh['gx_0'=2,'gx_1'=4,'gx_2'=2,'gy_0'=8,'gy_1'=4] {'gx_0','gy_0'}, dimensions={0} | all-to-all | bytes 16384 | tf_op jit(solution)/shard_map/all_to_all | solution.py:472
  195.4 12.1 %all_to_all.33 = f32[32,1,128]{2,1,0:T(1,128)S(1)} all-to-all(f32[32,1,128]{2,1,0:T(1,128)S(1)} %broadcast_in_dim.2), channel_id=1, replica_groups=mesh['gx_0'=2,'gx_1'=4,'gx_2'=2,'gy_0'=8,'gy_1'=4] {'gx_1','gx_2','gy_1'}, dimensions={0} | all-to-all | bytes 32768 | tf_op jit(solution)/shard_map/all_to_all | solution.py:473
  207.5 0.5 add_sqrt_fusion
  (11 shorter events, 0.2 us)
Async XLA Ops:
  0.6 1.0 copy-start
  1.6 0.9 copy-start.1
  12.7 9.6 %collective-permute-start = (f32[16,8,128]{2,1,0:T(8,128)S(1)}, f32[16,8,128]{2,1,0:T(8,128)S(1)}, u32[]{:S(2)}, u32[]{:S(2)}) collective-permute-start(f32[16,8,128]{2,1,0:T(8,128)S(1)} %bitcast.12), channel_id=1, source_target_pairs={{0,32},{32,0},{64,96},{96,64},{128,160},{160,128},{192,224},{224,1... | collective-permute-start | bytes 196616 | tf_op jit(solution)/shard_map/ppermute | solution.py:408
  22.4 18.0 %collective-permute-start.1 = (f32[24,8,128]{2,1,0:T(8,128)S(1)}, f32[24,8,128]{2,1,0:T(8,128)S(1)}, u32[]{:S(2)}, u32[]{:S(2)}) collective-permute-start(f32[24,8,128]{2,1,0:T(8,128)S(1)} %slice_select_fusion), channel_id=1, source_target_pairs={{32,64},{64,32},{96,128},{128,96},{160,192},{192,160},{224,256},{2... | collective-permute-start | bytes 294920 | tf_op jit(solution)/shard_map/ppermute | solution.py:408
  24.3 16.1 %collective-permute-start.2 = (f32[8,8,128]{2,1,0:T(8,128)S(1)}, f32[8,8,128]{2,1,0:T(8,128)S(1)}, u32[]{:S(2)}, u32[]{:S(2)}) collective-permute-start(f32[8,8,128]{2,1,0:T(8,128)S(1)} %slice_select_fusion.1), channel_id=1, source_target_pairs={{0,96},{96,0},{64,160},{160,64},{128,224},{224,128},{192,288},{288... | collective-permute-start | bytes 98312 | tf_op jit(solution)/shard_map/ppermute | solution.py:408
  40.4 9.6 %collective-permute-start.3 = (f32[64,8,128]{2,1,0:T(8,128)S(1)}, f32[64,8,128]{2,1,0:T(8,128)S(1)}, u32[]{:S(2)}, u32[]{:S(2)}) collective-permute-start(f32[64,8,128]{2,1,0:T(8,128)S(1)} %maximum_select_fusion.wide), channel_id=1, source_target_pairs={{0,1},{1,0},{2,3},{3,2},{4,5},{5,4},{6,7},{7,6},{8,9},{9,8},{10,11... | collective-permute-start | bytes 786440 | tf_op jit(solution)/shard_map/ppermute | solution.py:408
  50.0 43.7 %collective-permute-start.5 = (f32[80,8,128]{2,1,0:T(8,128)S(1)}, f32[80,8,128]{2,1,0:T(8,128)S(1)}, u32[]{:S(2)}, u32[]{:S(2)}) collective-permute-start(f32[80,8,128]{2,1,0:T(8,128)S(1)} %get-tuple-element.24), channel_id=1, source_target_pairs={{0,3},{3,0},{2,5},{5,2},{4,7},{7,4},{6,9},{9,6},{8,11},{11,8},{10,... | collective-permute-start | bytes 983048 | tf_op jit(solution)/shard_map/ppermute | solution.py:408
  52.5 14.4 %collective-permute-start.4 = (f32[32,8,128]{2,1,0:T(8,128)S(1)}, f32[32,8,128]{2,1,0:T(8,128)S(1)}, u32[]{:S(2)}, u32[]{:S(2)}) collective-permute-start(f32[32,8,128]{2,1,0:T(8,128)S(1)} %slice.43), channel_id=1, source_target_pairs={{1,2},{2,1},{3,4},{4,3},{5,6},{6,5},{7,8},{8,7},{9,10},{10,9},{11,... | collective-permute-start | bytes 393224 | tf_op jit(solution)/shard_map/ppermute | solution.py:408
  63.2 19.2 %collective-permute-start.6 = (f32[32,8,128]{2,1,0:T(8,128)S(1)}, f32[32,8,128]{2,1,0:T(8,128)S(1)}, u32[]{:S(2)}, u32[]{:S(2)}) collective-permute-start(f32[32,8,128]{2,1,0:T(8,128)S(1)} %slice.43), channel_id=1, source_target_pairs={{1,4},{4,1},{3,6},{6,3},{5,8},{8,5},{7,10},{10,7},{9,12},{12,9},{1... | collective-permute-start | bytes 393224 | tf_op jit(solution)/shard_map/ppermute | solution.py:408
  69.5 24.2 %all-to-all-start = ((f32[16,2,128]{2,1,0:T(2,128)}), f32[16,2,128]{2,1,0:T(2,128)S(1)}, u32[]{:S(2)}, u32[]{:S(2)}) async-start(f32[16,2,128]{2,1,0:T(2,128)} %shard_map.50), calls=%async_computation | async-start | bytes 32768 | tf_op jit(solution)/shard_map/all_to_all | solution.py:420
  95.1 29.8 %all-to-all-start.1 = ((f32[32,11,2,128]{3,2,1,0:T(2,128)}), f32[32,11,2,128]{3,2,1,0:T(2,128)S(1)}, u32[]{:S(2)}, u32[]{:S(2)}) async-start(f32[32,11,2,128]{3,2,1,0:T(2,128)} %shard_map.51), calls=%async_computation.1 | async-start | bytes 720896 | tf_op jit(solution)/shard_map/all_to_all | solution.py:422
  105.3 19.6 %collective-permute-start.7 = (f32[80,8,128]{2,1,0:T(8,128)S(1)}, f32[80,8,128]{2,1,0:T(8,128)S(1)}, u32[]{:S(2)}, u32[]{:S(2)}) collective-permute-start(f32[80,8,128]{2,1,0:T(8,128)S(1)} %get-tuple-element.23), channel_id=1, source_target_pairs={{1,2},{2,1},{3,4},{4,3},{5,6},{6,5},{7,8},{8,7},{9,10},{10,9},{11,... | collective-permute-start | bytes 983048 | tf_op jit(solution)/shard_map/ppermute | solution.py:408
